TPU v7x, 512 devices: a whole 4x8x8 slice. The times are simulated.
512 devices in a mesh: seq: 32 (over y, x), head: 8 (over z), dp: 2 (over core).
Axes of the slice: x: 4, y: 8, z: 8, core: 2. Of those that a mesh axis runs over, the one named last changes fastest.
Arguments:
- queries: bfloat16 [32768, 4096], P(('dp', 'seq'), 'head'), parts along dimension 0, may hold values from -200 to 200
- keys: bfloat16 [32768, 1024], P(('dp', 'seq'), 'head'), parts along dimension 0, may hold values from -4 to 4
- values: bfloat16 [32768, 1024], P(('dp', 'seq'), 'head'), parts along dimension 0, may hold values from -15 to 15
- doc_ids: int32 [32768], P(('dp', 'seq')), parts along dimension 0, may hold values from 0 to 7, as said below
- block_lists: int32 [256, 16], P(('dp', 'seq')), parts along dimension 0, may hold values from 0 to 128, as said below
- w_out: bfloat16 [4096, 4096], P('head'), may hold values from -0.09375 to 0.09375
Outputs:
- mixed: bfloat16 [32768, 4096], P(('dp', 'seq'), 'head'), parts along dimension 0
There are 2 independent parts, one for each index of `dp`. A program takes and returns all parts, laid end to end along the dimension named above; an argument that names none is the same for every part. Nothing has to cross between parts.
Inputs may be any that keep to these rules, and one draw needn't show every extreme that they name: `block_lists`: row i lists the blocks that query block i reads: 16 entries, each a block of the sequence or the null value 128; the non-null entries of a row are distinct and include i. Blocks k * 4 to k * 4 + 3 lie on index k of seq; over the rows of one index of seq together, at most one distinct block of each other index of seq is named (so each index of seq sends at most one of its blocks to each other index). `doc_ids`: never falling along the sequence.
All inputs are finite; a program needn't handle non-finite values.
Results may differ from a plain program's by a relative error of at most 0.013.
Values may be sent and summed in bfloat16 or wider, within the bound.
No kernel may reach another device: no remote copies, remote signals or barrier semaphores. Data moves between devices by JAX's collectives and lax.ppermute only.
A program may use at most 64 MiB of HBM per device.

v0:
```python
import functools
import math

import jax
import jax.numpy as jnp
from jax import lax
from jax.experimental import pallas as pl
from jax.experimental.pallas import tpu as pltpu
from jax.sharding import Mesh, PartitionSpec as P


HEAD_SIZE = 128
BLOCK_TOKENS = 128
DOCS = 8
TOPK = 16
CHUNK = 4

negative = -1e30
far_position = 1073741824
null_base = -1073741824
score_scale = math.log2(math.e) / math.sqrt(HEAD_SIZE)


def attention_kernel(slot, base, start_ref, end_ref, q_hbm, w_hbm, *refs):
    *pieces, out_ref, table, q_all, q4, kcat, vcat, scores, attn, w_ref, sems = refs
    row = pl.program_id(0)
    heads = q_all.shape[1] // HEAD_SIZE
    keys = CHUNK * BLOCK_TOKENS
    w_copy = pltpu.make_async_copy(w_hbm, w_ref, sems.at[0])

    @pl.when(row == 0)
    def _():
        copies = [pltpu.make_async_copy(q_hbm, q_all, sems.at[1])]
        at = 0
        for n, piece in enumerate(pieces):
            place = table.at[at : at + piece.shape[0]]
            copies.append(pltpu.make_async_copy(piece, place, sems.at[n + 2]))
            at += piece.shape[0]
        for copy in copies:
            copy.start()
        w_copy.start()
        vcat[:, HEAD_SIZE:] = jnp.ones((vcat.shape[0], HEAD_SIZE), vcat.dtype)
        for copy in copies:
            copy.wait()

    own = pl.ds(pl.multiple_of(row * BLOCK_TOKENS, BLOCK_TOKENS), BLOCK_TOKENS)
    for h in range(heads):
        q4[h * BLOCK_TOKENS : (h + 1) * BLOCK_TOKENS, :] = q_all[
            own, h * HEAD_SIZE : (h + 1) * HEAD_SIZE
        ]
    for j in range(TOPK):
        rows = slice(j * BLOCK_TOKENS, (j + 1) * BLOCK_TOKENS)
        place = slot[row * TOPK + j]
        kcat[rows, :] = table[place, :, :HEAD_SIZE]
        vcat[rows, :HEAD_SIZE] = table[place, :, HEAD_SIZE:]
    starts = start_ref[...]
    ends = end_ref[...]
    lane = lax.broadcasted_iota(jnp.int32, (BLOCK_TOKENS, BLOCK_TOKENS), 1)
    peak = None
    for c in range(TOPK // CHUNK):
        cols = slice(c * keys, (c + 1) * keys)
        bias = []
        for j in range(c * CHUNK, (c + 1) * CHUNK):
            position = lane + base[row * TOPK + j]
            allowed = (position >= starts) & (position < ends)
            bias.append(jnp.where(allowed, 0.0, negative))
        bias = jnp.concatenate(bias, axis=1)
        raw = lax.dot_general(
            q4[...], kcat[cols, :], (((1,), (1,)), ((), ())), preferred_element_type=jnp.float32
        )
        for h in range(heads):
            rows = slice(h * BLOCK_TOKENS, (h + 1) * BLOCK_TOKENS)
            scores[rows, cols] = raw[rows] * score_scale + bias
        part = scores[:, cols]
        for j in range(CHUNK):
            piece = part[:, j * BLOCK_TOKENS : (j + 1) * BLOCK_TOKENS]
            peak = piece if peak is None else jnp.maximum(peak, piece)
    top = jnp.max(peak, axis=1, keepdims=True)
    total = jnp.zeros((heads * BLOCK_TOKENS, 2 * HEAD_SIZE), jnp.float32)
    for c in range(TOPK // CHUNK):
        cols = slice(c * keys, (c + 1) * keys)
        weights = jnp.exp2(scores[:, cols] - top).astype(jnp.bfloat16)
        total += jnp.dot(weights, vcat[cols, :], preferred_element_type=jnp.float32)
    result = (total[:, :HEAD_SIZE] / total[:, HEAD_SIZE:]).astype(attn.dtype)
    for h in range(heads):
        attn[:, h * HEAD_SIZE : (h + 1) * HEAD_SIZE] = result[
            h * BLOCK_TOKENS : (h + 1) * BLOCK_TOKENS
        ]

    @pl.when(row == 0)
    def _():
        w_copy.wait()

    step = 1024
    for c in range(0, w_ref.shape[1], step):
        out_ref[:, c : c + step] = jnp.dot(
            attn[...], w_ref[:, c : c + step], preferred_element_type=jnp.float32
        ).astype(out_ref.dtype)


def attention(queries, starts, ends, w_out, pieces, slot, base):
    tokens, width = queries.shape
    blocks = tokens // BLOCK_TOKENS
    rows = width // HEAD_SIZE * BLOCK_TOKENS
    listed = TOPK * BLOCK_TOKENS
    per_block = lambda i, *_: (i, 0)
    table = (sum(p.shape[0] for p in pieces), *pieces[0].shape[1:])
    return pl.pallas_call(
        attention_kernel,
        out_shape=jax.ShapeDtypeStruct((tokens, w_out.shape[1]), jnp.bfloat16),
        grid_spec=pltpu.PrefetchScalarGridSpec(
            num_scalar_prefetch=2,
            grid=(blocks,),
            in_specs=[
                pl.BlockSpec((BLOCK_TOKENS, BLOCK_TOKENS), per_block),
                pl.BlockSpec((BLOCK_TOKENS, BLOCK_TOKENS), per_block),
                *[pl.BlockSpec(memory_space=pl.ANY)] * (2 + len(pieces)),
            ],
            out_specs=pl.BlockSpec((BLOCK_TOKENS, w_out.shape[1]), per_block),
            scratch_shapes=[
                pltpu.VMEM(table, jnp.bfloat16),
                pltpu.VMEM(queries.shape, queries.dtype),
                pltpu.VMEM((rows, HEAD_SIZE), jnp.bfloat16),
                pltpu.VMEM((listed, HEAD_SIZE), jnp.bfloat16),
                pltpu.VMEM((listed, 2 * HEAD_SIZE), jnp.bfloat16),
                pltpu.VMEM((rows, listed), jnp.float32),
                pltpu.VMEM((BLOCK_TOKENS, width), jnp.bfloat16),
                pltpu.VMEM(w_out.shape, w_out.dtype),
                pltpu.SemaphoreType.DMA((2 + len(pieces),)),
            ],
        ),
        compiler_params=pltpu.CompilerParams(vmem_limit_bytes=44 * 1024 * 1024),
        cost_estimate=pl.CostEstimate(
            flops=4 * blocks * rows * listed * HEAD_SIZE + 2 * tokens * width * w_out.shape[1],
            bytes_accessed=4 * 1024 * 1024,
            transcendentals=blocks * rows * listed,
        ),
        name="attention",
    )(slot, base, starts, ends, queries, w_out, *pieces)


def pick_kernel(piece_count, index, *refs):
    pieces, out_ref = refs[:piece_count], refs[piece_count]
    for r in range(out_ref.shape[0]):
        for d, piece in enumerate(pieces):
            out_ref[r, d] = piece[index[r * piece_count + d]]


def small_kernel(body, out_shape, scalars, *operands):
    return pl.pallas_call(
        body,
        out_shape=out_shape,
        in_specs=[pl.BlockSpec(memory_space=pltpu.SMEM)]
        + [pl.BlockSpec(memory_space=pltpu.VMEM)] * len(operands),
        out_specs=jax.tree.map(lambda _: pl.BlockSpec(memory_space=pltpu.VMEM), out_shape),
        compiler_params=pltpu.CompilerParams(vmem_limit_bytes=8 * 1024 * 1024),
        cost_estimate=pl.CostEstimate(
            flops=1024 * 1024, bytes_accessed=1024 * 1024, transcendentals=0
        ),
    )(scalars, *operands)


def pick(pieces, index):
    out = jax.ShapeDtypeStruct((*index.shape, *pieces[0].shape[1:]), pieces[0].dtype)
    body = functools.partial(pick_kernel, len(pieces))
    return small_kernel(body, out, index.reshape(-1), *pieces)


def hold_kernel(source_ref, *refs):
    refs[-1][...] = source_ref[...]


def hold(source, *after):
    return pl.pallas_call(
        hold_kernel,
        out_shape=jax.ShapeDtypeStruct(source.shape, source.dtype),
        in_specs=[pl.BlockSpec(memory_space=pltpu.VMEM)]
        + [pl.BlockSpec(memory_space=pl.ANY)] * len(after),
        out_specs=pl.BlockSpec(memory_space=pltpu.VMEM),
        compiler_params=pltpu.CompilerParams(vmem_limit_bytes=1024 * 1024),
        name="hold",
    )(source, *after)


def shifted(x, axis, shift):
    size = lax.axis_size(axis)
    return lax.ppermute(x, axis, [(i, (i + shift) % size) for i in range(size)])


def ring_gather(x, axis):
    size = lax.axis_size(axis)
    pieces = {0: x}
    for step in range(1, size // 2 + 1):
        pieces[step] = shifted(pieces[step - 1], axis, 1)
        if size - step > step:
            pieces[size - step] = shifted(pieces[(size - step + 1) % size], axis, -1)
    return [pieces[d] for d in range(size)]


def add_kernel(size, groups, me, partial_ref, *refs):
    out_ref = refs[-1]
    arrived = list(refs[:-1])
    at = 0
    for first, rows, distance, terms in groups:
        width = out_ref.shape[1]
        column = pl.multiple_of(lax.rem(me[0] + (distance + size), size) * width, width)
        total = partial_ref[first : first + rows, pl.ds(column, width)].astype(jnp.float32)
        for _ in range(terms):
            total += arrived.pop(0)[...].astype(jnp.float32)
        out_ref[at : at + rows, :] = total.astype(out_ref.dtype)
        at += rows


def ring_scatter(partial, axis, streams):
    size = lax.axis_size(axis)
    me = lax.axis_index(axis).reshape(1).astype(jnp.int32)
    width = partial.shape[1] // size
    rows = partial.shape[0] // streams

    def add(groups, *arrived):
        out = jax.ShapeDtypeStruct((sum(g[1] for g in groups), width), partial.dtype)
        body = functools.partial(add_kernel, size, groups)
        return small_kernel(body, out, me, partial, *arrived)

    far = size // 2
    lengths = [(far, size - 1 - far) if b % 2 == 0 else (size - 1 - far, far) for b in range(streams)]
    sums = [[None, None] for _ in range(streams)]
    for b in range(streams):
        for side, sign in enumerate((1, -1)):
            sums[b][side] = add(((b * rows, rows, sign * lengths[b][side], 0),))
    for step in range(1, far + 1):
        for b in range(streams):
            for side, sign in enumerate((1, -1)):
                left = lengths[b][side] - step
                if left < 0:
                    continue
                moved = shifted(sums[b][side], axis, sign)
                if left:
                    moved = add(((b * rows, rows, sign * left, 1),), moved)
                sums[b][side] = moved
    groups = tuple((b * rows, rows, 0, 2) for b in range(streams))
    return add(groups, *[term for pair in sums for term in pair])


def per_device(y_count, x_count, queries, keys, values, doc_ids, block_lists, w_out):
    tok_rows = queries.shape[0]
    blocks_dev = tok_rows // BLOCK_TOKENS
    seq_count = y_count * x_count
    block_count = blocks_dev * seq_count
    own_y, own_x = lax.axis_index("y"), lax.axis_index("x")
    own_index = own_y * x_count + own_x

    own_blocks = jnp.concatenate([keys, values], axis=1).reshape(
        blocks_dev, BLOCK_TOKENS, 2 * HEAD_SIZE
    )
    column = ring_gather(own_blocks, "y")

    positions = own_index * tok_rows + jnp.arange(tok_rows, dtype=jnp.int32)
    doc_range = jnp.arange(DOCS, dtype=jnp.int32)
    first_local = jnp.min(
        jnp.where(doc_ids[None, :] == doc_range[:, None], positions[None, :], far_position), axis=1
    )
    info = jnp.concatenate([block_lists.reshape(-1), first_local])
    info = jnp.broadcast_to(info[None], (seq_count, info.shape[0]))
    info = lax.all_to_all(info, ("y", "x"), 0, 0, tiled=True)
    quarter = y_count // 4
    info = hold(info, column[quarter], column[-quarter])
    entries = blocks_dev * TOPK
    listing = info[:, :entries]
    firsts = jnp.min(info[:, entries:], axis=0)

    readers = lax.dynamic_slice_in_dim(listing, own_y * x_count, x_count, 0)
    back = jnp.arange(y_count, dtype=jnp.int32)
    owners = (own_y - back + y_count) % y_count * x_count + own_x
    wanted = (readers[:, None, :] < block_count) & (
        readers[:, None, :] // blocks_dev == owners[None, :, None]
    )
    row_offset = jnp.max(jnp.where(wanted, readers[:, None, :] % blocks_dev, 0), axis=2)
    reach = [min(d, y_count - d) for d in range(y_count)]
    near = [d for d in range(y_count) if reach[d] <= y_count // 4]
    far = [d for d in range(y_count) if reach[d] > y_count // 4]
    tables = [own_blocks]
    place = [0] * y_count
    for group in (near, far):
        if not group:
            continue
        first = sum(table.shape[0] for table in tables)
        for at, d in enumerate(group):
            place[d] = (first + at, len(group))
        outgoing = pick([column[d] for d in group], jnp.stack([row_offset[:, d] for d in group], 1))
        arrived = lax.all_to_all(outgoing, "x", 0, 0, tiled=True)
        tables.append(arrived.reshape(-1, *arrived.shape[2:]))

    valid = block_lists < block_count
    owner = block_lists // blocks_dev
    owner_y, owner_x = owner // x_count, owner % x_count
    distance = (own_y - owner_y + y_count) % y_count
    slot = 0
    for d in range(y_count):
        start, stride = place[d]
        slot = jnp.where(distance == d, start + owner_x * stride, slot)
    slot = jnp.where(owner == own_index, block_lists % blocks_dev, slot)
    slot = jnp.where(valid, slot, 0).reshape(-1)
    base = jnp.where(valid, block_lists * BLOCK_TOKENS, null_base).reshape(-1)

    later = doc_range[None, :] > doc_range[:, None]
    ends_doc = jnp.min(jnp.where(later, firsts[None, :], far_position), axis=1)
    match = doc_ids[:, None] == doc_range[None, :]
    starts = jnp.sum(jnp.where(match, firsts[None, :], 0), axis=1)
    ends = jnp.sum(jnp.where(match, ends_doc[None, :], 0), axis=1)
    starts = jnp.broadcast_to(starts[:, None], (tok_rows, BLOCK_TOKENS))
    ends = jnp.broadcast_to(ends[:, None], (tok_rows, BLOCK_TOKENS))

    partial = attention(queries, starts, ends, w_out, tables, slot, base)
    return ring_scatter(partial, "head", 2)


def solution(mesh):
    seq_count = mesh.shape["seq"]
    x_count = 4 if seq_count % 4 == 0 else 1
    y_count = seq_count // x_count
    grid = Mesh(
        mesh.devices.reshape(y_count, x_count, mesh.shape["head"], mesh.shape["dp"]),
        ("y", "x", "head", "dp"),
    )
    rows = ("dp", "y", "x")
    in_specs = (
        P(rows, "head"),
        P(rows, "head"),
        P(rows, "head"),
        P(rows),
        P(rows, None),
        P("head", None),
    )

    def body(*operands):
        return per_device(y_count, x_count, *operands)

    return jax.shard_map(
        body, mesh=grid, in_specs=in_specs, out_specs=P(rows, "head"), check_vma=False
    )
```

profile of v0, /device:TPU:2, one launch (start us, length us, event | category | flops | bytes accessed | tf_op | source)
XLA Modules:
  0.0 151.1 jit_solution(10866973148757612450)
XLA Ops:
  1.0 5.4 %collective-permute-start.2 = (bf16[4,128,256]{2,1,0:T(8,128)(2,1)S(1)}, bf16[4,128,256]{2,1,0:T(8,128)(2,1)S(1)}, u32[]{:S(2)}, u32[]{:S(2)}) collective-permute-start(bf16[4,128,256]{2,1,0:T(8,128)(2,1)S(1)} %bitcast.7), channel_id=1, source_target_pairs={{0,448},{64,0},{128,64},{192,128},{256,192},{320,256},{384,320},{4... | collective-permute-start | bytes 786440 | tf_op jit(solution)/shard_map/ppermute | solution.py:187
  6.4 1.9 %collective-permute-start = (bf16[4,128,256]{2,1,0:T(8,128)(2,1)S(1)}, bf16[4,128,256]{2,1,0:T(8,128)(2,1)S(1)}, u32[]{:S(2)}, u32[]{:S(2)}) collective-permute-start(bf16[4,128,256]{2,1,0:T(8,128)(2,1)S(1)} %bitcast.8), channel_id=1, source_target_pairs={{0,64},{64,128},{128,192},{192,256},{256,320},{320,384},{384,448},... | collective-permute-start | bytes 786440 | tf_op jit(solution)/shard_map/ppermute | solution.py:187
  8.3 3.6 %collective-permute-done.2.refs_4_ = bf16[4,128,256]{2,1,0:T(8,128)(2,1)S(1)} collective-permute-done((bf16[4,128,256]{2,1,0:T(8,128)(2,1)S(1)}, bf16[4,128,256]{2,1,0:T(8,128)(2,1)S(1)}, u32[]{:S(2)}, u32[]{:S(2)}) %collective-permute-start.2) | collective-permute-done | bytes 262176 | tf_op jit(solution)/shard_map/ppermute | solution.py:187
  11.9 5.6 %collective-permute-start.3 = (bf16[4,128,256]{2,1,0:T(8,128)(2,1)S(1)}, bf16[4,128,256]{2,1,0:T(8,128)(2,1)S(1)}, u32[]{:S(2)}, u32[]{:S(2)}) collective-permute-start(bf16[4,128,256]{2,1,0:T(8,128)(2,1)S(1)} %collective-permute-done.2.refs_4_), channel_id=1, source_target_pairs={{0,448},{64,0},{128,64},{192,128},{256,192},{320,256},{384,320},{4... | collective-permute-start | bytes 786440 | tf_op jit(solution)/shard_map/ppermute | solution.py:187
  17.5 1.9 %collective-permute-start.1 = (bf16[4,128,256]{2,1,0:T(8,128)(2,1)S(1)}, bf16[4,128,256]{2,1,0:T(8,128)(2,1)S(1)}, u32[]{:S(2)}, u32[]{:S(2)}) collective-permute-start(bf16[4,128,256]{2,1,0:T(8,128)(2,1)S(1)} %collective-permute-done.refs_1_), channel_id=1, source_target_pairs={{0,64},{64,128},{128,192},{192,256},{256,320},{320,384},{384,448},... | collective-permute-start | bytes 786440 | tf_op jit(solution)/shard_map/ppermute | solution.py:187
  21.7 7.8 %all-to-all-start = ((s32[32,1,72]{2,1,0:T(1,128)}), s32[32,1,72]{2,1,0:T(1,128)S(1)}, u32[]{:S(2)}, u32[]{:S(2)}) async-start(s32[32,1,72]{2,1,0:T(1,128)} %broadcast_in_dim.95), calls=%async_computation | async-start | bytes 32768 | tf_op jit(solution)/shard_map/all_to_all | solution.py:265
  29.5 8.5 %all-to-all-done = s32[32,1,72]{2,1,0:T(1,128)S(1)} async-done(((s32[32,1,72]{2,1,0:T(1,128)}), s32[32,1,72]{2,1,0:T(1,128)S(1)}, u32[]{:S(2)}, u32[]{:S(2)}) %all-to-all-start) | async-done | bytes 9248 | tf_op jit(solution)/shard_map/all_to_all | solution.py:265
  38.6 1.7 %shard_map.64 = bf16[4,5,128,256]{3,2,1,0:T(8,128)(2,1)} custom-call(s32[20]{0:T(128)S(1)} %reshape.94.index, bf16[4,128,256]{2,1,0:T(8,128)(2,1)S(1)} %bitcast.9, bf16[4,128,256]{2,1,0:T(8,128)(2,1)S(1)} %collective-permute-done.refs_1_, bf16[4,128,256]{2,1,0:T(8,128)(2,1)S(1)} %collective-permute-done.1.refs_0_.refs_2_, ...), custom_call_target="tpu_custom_call" | custom-call | flops 1048576 | bytes 1048576 | tf_op jit(solution)/shard_map/pallas_call | solution.py:150
  40.3 5.0 %all-to-all-start.1 = ((bf16[4,5,128,256]{3,2,1,0:T(8,128)(2,1)}), bf16[4,5,128,256]{3,2,1,0:T(8,128)(2,1)S(1)}, u32[]{:S(2)}, u32[]{:S(2)}) async-start(bf16[4,5,128,256]{3,2,1,0:T(8,128)(2,1)} %shard_map.64), calls=%async_computation.1 | async-start | bytes 2621440 | tf_op jit(solution)/shard_map/all_to_all | solution.py:291
  45.2 2.5 %collective-permute-start.4 = (bf16[4,128,256]{2,1,0:T(8,128)(2,1)S(1)}, bf16[4,128,256]{2,1,0:T(8,128)(2,1)S(1)}, u32[]{:S(2)}, u32[]{:S(2)}) collective-permute-start(bf16[4,128,256]{2,1,0:T(8,128)(2,1)S(1)} %collective-permute-done.1.refs_0_.refs_2_), channel_id=1, source_target_pairs={{0,64},{64,128},{128,192},{192,256},{256,320},{320,384},{384,448},... | collective-permute-start | bytes 786440 | tf_op jit(solution)/shard_map/ppermute | solution.py:187
  47.8 4.5 %collective-permute-start.6 = (bf16[4,128,256]{2,1,0:T(8,128)(2,1)S(1)}, bf16[4,128,256]{2,1,0:T(8,128)(2,1)S(1)}, u32[]{:S(2)}, u32[]{:S(2)}) collective-permute-start(bf16[4,128,256]{2,1,0:T(8,128)(2,1)S(1)} %collective-permute-done.3.refs_1_.refs_3_), channel_id=1, source_target_pairs={{0,448},{64,0},{128,64},{192,128},{256,192},{320,256},{384,320},{4... | collective-permute-start | bytes 786440 | tf_op jit(solution)/shard_map/ppermute | solution.py:187
  52.3 2.4 %collective-permute-done.4.refs_0_ = bf16[4,128,256]{2,1,0:T(8,128)(2,1)S(1)} collective-permute-done((bf16[4,128,256]{2,1,0:T(8,128)(2,1)S(1)}, bf16[4,128,256]{2,1,0:T(8,128)(2,1)S(1)}, u32[]{:S(2)}, u32[]{:S(2)}) %collective-permute-start.4) | collective-permute-done | bytes 262176 | tf_op jit(solution)/shard_map/ppermute | solution.py:187
  54.7 1.9 %collective-permute-start.5 = (bf16[4,128,256]{2,1,0:T(8,128)(2,1)S(1)}, bf16[4,128,256]{2,1,0:T(8,128)(2,1)S(1)}, u32[]{:S(2)}, u32[]{:S(2)}) collective-permute-start(bf16[4,128,256]{2,1,0:T(8,128)(2,1)S(1)} %collective-permute-done.4.refs_0_), channel_id=1, source_target_pairs={{0,64},{64,128},{128,192},{192,256},{256,320},{320,384},{384,448},... | collective-permute-start | bytes 786440 | tf_op jit(solution)/shard_map/ppermute | solution.py:187
  56.7 7.5 %collective-permute-done.5.refs_1_ = bf16[4,128,256]{2,1,0:T(8,128)(2,1)S(1)} collective-permute-done((bf16[4,128,256]{2,1,0:T(8,128)(2,1)S(1)}, bf16[4,128,256]{2,1,0:T(8,128)(2,1)S(1)}, u32[]{:S(2)}, u32[]{:S(2)}) %collective-permute-start.5) | collective-permute-done | bytes 262176 | tf_op jit(solution)/shard_map/ppermute | solution.py:187
  65.7 4.8 %all-to-all-start.2 = ((bf16[4,3,128,256]{3,2,1,0:T(8,128)(2,1)}), bf16[4,3,128,256]{3,2,1,0:T(8,128)(2,1)S(1)}, u32[]{:S(2)}, u32[]{:S(2)}) async-start(bf16[4,3,128,256]{3,2,1,0:T(8,128)(2,1)} %shard_map.65), calls=%async_computation.2 | async-start | bytes 1572864 | tf_op jit(solution)/shard_map/all_to_all | solution.py:291
  71.0 7.5 %all-to-all-done.2 = bf16[4,3,128,256]{3,2,1,0:T(8,128)(2,1)S(1)} async-done(((bf16[4,3,128,256]{3,2,1,0:T(8,128)(2,1)}), bf16[4,3,128,256]{3,2,1,0:T(8,128)(2,1)S(1)}, u32[]{:S(2)}, u32[]{:S(2)}) %all-to-all-start.2) | async-done | bytes 786464 | tf_op jit(solution)/shard_map/all_to_all | solution.py:291
  78.8 14.3 %attention.1.partial_ref = bf16[512,4096]{1,0:T(8,128)(2,1)S(1)} custom-call(s32[64]{0:T(128)S(1)} %reshape.90.slot, s32[64]{0:T(128)S(1)} %reshape.91.base, s32[512,128]{1,0:T(8,128)S(1)} %broadcast_in_dim.98.start_ref, s32[512,128]{1,0:T(8,128)S(1)} %broadcast_in_dim.102.end_ref, bf16[512,512]{1,0:T(8,128)(2,1)S(1)} %copy-done, bf16[512,4096]{1,0:T(8,128)(2,1)} %w_hbm.1, ...), custom_call_target="tpu_custom_call" | custom-call | flops 4294967296 | bytes 4194304 | tf_op jit(solution)/shard_map/attention/pallas_call | solution.py:108
  93.1 4.3 %collective-permute-start.7 = (bf16[256,512]{1,0:T(8,128)(2,1)S(1)}, bf16[256,512]{1,0:T(8,128)(2,1)S(1)}, u32[]{:S(2)}, u32[]{:S(2)}) collective-permute-start(bf16[256,512]{1,0:T(8,128)(2,1)S(1)} %shard_map.66), channel_id=1, source_target_pairs={{0,2},{2,4},{4,6},{6,8},{8,10},{10,12},{12,14},{14,0},{1,3},{3,5},... | collective-permute-start | bytes 786440 | tf_op jit(solution)/shard_map/ppermute | solution.py:187
  97.4 8.6 %collective-permute-start.17 = (bf16[256,512]{1,0:T(8,128)(2,1)S(1)}, bf16[256,512]{1,0:T(8,128)(2,1)S(1)}, u32[]{:S(2)}, u32[]{:S(2)}) collective-permute-start(bf16[256,512]{1,0:T(8,128)(2,1)S(1)} %shard_map.76), channel_id=1, source_target_pairs={{0,14},{2,0},{4,2},{6,4},{8,6},{10,8},{12,10},{14,12},{1,15},{3,1}... | collective-permute-start | bytes 786440 | tf_op jit(solution)/shard_map/ppermute | solution.py:187
  106.1 3.9 %collective-permute-start.11 = (bf16[256,512]{1,0:T(8,128)(2,1)S(1)}, bf16[256,512]{1,0:T(8,128)(2,1)S(1)}, u32[]{:S(2)}, u32[]{:S(2)}) collective-permute-start(bf16[256,512]{1,0:T(8,128)(2,1)S(1)} %shard_map.70), channel_id=1, source_target_pairs={{0,14},{2,0},{4,2},{6,4},{8,6},{10,8},{12,10},{14,12},{1,15},{3,1}... | collective-permute-start | bytes 786440 | tf_op jit(solution)/shard_map/ppermute | solution.py:187
  110.0 1.9 %collective-permute-start.14 = (bf16[256,512]{1,0:T(8,128)(2,1)S(1)}, bf16[256,512]{1,0:T(8,128)(2,1)S(1)}, u32[]{:S(2)}, u32[]{:S(2)}) collective-permute-start(bf16[256,512]{1,0:T(8,128)(2,1)S(1)} %shard_map.73), channel_id=1, source_target_pairs={{0,2},{2,4},{4,6},{6,8},{8,10},{10,12},{12,14},{14,0},{1,3},{3,5},... | collective-permute-start | bytes 786440 | tf_op jit(solution)/shard_map/ppermute | solution.py:187
  112.0 1.9 %collective-permute-start.8 = (bf16[256,512]{1,0:T(8,128)(2,1)S(1)}, bf16[256,512]{1,0:T(8,128)(2,1)S(1)}, u32[]{:S(2)}, u32[]{:S(2)}) collective-permute-start(bf16[256,512]{1,0:T(8,128)(2,1)S(1)} %shard_map.67), channel_id=1, source_target_pairs={{0,2},{2,4},{4,6},{6,8},{8,10},{10,12},{12,14},{14,0},{1,3},{3,5},... | collective-permute-start | bytes 786440 | tf_op jit(solution)/shard_map/ppermute | solution.py:187
  114.1 5.1 %collective-permute-start.18 = (bf16[256,512]{1,0:T(8,128)(2,1)S(1)}, bf16[256,512]{1,0:T(8,128)(2,1)S(1)}, u32[]{:S(2)}, u32[]{:S(2)}) collective-permute-start(bf16[256,512]{1,0:T(8,128)(2,1)S(1)} %shard_map.77), channel_id=1, source_target_pairs={{0,14},{2,0},{4,2},{6,4},{8,6},{10,8},{12,10},{14,12},{1,15},{3,1}... | collective-permute-start | bytes 786440 | tf_op jit(solution)/shard_map/ppermute | solution.py:187
  119.3 3.9 %collective-permute-start.12 = (bf16[256,512]{1,0:T(8,128)(2,1)S(1)}, bf16[256,512]{1,0:T(8,128)(2,1)S(1)}, u32[]{:S(2)}, u32[]{:S(2)}) collective-permute-start(bf16[256,512]{1,0:T(8,128)(2,1)S(1)} %shard_map.71), channel_id=1, source_target_pairs={{0,14},{2,0},{4,2},{6,4},{8,6},{10,8},{12,10},{14,12},{1,15},{3,1}... | collective-permute-start | bytes 786440 | tf_op jit(solution)/shard_map/ppermute | solution.py:187
  123.3 1.9 %collective-permute-start.15 = (bf16[256,512]{1,0:T(8,128)(2,1)S(1)}, bf16[256,512]{1,0:T(8,128)(2,1)S(1)}, u32[]{:S(2)}, u32[]{:S(2)}) collective-permute-start(bf16[256,512]{1,0:T(8,128)(2,1)S(1)} %shard_map.74), channel_id=1, source_target_pairs={{0,2},{2,4},{4,6},{6,8},{8,10},{10,12},{12,14},{14,0},{1,3},{3,5},... | collective-permute-start | bytes 786440 | tf_op jit(solution)/shard_map/ppermute | solution.py:187
  125.3 1.9 %collective-permute-start.9 = (bf16[256,512]{1,0:T(8,128)(2,1)S(1)}, bf16[256,512]{1,0:T(8,128)(2,1)S(1)}, u32[]{:S(2)}, u32[]{:S(2)}) collective-permute-start(bf16[256,512]{1,0:T(8,128)(2,1)S(1)} %shard_map.68), channel_id=1, source_target_pairs={{0,2},{2,4},{4,6},{6,8},{8,10},{10,12},{12,14},{14,0},{1,3},{3,5},... | collective-permute-start | bytes 786440 | tf_op jit(solution)/shard_map/ppermute | solution.py:187
  127.3 5.1 %collective-permute-start.19 = (bf16[256,512]{1,0:T(8,128)(2,1)S(1)}, bf16[256,512]{1,0:T(8,128)(2,1)S(1)}, u32[]{:S(2)}, u32[]{:S(2)}) collective-permute-start(bf16[256,512]{1,0:T(8,128)(2,1)S(1)} %shard_map.78), channel_id=1, source_target_pairs={{0,14},{2,0},{4,2},{6,4},{8,6},{10,8},{12,10},{14,12},{1,15},{3,1}... | collective-permute-start | bytes 786440 | tf_op jit(solution)/shard_map/ppermute | solution.py:187
  132.6 3.9 %collective-permute-start.13 = (bf16[256,512]{1,0:T(8,128)(2,1)S(1)}, bf16[256,512]{1,0:T(8,128)(2,1)S(1)}, u32[]{:S(2)}, u32[]{:S(2)}) collective-permute-start(bf16[256,512]{1,0:T(8,128)(2,1)S(1)} %shard_map.72), channel_id=1, source_target_pairs={{0,14},{2,0},{4,2},{6,4},{8,6},{10,8},{12,10},{14,12},{1,15},{3,1}... | collective-permute-start | bytes 786440 | tf_op jit(solution)/shard_map/ppermute | solution.py:187
  136.6 1.9 %collective-permute-start.16 = (bf16[256,512]{1,0:T(8,128)(2,1)S(1)}, bf16[256,512]{1,0:T(8,128)(2,1)S(1)}, u32[]{:S(2)}, u32[]{:S(2)}) collective-permute-start(bf16[256,512]{1,0:T(8,128)(2,1)S(1)} %shard_map.75), channel_id=1, source_target_pairs={{0,2},{2,4},{4,6},{6,8},{8,10},{10,12},{12,14},{14,0},{1,3},{3,5},... | collective-permute-start | bytes 786440 | tf_op jit(solution)/shard_map/ppermute | solution.py:187
  139.1 1.9 %collective-permute-start.10 = (bf16[256,512]{1,0:T(8,128)(2,1)S(1)}, bf16[256,512]{1,0:T(8,128)(2,1)S(1)}, u32[]{:S(2)}, u32[]{:S(2)}) collective-permute-start(bf16[256,512]{1,0:T(8,128)(2,1)S(1)} %shard_map.69), channel_id=1, source_target_pairs={{0,2},{2,4},{4,6},{6,8},{8,10},{10,12},{12,14},{14,0},{1,3},{3,5},... | collective-permute-start | bytes 786440 | tf_op jit(solution)/shard_map/ppermute | solution.py:187
  141.1 5.1 %collective-permute-start.20 = (bf16[256,512]{1,0:T(8,128)(2,1)S(1)}, bf16[256,512]{1,0:T(8,128)(2,1)S(1)}, u32[]{:S(2)}, u32[]{:S(2)}) collective-permute-start(bf16[256,512]{1,0:T(8,128)(2,1)S(1)} %shard_map.79), channel_id=1, source_target_pairs={{0,14},{2,0},{4,2},{6,4},{8,6},{10,8},{12,10},{14,12},{1,15},{3,1}... | collective-permute-start | bytes 786440 | tf_op jit(solution)/shard_map/ppermute | solution.py:187
  146.2 2.6 %collective-permute-done.10.refs_0_ = bf16[256,512]{1,0:T(8,128)(2,1)S(1)} collective-permute-done((bf16[256,512]{1,0:T(8,128)(2,1)S(1)}, bf16[256,512]{1,0:T(8,128)(2,1)S(1)}, u32[]{:S(2)}, u32[]{:S(2)}) %collective-permute-start.10) | collective-permute-done | bytes 262176 | tf_op jit(solution)/shard_map/ppermute | solution.py:187
  (64 shorter events, 9.7 us)
Async XLA Ops:
  1.0 10.9 %collective-permute-start.2 = (bf16[4,128,256]{2,1,0:T(8,128)(2,1)S(1)}, bf16[4,128,256]{2,1,0:T(8,128)(2,1)S(1)}, u32[]{:S(2)}, u32[]{:S(2)}) collective-permute-start(bf16[4,128,256]{2,1,0:T(8,128)(2,1)S(1)} %bitcast.7), channel_id=1, source_target_pairs={{0,448},{64,0},{128,64},{192,128},{256,192},{320,256},{384,320},{4... | collective-permute-start | bytes 786440 | tf_op jit(solution)/shard_map/ppermute | solution.py:187
  6.4 11.1 %collective-permute-start = (bf16[4,128,256]{2,1,0:T(8,128)(2,1)S(1)}, bf16[4,128,256]{2,1,0:T(8,128)(2,1)S(1)}, u32[]{:S(2)}, u32[]{:S(2)}) collective-permute-start(bf16[4,128,256]{2,1,0:T(8,128)(2,1)S(1)} %bitcast.8), channel_id=1, source_target_pairs={{0,64},{64,128},{128,192},{192,256},{256,320},{320,384},{384,448},... | collective-permute-start | bytes 786440 | tf_op jit(solution)/shard_map/ppermute | solution.py:187
  11.9 26.1 %collective-permute-start.3 = (bf16[4,128,256]{2,1,0:T(8,128)(2,1)S(1)}, bf16[4,128,256]{2,1,0:T(8,128)(2,1)S(1)}, u32[]{:S(2)}, u32[]{:S(2)}) collective-permute-start(bf16[4,128,256]{2,1,0:T(8,128)(2,1)S(1)} %collective-permute-done.2.refs_4_), channel_id=1, source_target_pairs={{0,448},{64,0},{128,64},{192,128},{256,192},{320,256},{384,320},{4... | collective-permute-start | bytes 786440 | tf_op jit(solution)/shard_map/ppermute | solution.py:187
  17.5 20.5 %collective-permute-start.1 = (bf16[4,128,256]{2,1,0:T(8,128)(2,1)S(1)}, bf16[4,128,256]{2,1,0:T(8,128)(2,1)S(1)}, u32[]{:S(2)}, u32[]{:S(2)}) collective-permute-start(bf16[4,128,256]{2,1,0:T(8,128)(2,1)S(1)} %collective-permute-done.refs_1_), channel_id=1, source_target_pairs={{0,64},{64,128},{128,192},{192,256},{256,320},{320,384},{384,448},... | collective-permute-start | bytes 786440 | tf_op jit(solution)/shard_map/ppermute | solution.py:187
  21.7 16.3 %all-to-all-start = ((s32[32,1,72]{2,1,0:T(1,128)}), s32[32,1,72]{2,1,0:T(1,128)S(1)}, u32[]{:S(2)}, u32[]{:S(2)}) async-start(s32[32,1,72]{2,1,0:T(1,128)} %broadcast_in_dim.95), calls=%async_computation | async-start | bytes 32768 | tf_op jit(solution)/shard_map/all_to_all | solution.py:265
  38.6 31.9 %copy-start.1 = (s32[4,16]{1,0:T(4,128)S(1)}, s32[4,16]{1,0:T(4,128)}, u32[]{:S(2)}) copy-start(s32[4,16]{1,0:T(4,128)} %param.10) | copy-start | bytes 772
  38.6 32.3 %copy-start.2 = (s32[512]{0:T(512)S(1)}, s32[512]{0:T(512)}, u32[]{:S(2)}) copy-start(s32[512]{0:T(512)} %param.9) | copy-start | bytes 6148
  38.6 40.2 %copy-start = (bf16[512,512]{1,0:T(8,128)(2,1)S(1)}, bf16[512,512]{1,0:T(8,128)(2,1)}, u32[]{:S(2)}) copy-start(bf16[512,512]{1,0:T(8,128)(2,1)} %q_hbm.1) | copy-start | bytes 1572868
  40.3 25.4 %all-to-all-start.1 = ((bf16[4,5,128,256]{3,2,1,0:T(8,128)(2,1)}), bf16[4,5,128,256]{3,2,1,0:T(8,128)(2,1)S(1)}, u32[]{:S(2)}, u32[]{:S(2)}) async-start(bf16[4,5,128,256]{3,2,1,0:T(8,128)(2,1)} %shard_map.64), calls=%async_computation.1 | async-start | bytes 2621440 | tf_op jit(solution)/shard_map/all_to_all | solution.py:291
  45.2 9.5 %collective-permute-start.4 = (bf16[4,128,256]{2,1,0:T(8,128)(2,1)S(1)}, bf16[4,128,256]{2,1,0:T(8,128)(2,1)S(1)}, u32[]{:S(2)}, u32[]{:S(2)}) collective-permute-start(bf16[4,128,256]{2,1,0:T(8,128)(2,1)S(1)} %collective-permute-done.1.refs_0_.refs_2_), channel_id=1, source_target_pairs={{0,64},{64,128},{128,192},{192,256},{256,320},{320,384},{384,448},... | collective-permute-start | bytes 786440 | tf_op jit(solution)/shard_map/ppermute | solution.py:187
  47.8 8.9 %collective-permute-start.6 = (bf16[4,128,256]{2,1,0:T(8,128)(2,1)S(1)}, bf16[4,128,256]{2,1,0:T(8,128)(2,1)S(1)}, u32[]{:S(2)}, u32[]{:S(2)}) collective-permute-start(bf16[4,128,256]{2,1,0:T(8,128)(2,1)S(1)} %collective-permute-done.3.refs_1_.refs_3_), channel_id=1, source_target_pairs={{0,448},{64,0},{128,64},{192,128},{256,192},{320,256},{384,320},{4... | collective-permute-start | bytes 786440 | tf_op jit(solution)/shard_map/ppermute | solution.py:187
  54.7 9.5 %collective-permute-start.5 = (bf16[4,128,256]{2,1,0:T(8,128)(2,1)S(1)}, bf16[4,128,256]{2,1,0:T(8,128)(2,1)S(1)}, u32[]{:S(2)}, u32[]{:S(2)}) collective-permute-start(bf16[4,128,256]{2,1,0:T(8,128)(2,1)S(1)} %collective-permute-done.4.refs_0_), channel_id=1, source_target_pairs={{0,64},{64,128},{128,192},{192,256},{256,320},{320,384},{384,448},... | collective-permute-start | bytes 786440 | tf_op jit(solution)/shard_map/ppermute | solution.py:187
  65.7 12.8 %all-to-all-start.2 = ((bf16[4,3,128,256]{3,2,1,0:T(8,128)(2,1)}), bf16[4,3,128,256]{3,2,1,0:T(8,128)(2,1)S(1)}, u32[]{:S(2)}, u32[]{:S(2)}) async-start(bf16[4,3,128,256]{3,2,1,0:T(8,128)(2,1)} %shard_map.65), calls=%async_computation.2 | async-start | bytes 1572864 | tf_op jit(solution)/shard_map/all_to_all | solution.py:291
  93.1 18.9 %collective-permute-start.7 = (bf16[256,512]{1,0:T(8,128)(2,1)S(1)}, bf16[256,512]{1,0:T(8,128)(2,1)S(1)}, u32[]{:S(2)}, u32[]{:S(2)}) collective-permute-start(bf16[256,512]{1,0:T(8,128)(2,1)S(1)} %shard_map.66), channel_id=1, source_target_pairs={{0,2},{2,4},{4,6},{6,8},{8,10},{10,12},{12,14},{14,0},{1,3},{3,5},... | collective-permute-start | bytes 786440 | tf_op jit(solution)/shard_map/ppermute | solution.py:187
  97.4 16.5 %collective-permute-start.17 = (bf16[256,512]{1,0:T(8,128)(2,1)S(1)}, bf16[256,512]{1,0:T(8,128)(2,1)S(1)}, u32[]{:S(2)}, u32[]{:S(2)}) collective-permute-start(bf16[256,512]{1,0:T(8,128)(2,1)S(1)} %shard_map.76), channel_id=1, source_target_pairs={{0,14},{2,0},{4,2},{6,4},{8,6},{10,8},{12,10},{14,12},{1,15},{3,1}... | collective-permute-start | bytes 786440 | tf_op jit(solution)/shard_map/ppermute | solution.py:187
  106.1 13.1 %collective-permute-start.11 = (bf16[256,512]{1,0:T(8,128)(2,1)S(1)}, bf16[256,512]{1,0:T(8,128)(2,1)S(1)}, u32[]{:S(2)}, u32[]{:S(2)}) collective-permute-start(bf16[256,512]{1,0:T(8,128)(2,1)S(1)} %shard_map.70), channel_id=1, source_target_pairs={{0,14},{2,0},{4,2},{6,4},{8,6},{10,8},{12,10},{14,12},{1,15},{3,1}... | collective-permute-start | bytes 786440 | tf_op jit(solution)/shard_map/ppermute | solution.py:187
  110.0 13.2 %collective-permute-start.14 = (bf16[256,512]{1,0:T(8,128)(2,1)S(1)}, bf16[256,512]{1,0:T(8,128)(2,1)S(1)}, u32[]{:S(2)}, u32[]{:S(2)}) collective-permute-start(bf16[256,512]{1,0:T(8,128)(2,1)S(1)} %shard_map.73), channel_id=1, source_target_pairs={{0,2},{2,4},{4,6},{6,8},{8,10},{10,12},{12,14},{14,0},{1,3},{3,5},... | collective-permute-start | bytes 786440 | tf_op jit(solution)/shard_map/ppermute | solution.py:187
  112.0 13.2 %collective-permute-start.8 = (bf16[256,512]{1,0:T(8,128)(2,1)S(1)}, bf16[256,512]{1,0:T(8,128)(2,1)S(1)}, u32[]{:S(2)}, u32[]{:S(2)}) collective-permute-start(bf16[256,512]{1,0:T(8,128)(2,1)S(1)} %shard_map.67), channel_id=1, source_target_pairs={{0,2},{2,4},{4,6},{6,8},{8,10},{10,12},{12,14},{14,0},{1,3},{3,5},... | collective-permute-start | bytes 786440 | tf_op jit(solution)/shard_map/ppermute | solution.py:187
  114.1 13.2 %collective-permute-start.18 = (bf16[256,512]{1,0:T(8,128)(2,1)S(1)}, bf16[256,512]{1,0:T(8,128)(2,1)S(1)}, u32[]{:S(2)}, u32[]{:S(2)}) collective-permute-start(bf16[256,512]{1,0:T(8,128)(2,1)S(1)} %shard_map.77), channel_id=1, source_target_pairs={{0,14},{2,0},{4,2},{6,4},{8,6},{10,8},{12,10},{14,12},{1,15},{3,1}... | collective-permute-start | bytes 786440 | tf_op jit(solution)/shard_map/ppermute | solution.py:187
  119.3 13.2 %collective-permute-start.12 = (bf16[256,512]{1,0:T(8,128)(2,1)S(1)}, bf16[256,512]{1,0:T(8,128)(2,1)S(1)}, u32[]{:S(2)}, u32[]{:S(2)}) collective-permute-start(bf16[256,512]{1,0:T(8,128)(2,1)S(1)} %shard_map.71), channel_id=1, source_target_pairs={{0,14},{2,0},{4,2},{6,4},{8,6},{10,8},{12,10},{14,12},{1,15},{3,1}... | collective-permute-start | bytes 786440 | tf_op jit(solution)/shard_map/ppermute | solution.py:187
  123.3 13.2 %collective-permute-start.15 = (bf16[256,512]{1,0:T(8,128)(2,1)S(1)}, bf16[256,512]{1,0:T(8,128)(2,1)S(1)}, u32[]{:S(2)}, u32[]{:S(2)}) collective-permute-start(bf16[256,512]{1,0:T(8,128)(2,1)S(1)} %shard_map.74), channel_id=1, source_target_pairs={{0,2},{2,4},{4,6},{6,8},{8,10},{10,12},{12,14},{14,0},{1,3},{3,5},... | collective-permute-start | bytes 786440 | tf_op jit(solution)/shard_map/ppermute | solution.py:187
  125.3 13.7 %collective-permute-start.9 = (bf16[256,512]{1,0:T(8,128)(2,1)S(1)}, bf16[256,512]{1,0:T(8,128)(2,1)S(1)}, u32[]{:S(2)}, u32[]{:S(2)}) collective-permute-start(bf16[256,512]{1,0:T(8,128)(2,1)S(1)} %shard_map.68), channel_id=1, source_target_pairs={{0,2},{2,4},{4,6},{6,8},{8,10},{10,12},{12,14},{14,0},{1,3},{3,5},... | collective-permute-start | bytes 786440 | tf_op jit(solution)/shard_map/ppermute | solution.py:187
  127.3 13.7 %collective-permute-start.19 = (bf16[256,512]{1,0:T(8,128)(2,1)S(1)}, bf16[256,512]{1,0:T(8,128)(2,1)S(1)}, u32[]{:S(2)}, u32[]{:S(2)}) collective-permute-start(bf16[256,512]{1,0:T(8,128)(2,1)S(1)} %shard_map.78), channel_id=1, source_target_pairs={{0,14},{2,0},{4,2},{6,4},{8,6},{10,8},{12,10},{14,12},{1,15},{3,1}... | collective-permute-start | bytes 786440 | tf_op jit(solution)/shard_map/ppermute | solution.py:187
  132.6 13.7 %collective-permute-start.13 = (bf16[256,512]{1,0:T(8,128)(2,1)S(1)}, bf16[256,512]{1,0:T(8,128)(2,1)S(1)}, u32[]{:S(2)}, u32[]{:S(2)}) collective-permute-start(bf16[256,512]{1,0:T(8,128)(2,1)S(1)} %shard_map.72), channel_id=1, source_target_pairs={{0,14},{2,0},{4,2},{6,4},{8,6},{10,8},{12,10},{14,12},{1,15},{3,1}... | collective-permute-start | bytes 786440 | tf_op jit(solution)/shard_map/ppermute | solution.py:187
  136.6 9.7 %collective-permute-start.16 = (bf16[256,512]{1,0:T(8,128)(2,1)S(1)}, bf16[256,512]{1,0:T(8,128)(2,1)S(1)}, u32[]{:S(2)}, u32[]{:S(2)}) collective-permute-start(bf16[256,512]{1,0:T(8,128)(2,1)S(1)} %shard_map.75), channel_id=1, source_target_pairs={{0,2},{2,4},{4,6},{6,8},{8,10},{10,12},{12,14},{14,0},{1,3},{3,5},... | collective-permute-start | bytes 786440 | tf_op jit(solution)/shard_map/ppermute | solution.py:187
  139.1 9.8 %collective-permute-start.10 = (bf16[256,512]{1,0:T(8,128)(2,1)S(1)}, bf16[256,512]{1,0:T(8,128)(2,1)S(1)}, u32[]{:S(2)}, u32[]{:S(2)}) collective-permute-start(bf16[256,512]{1,0:T(8,128)(2,1)S(1)} %shard_map.69), channel_id=1, source_target_pairs={{0,2},{2,4},{4,6},{6,8},{8,10},{10,12},{12,14},{14,0},{1,3},{3,5},... | collective-permute-start | bytes 786440 | tf_op jit(solution)/shard_map/ppermute | solution.py:187
  141.1 9.0 %collective-permute-start.20 = (bf16[256,512]{1,0:T(8,128)(2,1)S(1)}, bf16[256,512]{1,0:T(8,128)(2,1)S(1)}, u32[]{:S(2)}, u32[]{:S(2)}) collective-permute-start(bf16[256,512]{1,0:T(8,128)(2,1)S(1)} %shard_map.79), channel_id=1, source_target_pairs={{0,14},{2,0},{4,2},{6,4},{8,6},{10,8},{12,10},{14,12},{1,15},{3,1}... | collective-permute-start | bytes 786440 | tf_op jit(solution)/shard_map/ppermute | solution.py:187
where the time goes:
time: 152 us; the launch traced here: 151 us
  starting transfers between devices  92.8 us (61%)
  waiting for transfers between devices  33.8 us (22%)
  Pallas kernels  19.3 us (13%)
  other arithmetic  2.56 us (2%)
  local copies, waits for them, and re-layouts  2.12 us (1%)
    ppermute x21, starting transfers between devices, shifted(): return lax.ppermute(x, axis, [(i, (i + shift) % size) for i in range(size)])  75.3 us
    ppermute x21, waiting for transfers between devices, shifted(): return lax.ppermute(x, axis, [(i, (i + shift) % size) for i in range(size)])  17.8 us
    pallas_call x1, Pallas kernels, attention(): pl.pallas_call(attention_kernel, out_shape=jax.ShapeDtypeStruct((tokens,...  14.3 us
    all_to_all x2, starting transfers between devices, per_device(): arrived = lax.all_to_all(outgoing, 'x', 0, 0, tiled=True)  9.75 us
    all_to_all x1, waiting for transfers between devices, per_device(): info = lax.all_to_all(info, ('y', 'x'), 0, 0, tiled=True)  8.46 us
    all_to_all x1, starting transfers between devices, per_device(): info = lax.all_to_all(info, ('y', 'x'), 0, 0, tiled=True)  7.78 us
    all_to_all x2, waiting for transfers between devices, per_device(): arrived = lax.all_to_all(outgoing, 'x', 0, 0, tiled=True)  7.52 us
    pallas_call x17, Pallas kernels, small_kernel(): pl.pallas_call(body, out_shape=out_shape, in_specs=[pl.BlockSpec(memory_s...  4.99 us
  transfers between devices with their start and end apart: 24, of which 8 were waited for; matrix products, arithmetic and copies ran while one was open for 2% of the time, Pallas kernels for 2%

commit v1 on v0

--- a/solution.py
+++ b/solution.py
@@ -13,7 +13,9 @@
 BLOCK_TOKENS = 128
 DOCS = 8
 TOPK = 16
-CHUNK = 4
+CHUNK = 2
+SPLIT = 2
+WIDTH = 512
 
 negative = -1e30
 far_position = 1073741824
@@ -56,7 +58,8 @@
     starts = start_ref[...]
     ends = end_ref[...]
     lane = lax.broadcasted_iota(jnp.int32, (BLOCK_TOKENS, BLOCK_TOKENS), 1)
-    peak = None
+    stacked = heads * BLOCK_TOKENS
+    peaks = [None] * SPLIT
     for c in range(TOPK // CHUNK):
         cols = slice(c * keys, (c + 1) * keys)
         bias = []
@@ -64,38 +67,52 @@
             position = lane + base[row * TOPK + j]
             allowed = (position >= starts) & (position < ends)
             bias.append(jnp.where(allowed, 0.0, negative))
-        bias = jnp.concatenate(bias, axis=1)
-        raw = lax.dot_general(
-            q4[...], kcat[cols, :], (((1,), (1,)), ((), ())), preferred_element_type=jnp.float32
-        )
-        for h in range(heads):
-            rows = slice(h * BLOCK_TOKENS, (h + 1) * BLOCK_TOKENS)
-            scores[rows, cols] = raw[rows] * score_scale + bias
-        part = scores[:, cols]
-        for j in range(CHUNK):
-            piece = part[:, j * BLOCK_TOKENS : (j + 1) * BLOCK_TOKENS]
-            peak = piece if peak is None else jnp.maximum(peak, piece)
-    top = jnp.max(peak, axis=1, keepdims=True)
-    total = jnp.zeros((heads * BLOCK_TOKENS, 2 * HEAD_SIZE), jnp.float32)
+        for r in range(SPLIT):
+            first = r * (stacked // SPLIT)
+            raw = lax.dot_general(
+                q4[first : first + stacked // SPLIT, :],
+                kcat[cols, :],
+                (((1,), (1,)), ((), ())),
+                preferred_element_type=jnp.float32,
+            )
+            parts = []
+            for h in range(stacked // SPLIT // BLOCK_TOKENS):
+                at = slice(h * BLOCK_TOKENS, (h + 1) * BLOCK_TOKENS)
+                largest = None
+                for j in range(CHUNK):
+                    lanes = slice(j * BLOCK_TOKENS, (j + 1) * BLOCK_TOKENS)
+                    piece = raw[at, lanes] + bias[j]
+                    scores[
+                        first + h * BLOCK_TOKENS : first + (h + 1) * BLOCK_TOKENS,
+                        (c * CHUNK + j) * BLOCK_TOKENS : (c * CHUNK + j + 1) * BLOCK_TOKENS,
+                    ] = piece
+                    largest = piece if largest is None else jnp.maximum(largest, piece)
+                parts.append(largest)
+            largest = jnp.concatenate(parts, axis=0)
+            peaks[r] = largest if c == 0 else jnp.maximum(peaks[r], largest)
+    tops = [jnp.max(peak, axis=1, keepdims=True) for peak in peaks]
+    totals = [jnp.zeros((stacked // SPLIT, 2 * HEAD_SIZE), jnp.float32)] * SPLIT
     for c in range(TOPK // CHUNK):
         cols = slice(c * keys, (c + 1) * keys)
-        weights = jnp.exp2(scores[:, cols] - top).astype(jnp.bfloat16)
-        total += jnp.dot(weights, vcat[cols, :], preferred_element_type=jnp.float32)
-    result = (total[:, :HEAD_SIZE] / total[:, HEAD_SIZE:]).astype(attn.dtype)
-    for h in range(heads):
-        attn[:, h * HEAD_SIZE : (h + 1) * HEAD_SIZE] = result[
-            h * BLOCK_TOKENS : (h + 1) * BLOCK_TOKENS
-        ]
-
-    @pl.when(row == 0)
+        for r in range(SPLIT):
+            at = slice(r * (stacked // SPLIT), (r + 1) * (stacked // SPLIT))
+            weights = jnp.exp2((scores[at, cols] - tops[r]) * score_scale).astype(jnp.bfloat16)
+            totals[r] += jnp.dot(weights, vcat[cols, :], preferred_element_type=jnp.float32)
+    for r in range(SPLIT):
+        result = (totals[r][:, :HEAD_SIZE] / totals[r][:, HEAD_SIZE:]).astype(attn.dtype)
+        for h in range(heads // SPLIT):
+            column = (r * (heads // SPLIT) + h) * HEAD_SIZE
+            attn[own, column : column + HEAD_SIZE] = result[
+                h * BLOCK_TOKENS : (h + 1) * BLOCK_TOKENS
+            ]
+
+    @pl.when(row == pl.num_programs(0) - 1)
     def _():
         w_copy.wait()
-
-    step = 1024
-    for c in range(0, w_ref.shape[1], step):
-        out_ref[:, c : c + step] = jnp.dot(
-            attn[...], w_ref[:, c : c + step], preferred_element_type=jnp.float32
-        ).astype(out_ref.dtype)
+        for c in range(0, w_ref.shape[1], WIDTH):
+            out_ref[:, c : c + WIDTH] = jnp.dot(
+                attn[...], w_ref[:, c : c + WIDTH], preferred_element_type=jnp.float32
+            ).astype(out_ref.dtype)
 
 
 def attention(queries, starts, ends, w_out, pieces, slot, base):
@@ -116,7 +133,7 @@
                 pl.BlockSpec((BLOCK_TOKENS, BLOCK_TOKENS), per_block),
                 *[pl.BlockSpec(memory_space=pl.ANY)] * (2 + len(pieces)),
             ],
-            out_specs=pl.BlockSpec((BLOCK_TOKENS, w_out.shape[1]), per_block),
+            out_specs=pl.BlockSpec(memory_space=pltpu.VMEM),
             scratch_shapes=[
                 pltpu.VMEM(table, jnp.bfloat16),
                 pltpu.VMEM(queries.shape, queries.dtype),
@@ -124,7 +141,7 @@
                 pltpu.VMEM((listed, HEAD_SIZE), jnp.bfloat16),
                 pltpu.VMEM((listed, 2 * HEAD_SIZE), jnp.bfloat16),
                 pltpu.VMEM((rows, listed), jnp.float32),
-                pltpu.VMEM((BLOCK_TOKENS, width), jnp.bfloat16),
+                pltpu.VMEM((tokens, width), jnp.bfloat16),
                 pltpu.VMEM(w_out.shape, w_out.dtype),
                 pltpu.SemaphoreType.DMA((2 + len(pieces),)),
             ],
@@ -260,22 +277,21 @@
     first_local = jnp.min(
         jnp.where(doc_ids[None, :] == doc_range[:, None], positions[None, :], far_position), axis=1
     )
-    info = jnp.concatenate([block_lists.reshape(-1), first_local])
-    info = jnp.broadcast_to(info[None], (seq_count, info.shape[0]))
+    first_local = jnp.pad(first_local, (0, TOPK - DOCS), constant_values=far_position)
+    info = jnp.concatenate([block_lists, first_local[None]], axis=0)
+    info = jnp.broadcast_to(info[None], (seq_count, *info.shape))
     info = lax.all_to_all(info, ("y", "x"), 0, 0, tiled=True)
     quarter = y_count // 4
     info = hold(info, column[quarter], column[-quarter])
-    entries = blocks_dev * TOPK
-    listing = info[:, :entries]
-    firsts = jnp.min(info[:, entries:], axis=0)
+    listing = info[:, :blocks_dev]
+    firsts = jnp.min(info[:, blocks_dev, :DOCS], axis=0)
 
     readers = lax.dynamic_slice_in_dim(listing, own_y * x_count, x_count, 0)
     back = jnp.arange(y_count, dtype=jnp.int32)
     owners = (own_y - back + y_count) % y_count * x_count + own_x
-    wanted = (readers[:, None, :] < block_count) & (
-        readers[:, None, :] // blocks_dev == owners[None, :, None]
-    )
-    row_offset = jnp.max(jnp.where(wanted, readers[:, None, :] % blocks_dev, 0), axis=2)
+    readers = readers[:, None]
+    wanted = (readers < block_count) & (readers // blocks_dev == owners[None, :, None, None])
+    row_offset = jnp.max(jnp.where(wanted, readers % blocks_dev, 0), axis=(2, 3))
     reach = [min(d, y_count - d) for d in range(y_count)]
     near = [d for d in range(y_count) if reach[d] <= y_count // 4]
     far = [d for d in range(y_count) if reach[d] > y_count // 4]

time: 152 us -> 147 us (0.967)
  Pallas kernels: 19.3 us -> 14.5 us
    pallas_call x1, Pallas kernels: 14.3 us -> 9.46 us  [attention(): pl.pallas_call(attention_kernel, out_shape=jax.ShapeDtypeStruct((tokens,...]
where the time goes in v1:
time: 147 us; the launch traced here: 146 us
  starting transfers between devices  93.3 us (63%)
  waiting for transfers between devices  33.5 us (23%)
  Pallas kernels  14.5 us (10%)
  other arithmetic  3.14 us (2%)
    ppermute x21, starting transfers between devices, shifted(): return lax.ppermute(x, axis, [(i, (i + shift) % size) for i in range(size)])  75.3 us
    ppermute x21, waiting for transfers between devices, shifted(): return lax.ppermute(x, axis, [(i, (i + shift) % size) for i in range(size)])  17.1 us
    all_to_all x2, starting transfers between devices, per_device(): arrived = lax.all_to_all(outgoing, 'x', 0, 0, tiled=True)  10.2 us
    pallas_call x1, Pallas kernels, attention(): pl.pallas_call(attention_kernel, out_shape=jax.ShapeDtypeStruct((tokens,...  9.46 us
    all_to_all x1, waiting for transfers between devices, per_device(): info = lax.all_to_all(info, ('y', 'x'), 0, 0, tiled=True)  8.84 us
    all_to_all x1, starting transfers between devices, per_device(): info = lax.all_to_all(info, ('y', 'x'), 0, 0, tiled=True)  7.78 us
    all_to_all x2, waiting for transfers between devices, per_device(): arrived = lax.all_to_all(outgoing, 'x', 0, 0, tiled=True)  7.56 us
    pallas_call x17, Pallas kernels, small_kernel(): pl.pallas_call(body, out_shape=out_shape, in_specs=[pl.BlockSpec(memory_s...  4.99 us
  transfers between devices with their start and end apart: 24, of which 8 were waited for; matrix products, arithmetic and copies ran while one was open for 2% of the time, Pallas kernels for 2%

profile of v1, /device:TPU:2, one launch (start us, length us, event | category | flops | bytes accessed | tf_op | source)
XLA Modules:
  0.0 146.3 jit_solution(4361939054599373192)
XLA Ops:
  1.0 5.4 %collective-permute-start.2 = (bf16[4,128,256]{2,1,0:T(8,128)(2,1)S(1)}, bf16[4,128,256]{2,1,0:T(8,128)(2,1)S(1)}, u32[]{:S(2)}, u32[]{:S(2)}) collective-permute-start(bf16[4,128,256]{2,1,0:T(8,128)(2,1)S(1)} %bitcast.7), channel_id=1, source_target_pairs={{0,448},{64,0},{128,64},{192,128},{256,192},{320,256},{384,320},{4... | collective-permute-start | bytes 786440 | tf_op jit(solution)/shard_map/ppermute | solution.py:204
  6.4 1.9 %collective-permute-start = (bf16[4,128,256]{2,1,0:T(8,128)(2,1)S(1)}, bf16[4,128,256]{2,1,0:T(8,128)(2,1)S(1)}, u32[]{:S(2)}, u32[]{:S(2)}) collective-permute-start(bf16[4,128,256]{2,1,0:T(8,128)(2,1)S(1)} %bitcast.8), channel_id=1, source_target_pairs={{0,64},{64,128},{128,192},{192,256},{256,320},{320,384},{384,448},... | collective-permute-start | bytes 786440 | tf_op jit(solution)/shard_map/ppermute | solution.py:204
  9.1 2.8 %collective-permute-done.2.refs_4_ = bf16[4,128,256]{2,1,0:T(8,128)(2,1)S(1)} collective-permute-done((bf16[4,128,256]{2,1,0:T(8,128)(2,1)S(1)}, bf16[4,128,256]{2,1,0:T(8,128)(2,1)S(1)}, u32[]{:S(2)}, u32[]{:S(2)}) %collective-permute-start.2) | collective-permute-done | bytes 262176 | tf_op jit(solution)/shard_map/ppermute | solution.py:204
  11.9 5.6 %collective-permute-start.3 = (bf16[4,128,256]{2,1,0:T(8,128)(2,1)S(1)}, bf16[4,128,256]{2,1,0:T(8,128)(2,1)S(1)}, u32[]{:S(2)}, u32[]{:S(2)}) collective-permute-start(bf16[4,128,256]{2,1,0:T(8,128)(2,1)S(1)} %collective-permute-done.2.refs_4_), channel_id=1, source_target_pairs={{0,448},{64,0},{128,64},{192,128},{256,192},{320,256},{384,320},{4... | collective-permute-start | bytes 786440 | tf_op jit(solution)/shard_map/ppermute | solution.py:204
  17.5 1.9 %collective-permute-start.1 = (bf16[4,128,256]{2,1,0:T(8,128)(2,1)S(1)}, bf16[4,128,256]{2,1,0:T(8,128)(2,1)S(1)}, u32[]{:S(2)}, u32[]{:S(2)}) collective-permute-start(bf16[4,128,256]{2,1,0:T(8,128)(2,1)S(1)} %collective-permute-done.refs_1_), channel_id=1, source_target_pairs={{0,64},{64,128},{128,192},{192,256},{256,320},{320,384},{384,448},... | collective-permute-start | bytes 786440 | tf_op jit(solution)/shard_map/ppermute | solution.py:204
  20.8 7.8 %all-to-all-start = ((s32[32,5,16]{2,1,0:T(8,128)}), s32[32,5,16]{2,1,0:T(8,128)S(1)}, u32[]{:S(2)}, u32[]{:S(2)}) async-start(s32[32,5,16]{2,1,0:T(8,128)} %broadcast_in_dim.97), calls=%async_computation | async-start | bytes 262144 | tf_op jit(solution)/shard_map/all_to_all | solution.py:283
  28.6 8.8 %all-to-all-done.source_ref = s32[32,5,16]{2,1,0:T(8,128)S(1)} async-done(((s32[32,5,16]{2,1,0:T(8,128)}), s32[32,5,16]{2,1,0:T(8,128)S(1)}, u32[]{:S(2)}, u32[]{:S(2)}) %all-to-all-start) | async-done | bytes 10272 | tf_op jit(solution)/shard_map/all_to_all | solution.py:283
  38.1 1.7 %shard_map.64 = bf16[4,5,128,256]{3,2,1,0:T(8,128)(2,1)} custom-call(s32[20]{0:T(128)S(1)} %reshape.85.index, bf16[4,128,256]{2,1,0:T(8,128)(2,1)S(1)} %bitcast.9, bf16[4,128,256]{2,1,0:T(8,128)(2,1)S(1)} %collective-permute-done.refs_1_, bf16[4,128,256]{2,1,0:T(8,128)(2,1)S(1)} %collective-permute-done.1.refs_0_.refs_2_, ...), custom_call_target="tpu_custom_call" | custom-call | flops 1048576 | bytes 1048576 | tf_op jit(solution)/shard_map/pallas_call | solution.py:167
  39.8 5.4 %all-to-all-start.1 = ((bf16[4,5,128,256]{3,2,1,0:T(8,128)(2,1)}), bf16[4,5,128,256]{3,2,1,0:T(8,128)(2,1)S(1)}, u32[]{:S(2)}, u32[]{:S(2)}) async-start(bf16[4,5,128,256]{3,2,1,0:T(8,128)(2,1)} %shard_map.64), calls=%async_computation.1 | async-start | bytes 2621440 | tf_op jit(solution)/shard_map/all_to_all | solution.py:307
  45.2 2.7 %collective-permute-start.4 = (bf16[4,128,256]{2,1,0:T(8,128)(2,1)S(1)}, bf16[4,128,256]{2,1,0:T(8,128)(2,1)S(1)}, u32[]{:S(2)}, u32[]{:S(2)}) collective-permute-start(bf16[4,128,256]{2,1,0:T(8,128)(2,1)S(1)} %collective-permute-done.1.refs_0_.refs_2_), channel_id=1, source_target_pairs={{0,64},{64,128},{128,192},{192,256},{256,320},{320,384},{384,448},... | collective-permute-start | bytes 786440 | tf_op jit(solution)/shard_map/ppermute | solution.py:204
  48.0 4.3 %collective-permute-start.6 = (bf16[4,128,256]{2,1,0:T(8,128)(2,1)S(1)}, bf16[4,128,256]{2,1,0:T(8,128)(2,1)S(1)}, u32[]{:S(2)}, u32[]{:S(2)}) collective-permute-start(bf16[4,128,256]{2,1,0:T(8,128)(2,1)S(1)} %collective-permute-done.3.refs_1_.refs_3_), channel_id=1, source_target_pairs={{0,448},{64,0},{128,64},{192,128},{256,192},{320,256},{384,320},{4... | collective-permute-start | bytes 786440 | tf_op jit(solution)/shard_map/ppermute | solution.py:204
  52.3 2.4 %collective-permute-done.4.refs_0_ = bf16[4,128,256]{2,1,0:T(8,128)(2,1)S(1)} collective-permute-done((bf16[4,128,256]{2,1,0:T(8,128)(2,1)S(1)}, bf16[4,128,256]{2,1,0:T(8,128)(2,1)S(1)}, u32[]{:S(2)}, u32[]{:S(2)}) %collective-permute-start.4) | collective-permute-done | bytes 262176 | tf_op jit(solution)/shard_map/ppermute | solution.py:204
  54.7 1.9 %collective-permute-start.5 = (bf16[4,128,256]{2,1,0:T(8,128)(2,1)S(1)}, bf16[4,128,256]{2,1,0:T(8,128)(2,1)S(1)}, u32[]{:S(2)}, u32[]{:S(2)}) collective-permute-start(bf16[4,128,256]{2,1,0:T(8,128)(2,1)S(1)} %collective-permute-done.4.refs_0_), channel_id=1, source_target_pairs={{0,64},{64,128},{128,192},{192,256},{256,320},{320,384},{384,448},... | collective-permute-start | bytes 786440 | tf_op jit(solution)/shard_map/ppermute | solution.py:204
  56.7 7.5 %collective-permute-done.5.refs_1_ = bf16[4,128,256]{2,1,0:T(8,128)(2,1)S(1)} collective-permute-done((bf16[4,128,256]{2,1,0:T(8,128)(2,1)S(1)}, bf16[4,128,256]{2,1,0:T(8,128)(2,1)S(1)}, u32[]{:S(2)}, u32[]{:S(2)}) %collective-permute-start.5) | collective-permute-done | bytes 262176 | tf_op jit(solution)/shard_map/ppermute | solution.py:204
  65.7 4.8 %all-to-all-start.2 = ((bf16[4,3,128,256]{3,2,1,0:T(8,128)(2,1)}), bf16[4,3,128,256]{3,2,1,0:T(8,128)(2,1)S(1)}, u32[]{:S(2)}, u32[]{:S(2)}) async-start(bf16[4,3,128,256]{3,2,1,0:T(8,128)(2,1)} %shard_map.65), calls=%async_computation.2 | async-start | bytes 1572864 | tf_op jit(solution)/shard_map/all_to_all | solution.py:307
  71.0 7.6 %all-to-all-done.2 = bf16[4,3,128,256]{3,2,1,0:T(8,128)(2,1)S(1)} async-done(((bf16[4,3,128,256]{3,2,1,0:T(8,128)(2,1)}), bf16[4,3,128,256]{3,2,1,0:T(8,128)(2,1)S(1)}, u32[]{:S(2)}, u32[]{:S(2)}) %all-to-all-start.2) | async-done | bytes 786464 | tf_op jit(solution)/shard_map/all_to_all | solution.py:307
  78.8 9.5 %attention.1.partial_ref = bf16[512,4096]{1,0:T(8,128)(2,1)S(1)} custom-call(s32[64]{0:T(128)S(1)} %reshape.82.slot, s32[64]{0:T(128)S(1)} %reshape.83.base, s32[512,128]{1,0:T(8,128)S(1)} %broadcast_in_dim.100.start_ref, s32[512,128]{1,0:T(8,128)S(1)} %broadcast_in_dim.104.end_ref, bf16[512,512]{1,0:T(8,128)(2,1)S(1)} %copy-done, bf16[512,4096]{1,0:T(8,128)(2,1)} %w_hbm.1, ...), custom_call_target="tpu_custom_call" | custom-call | flops 4294967296 | bytes 4194304 | tf_op jit(solution)/shard_map/attention/pallas_call | solution.py:125
  88.3 4.3 %collective-permute-start.7 = (bf16[256,512]{1,0:T(8,128)(2,1)S(1)}, bf16[256,512]{1,0:T(8,128)(2,1)S(1)}, u32[]{:S(2)}, u32[]{:S(2)}) collective-permute-start(bf16[256,512]{1,0:T(8,128)(2,1)S(1)} %shard_map.66), channel_id=1, source_target_pairs={{0,2},{2,4},{4,6},{6,8},{8,10},{10,12},{12,14},{14,0},{1,3},{3,5},... | collective-permute-start | bytes 786440 | tf_op jit(solution)/shard_map/ppermute | solution.py:204
  92.6 8.6 %collective-permute-start.17 = (bf16[256,512]{1,0:T(8,128)(2,1)S(1)}, bf16[256,512]{1,0:T(8,128)(2,1)S(1)}, u32[]{:S(2)}, u32[]{:S(2)}) collective-permute-start(bf16[256,512]{1,0:T(8,128)(2,1)S(1)} %shard_map.76), channel_id=1, source_target_pairs={{0,14},{2,0},{4,2},{6,4},{8,6},{10,8},{12,10},{14,12},{1,15},{3,1}... | collective-permute-start | bytes 786440 | tf_op jit(solution)/shard_map/ppermute | solution.py:204
  101.2 3.9 %collective-permute-start.11 = (bf16[256,512]{1,0:T(8,128)(2,1)S(1)}, bf16[256,512]{1,0:T(8,128)(2,1)S(1)}, u32[]{:S(2)}, u32[]{:S(2)}) collective-permute-start(bf16[256,512]{1,0:T(8,128)(2,1)S(1)} %shard_map.70), channel_id=1, source_target_pairs={{0,14},{2,0},{4,2},{6,4},{8,6},{10,8},{12,10},{14,12},{1,15},{3,1}... | collective-permute-start | bytes 786440 | tf_op jit(solution)/shard_map/ppermute | solution.py:204
  105.2 1.9 %collective-permute-start.14 = (bf16[256,512]{1,0:T(8,128)(2,1)S(1)}, bf16[256,512]{1,0:T(8,128)(2,1)S(1)}, u32[]{:S(2)}, u32[]{:S(2)}) collective-permute-start(bf16[256,512]{1,0:T(8,128)(2,1)S(1)} %shard_map.73), channel_id=1, source_target_pairs={{0,2},{2,4},{4,6},{6,8},{8,10},{10,12},{12,14},{14,0},{1,3},{3,5},... | collective-permute-start | bytes 786440 | tf_op jit(solution)/shard_map/ppermute | solution.py:204
  107.2 1.9 %collective-permute-start.8 = (bf16[256,512]{1,0:T(8,128)(2,1)S(1)}, bf16[256,512]{1,0:T(8,128)(2,1)S(1)}, u32[]{:S(2)}, u32[]{:S(2)}) collective-permute-start(bf16[256,512]{1,0:T(8,128)(2,1)S(1)} %shard_map.67), channel_id=1, source_target_pairs={{0,2},{2,4},{4,6},{6,8},{8,10},{10,12},{12,14},{14,0},{1,3},{3,5},... | collective-permute-start | bytes 786440 | tf_op jit(solution)/shard_map/ppermute | solution.py:204
  109.2 5.1 %collective-permute-start.18 = (bf16[256,512]{1,0:T(8,128)(2,1)S(1)}, bf16[256,512]{1,0:T(8,128)(2,1)S(1)}, u32[]{:S(2)}, u32[]{:S(2)}) collective-permute-start(bf16[256,512]{1,0:T(8,128)(2,1)S(1)} %shard_map.77), channel_id=1, source_target_pairs={{0,14},{2,0},{4,2},{6,4},{8,6},{10,8},{12,10},{14,12},{1,15},{3,1}... | collective-permute-start | bytes 786440 | tf_op jit(solution)/shard_map/ppermute | solution.py:204
  114.5 3.9 %collective-permute-start.12 = (bf16[256,512]{1,0:T(8,128)(2,1)S(1)}, bf16[256,512]{1,0:T(8,128)(2,1)S(1)}, u32[]{:S(2)}, u32[]{:S(2)}) collective-permute-start(bf16[256,512]{1,0:T(8,128)(2,1)S(1)} %shard_map.71), channel_id=1, source_target_pairs={{0,14},{2,0},{4,2},{6,4},{8,6},{10,8},{12,10},{14,12},{1,15},{3,1}... | collective-permute-start | bytes 786440 | tf_op jit(solution)/shard_map/ppermute | solution.py:204
  118.5 1.9 %collective-permute-start.15 = (bf16[256,512]{1,0:T(8,128)(2,1)S(1)}, bf16[256,512]{1,0:T(8,128)(2,1)S(1)}, u32[]{:S(2)}, u32[]{:S(2)}) collective-permute-start(bf16[256,512]{1,0:T(8,128)(2,1)S(1)} %shard_map.74), channel_id=1, source_target_pairs={{0,2},{2,4},{4,6},{6,8},{8,10},{10,12},{12,14},{14,0},{1,3},{3,5},... | collective-permute-start | bytes 786440 | tf_op jit(solution)/shard_map/ppermute | solution.py:204
  120.5 1.9 %collective-permute-start.9 = (bf16[256,512]{1,0:T(8,128)(2,1)S(1)}, bf16[256,512]{1,0:T(8,128)(2,1)S(1)}, u32[]{:S(2)}, u32[]{:S(2)}) collective-permute-start(bf16[256,512]{1,0:T(8,128)(2,1)S(1)} %shard_map.68), channel_id=1, source_target_pairs={{0,2},{2,4},{4,6},{6,8},{8,10},{10,12},{12,14},{14,0},{1,3},{3,5},... | collective-permute-start | bytes 786440 | tf_op jit(solution)/shard_map/ppermute | solution.py:204
  122.5 5.1 %collective-permute-start.19 = (bf16[256,512]{1,0:T(8,128)(2,1)S(1)}, bf16[256,512]{1,0:T(8,128)(2,1)S(1)}, u32[]{:S(2)}, u32[]{:S(2)}) collective-permute-start(bf16[256,512]{1,0:T(8,128)(2,1)S(1)} %shard_map.78), channel_id=1, source_target_pairs={{0,14},{2,0},{4,2},{6,4},{8,6},{10,8},{12,10},{14,12},{1,15},{3,1}... | collective-permute-start | bytes 786440 | tf_op jit(solution)/shard_map/ppermute | solution.py:204
  127.7 3.9 %collective-permute-start.13 = (bf16[256,512]{1,0:T(8,128)(2,1)S(1)}, bf16[256,512]{1,0:T(8,128)(2,1)S(1)}, u32[]{:S(2)}, u32[]{:S(2)}) collective-permute-start(bf16[256,512]{1,0:T(8,128)(2,1)S(1)} %shard_map.72), channel_id=1, source_target_pairs={{0,14},{2,0},{4,2},{6,4},{8,6},{10,8},{12,10},{14,12},{1,15},{3,1}... | collective-permute-start | bytes 786440 | tf_op jit(solution)/shard_map/ppermute | solution.py:204
  131.7 1.9 %collective-permute-start.16 = (bf16[256,512]{1,0:T(8,128)(2,1)S(1)}, bf16[256,512]{1,0:T(8,128)(2,1)S(1)}, u32[]{:S(2)}, u32[]{:S(2)}) collective-permute-start(bf16[256,512]{1,0:T(8,128)(2,1)S(1)} %shard_map.75), channel_id=1, source_target_pairs={{0,2},{2,4},{4,6},{6,8},{8,10},{10,12},{12,14},{14,0},{1,3},{3,5},... | collective-permute-start | bytes 786440 | tf_op jit(solution)/shard_map/ppermute | solution.py:204
  134.3 1.9 %collective-permute-start.10 = (bf16[256,512]{1,0:T(8,128)(2,1)S(1)}, bf16[256,512]{1,0:T(8,128)(2,1)S(1)}, u32[]{:S(2)}, u32[]{:S(2)}) collective-permute-start(bf16[256,512]{1,0:T(8,128)(2,1)S(1)} %shard_map.69), channel_id=1, source_target_pairs={{0,2},{2,4},{4,6},{6,8},{8,10},{10,12},{12,14},{14,0},{1,3},{3,5},... | collective-permute-start | bytes 786440 | tf_op jit(solution)/shard_map/ppermute | solution.py:204
  136.3 5.1 %collective-permute-start.20 = (bf16[256,512]{1,0:T(8,128)(2,1)S(1)}, bf16[256,512]{1,0:T(8,128)(2,1)S(1)}, u32[]{:S(2)}, u32[]{:S(2)}) collective-permute-start(bf16[256,512]{1,0:T(8,128)(2,1)S(1)} %shard_map.79), channel_id=1, source_target_pairs={{0,14},{2,0},{4,2},{6,4},{8,6},{10,8},{12,10},{14,12},{1,15},{3,1}... | collective-permute-start | bytes 786440 | tf_op jit(solution)/shard_map/ppermute | solution.py:204
  141.5 2.6 %collective-permute-done.10.refs_0_ = bf16[256,512]{1,0:T(8,128)(2,1)S(1)} collective-permute-done((bf16[256,512]{1,0:T(8,128)(2,1)S(1)}, bf16[256,512]{1,0:T(8,128)(2,1)S(1)}, u32[]{:S(2)}, u32[]{:S(2)}) %collective-permute-start.10) | collective-permute-done | bytes 262176 | tf_op jit(solution)/shard_map/ppermute | solution.py:204
  (65 shorter events, 9.7 us)
Async XLA Ops:
  1.0 10.9 %collective-permute-start.2 = (bf16[4,128,256]{2,1,0:T(8,128)(2,1)S(1)}, bf16[4,128,256]{2,1,0:T(8,128)(2,1)S(1)}, u32[]{:S(2)}, u32[]{:S(2)}) collective-permute-start(bf16[4,128,256]{2,1,0:T(8,128)(2,1)S(1)} %bitcast.7), channel_id=1, source_target_pairs={{0,448},{64,0},{128,64},{192,128},{256,192},{320,256},{384,320},{4... | collective-permute-start | bytes 786440 | tf_op jit(solution)/shard_map/ppermute | solution.py:204
  6.4 11.1 %collective-permute-start = (bf16[4,128,256]{2,1,0:T(8,128)(2,1)S(1)}, bf16[4,128,256]{2,1,0:T(8,128)(2,1)S(1)}, u32[]{:S(2)}, u32[]{:S(2)}) collective-permute-start(bf16[4,128,256]{2,1,0:T(8,128)(2,1)S(1)} %bitcast.8), channel_id=1, source_target_pairs={{0,64},{64,128},{128,192},{192,256},{256,320},{320,384},{384,448},... | collective-permute-start | bytes 786440 | tf_op jit(solution)/shard_map/ppermute | solution.py:204
  11.9 25.6 %collective-permute-start.3 = (bf16[4,128,256]{2,1,0:T(8,128)(2,1)S(1)}, bf16[4,128,256]{2,1,0:T(8,128)(2,1)S(1)}, u32[]{:S(2)}, u32[]{:S(2)}) collective-permute-start(bf16[4,128,256]{2,1,0:T(8,128)(2,1)S(1)} %collective-permute-done.2.refs_4_), channel_id=1, source_target_pairs={{0,448},{64,0},{128,64},{192,128},{256,192},{320,256},{384,320},{4... | collective-permute-start | bytes 786440 | tf_op jit(solution)/shard_map/ppermute | solution.py:204
  17.5 20.0 %collective-permute-start.1 = (bf16[4,128,256]{2,1,0:T(8,128)(2,1)S(1)}, bf16[4,128,256]{2,1,0:T(8,128)(2,1)S(1)}, u32[]{:S(2)}, u32[]{:S(2)}) collective-permute-start(bf16[4,128,256]{2,1,0:T(8,128)(2,1)S(1)} %collective-permute-done.refs_1_), channel_id=1, source_target_pairs={{0,64},{64,128},{128,192},{192,256},{256,320},{320,384},{384,448},... | collective-permute-start | bytes 786440 | tf_op jit(solution)/shard_map/ppermute | solution.py:204
  20.8 16.6 %all-to-all-start = ((s32[32,5,16]{2,1,0:T(8,128)}), s32[32,5,16]{2,1,0:T(8,128)S(1)}, u32[]{:S(2)}, u32[]{:S(2)}) async-start(s32[32,5,16]{2,1,0:T(8,128)} %broadcast_in_dim.97), calls=%async_computation | async-start | bytes 262144 | tf_op jit(solution)/shard_map/all_to_all | solution.py:283
  38.1 32.4 %copy-start.1 = (s32[4,16]{1,0:T(4,128)S(1)}, s32[4,16]{1,0:T(4,128)}, u32[]{:S(2)}) copy-start(s32[4,16]{1,0:T(4,128)} %param.10) | copy-start | bytes 772
  38.1 32.7 %copy-start.2 = (s32[512]{0:T(512)S(1)}, s32[512]{0:T(512)}, u32[]{:S(2)}) copy-start(s32[512]{0:T(512)} %param.9) | copy-start | bytes 6148
  38.1 40.7 %copy-start = (bf16[512,512]{1,0:T(8,128)(2,1)S(1)}, bf16[512,512]{1,0:T(8,128)(2,1)}, u32[]{:S(2)}) copy-start(bf16[512,512]{1,0:T(8,128)(2,1)} %q_hbm.1) | copy-start | bytes 1572868
  39.8 25.9 %all-to-all-start.1 = ((bf16[4,5,128,256]{3,2,1,0:T(8,128)(2,1)}), bf16[4,5,128,256]{3,2,1,0:T(8,128)(2,1)S(1)}, u32[]{:S(2)}, u32[]{:S(2)}) async-start(bf16[4,5,128,256]{3,2,1,0:T(8,128)(2,1)} %shard_map.64), calls=%async_computation.1 | async-start | bytes 2621440 | tf_op jit(solution)/shard_map/all_to_all | solution.py:307
  45.2 9.5 %collective-permute-start.4 = (bf16[4,128,256]{2,1,0:T(8,128)(2,1)S(1)}, bf16[4,128,256]{2,1,0:T(8,128)(2,1)S(1)}, u32[]{:S(2)}, u32[]{:S(2)}) collective-permute-start(bf16[4,128,256]{2,1,0:T(8,128)(2,1)S(1)} %collective-permute-done.1.refs_0_.refs_2_), channel_id=1, source_target_pairs={{0,64},{64,128},{128,192},{192,256},{256,320},{320,384},{384,448},... | collective-permute-start | bytes 786440 | tf_op jit(solution)/shard_map/ppermute | solution.py:204
  48.0 8.8 %collective-permute-start.6 = (bf16[4,128,256]{2,1,0:T(8,128)(2,1)S(1)}, bf16[4,128,256]{2,1,0:T(8,128)(2,1)S(1)}, u32[]{:S(2)}, u32[]{:S(2)}) collective-permute-start(bf16[4,128,256]{2,1,0:T(8,128)(2,1)S(1)} %collective-permute-done.3.refs_1_.refs_3_), channel_id=1, source_target_pairs={{0,448},{64,0},{128,64},{192,128},{256,192},{320,256},{384,320},{4... | collective-permute-start | bytes 786440 | tf_op jit(solution)/shard_map/ppermute | solution.py:204
  54.7 9.5 %collective-permute-start.5 = (bf16[4,128,256]{2,1,0:T(8,128)(2,1)S(1)}, bf16[4,128,256]{2,1,0:T(8,128)(2,1)S(1)}, u32[]{:S(2)}, u32[]{:S(2)}) collective-permute-start(bf16[4,128,256]{2,1,0:T(8,128)(2,1)S(1)} %collective-permute-done.4.refs_0_), channel_id=1, source_target_pairs={{0,64},{64,128},{128,192},{192,256},{256,320},{320,384},{384,448},... | collective-permute-start | bytes 786440 | tf_op jit(solution)/shard_map/ppermute | solution.py:204
  65.7 12.8 %all-to-all-start.2 = ((bf16[4,3,128,256]{3,2,1,0:T(8,128)(2,1)}), bf16[4,3,128,256]{3,2,1,0:T(8,128)(2,1)S(1)}, u32[]{:S(2)}, u32[]{:S(2)}) async-start(bf16[4,3,128,256]{3,2,1,0:T(8,128)(2,1)} %shard_map.65), calls=%async_computation.2 | async-start | bytes 1572864 | tf_op jit(solution)/shard_map/all_to_all | solution.py:307
  88.3 18.8 %collective-permute-start.7 = (bf16[256,512]{1,0:T(8,128)(2,1)S(1)}, bf16[256,512]{1,0:T(8,128)(2,1)S(1)}, u32[]{:S(2)}, u32[]{:S(2)}) collective-permute-start(bf16[256,512]{1,0:T(8,128)(2,1)S(1)} %shard_map.66), channel_id=1, source_target_pairs={{0,2},{2,4},{4,6},{6,8},{8,10},{10,12},{12,14},{14,0},{1,3},{3,5},... | collective-permute-start | bytes 786440 | tf_op jit(solution)/shard_map/ppermute | solution.py:204
  92.6 16.5 %collective-permute-start.17 = (bf16[256,512]{1,0:T(8,128)(2,1)S(1)}, bf16[256,512]{1,0:T(8,128)(2,1)S(1)}, u32[]{:S(2)}, u32[]{:S(2)}) collective-permute-start(bf16[256,512]{1,0:T(8,128)(2,1)S(1)} %shard_map.76), channel_id=1, source_target_pairs={{0,14},{2,0},{4,2},{6,4},{8,6},{10,8},{12,10},{14,12},{1,15},{3,1}... | collective-permute-start | bytes 786440 | tf_op jit(solution)/shard_map/ppermute | solution.py:204
  101.2 13.1 %collective-permute-start.11 = (bf16[256,512]{1,0:T(8,128)(2,1)S(1)}, bf16[256,512]{1,0:T(8,128)(2,1)S(1)}, u32[]{:S(2)}, u32[]{:S(2)}) collective-permute-start(bf16[256,512]{1,0:T(8,128)(2,1)S(1)} %shard_map.70), channel_id=1, source_target_pairs={{0,14},{2,0},{4,2},{6,4},{8,6},{10,8},{12,10},{14,12},{1,15},{3,1}... | collective-permute-start | bytes 786440 | tf_op jit(solution)/shard_map/ppermute | solution.py:204
  105.2 13.2 %collective-permute-start.14 = (bf16[256,512]{1,0:T(8,128)(2,1)S(1)}, bf16[256,512]{1,0:T(8,128)(2,1)S(1)}, u32[]{:S(2)}, u32[]{:S(2)}) collective-permute-start(bf16[256,512]{1,0:T(8,128)(2,1)S(1)} %shard_map.73), channel_id=1, source_target_pairs={{0,2},{2,4},{4,6},{6,8},{8,10},{10,12},{12,14},{14,0},{1,3},{3,5},... | collective-permute-start | bytes 786440 | tf_op jit(solution)/shard_map/ppermute | solution.py:204
  107.2 13.2 %collective-permute-start.8 = (bf16[256,512]{1,0:T(8,128)(2,1)S(1)}, bf16[256,512]{1,0:T(8,128)(2,1)S(1)}, u32[]{:S(2)}, u32[]{:S(2)}) collective-permute-start(bf16[256,512]{1,0:T(8,128)(2,1)S(1)} %shard_map.67), channel_id=1, source_target_pairs={{0,2},{2,4},{4,6},{6,8},{8,10},{10,12},{12,14},{14,0},{1,3},{3,5},... | collective-permute-start | bytes 786440 | tf_op jit(solution)/shard_map/ppermute | solution.py:204
  109.2 13.2 %collective-permute-start.18 = (bf16[256,512]{1,0:T(8,128)(2,1)S(1)}, bf16[256,512]{1,0:T(8,128)(2,1)S(1)}, u32[]{:S(2)}, u32[]{:S(2)}) collective-permute-start(bf16[256,512]{1,0:T(8,128)(2,1)S(1)} %shard_map.77), channel_id=1, source_target_pairs={{0,14},{2,0},{4,2},{6,4},{8,6},{10,8},{12,10},{14,12},{1,15},{3,1}... | collective-permute-start | bytes 786440 | tf_op jit(solution)/shard_map/ppermute | solution.py:204
  114.5 13.2 %collective-permute-start.12 = (bf16[256,512]{1,0:T(8,128)(2,1)S(1)}, bf16[256,512]{1,0:T(8,128)(2,1)S(1)}, u32[]{:S(2)}, u32[]{:S(2)}) collective-permute-start(bf16[256,512]{1,0:T(8,128)(2,1)S(1)} %shard_map.71), channel_id=1, source_target_pairs={{0,14},{2,0},{4,2},{6,4},{8,6},{10,8},{12,10},{14,12},{1,15},{3,1}... | collective-permute-start | bytes 786440 | tf_op jit(solution)/shard_map/ppermute | solution.py:204
  118.5 13.2 %collective-permute-start.15 = (bf16[256,512]{1,0:T(8,128)(2,1)S(1)}, bf16[256,512]{1,0:T(8,128)(2,1)S(1)}, u32[]{:S(2)}, u32[]{:S(2)}) collective-permute-start(bf16[256,512]{1,0:T(8,128)(2,1)S(1)} %shard_map.74), channel_id=1, source_target_pairs={{0,2},{2,4},{4,6},{6,8},{8,10},{10,12},{12,14},{14,0},{1,3},{3,5},... | collective-permute-start | bytes 786440 | tf_op jit(solution)/shard_map/ppermute | solution.py:204
  120.5 13.7 %collective-permute-start.9 = (bf16[256,512]{1,0:T(8,128)(2,1)S(1)}, bf16[256,512]{1,0:T(8,128)(2,1)S(1)}, u32[]{:S(2)}, u32[]{:S(2)}) collective-permute-start(bf16[256,512]{1,0:T(8,128)(2,1)S(1)} %shard_map.68), channel_id=1, source_target_pairs={{0,2},{2,4},{4,6},{6,8},{8,10},{10,12},{12,14},{14,0},{1,3},{3,5},... | collective-permute-start | bytes 786440 | tf_op jit(solution)/shard_map/ppermute | solution.py:204
  122.5 13.7 %collective-permute-start.19 = (bf16[256,512]{1,0:T(8,128)(2,1)S(1)}, bf16[256,512]{1,0:T(8,128)(2,1)S(1)}, u32[]{:S(2)}, u32[]{:S(2)}) collective-permute-start(bf16[256,512]{1,0:T(8,128)(2,1)S(1)} %shard_map.78), channel_id=1, source_target_pairs={{0,14},{2,0},{4,2},{6,4},{8,6},{10,8},{12,10},{14,12},{1,15},{3,1}... | collective-permute-start | bytes 786440 | tf_op jit(solution)/shard_map/ppermute | solution.py:204
  127.7 13.7 %collective-permute-start.13 = (bf16[256,512]{1,0:T(8,128)(2,1)S(1)}, bf16[256,512]{1,0:T(8,128)(2,1)S(1)}, u32[]{:S(2)}, u32[]{:S(2)}) collective-permute-start(bf16[256,512]{1,0:T(8,128)(2,1)S(1)} %shard_map.72), channel_id=1, source_target_pairs={{0,14},{2,0},{4,2},{6,4},{8,6},{10,8},{12,10},{14,12},{1,15},{3,1}... | collective-permute-start | bytes 786440 | tf_op jit(solution)/shard_map/ppermute | solution.py:204
  131.7 9.7 %collective-permute-start.16 = (bf16[256,512]{1,0:T(8,128)(2,1)S(1)}, bf16[256,512]{1,0:T(8,128)(2,1)S(1)}, u32[]{:S(2)}, u32[]{:S(2)}) collective-permute-start(bf16[256,512]{1,0:T(8,128)(2,1)S(1)} %shard_map.75), channel_id=1, source_target_pairs={{0,2},{2,4},{4,6},{6,8},{8,10},{10,12},{12,14},{14,0},{1,3},{3,5},... | collective-permute-start | bytes 786440 | tf_op jit(solution)/shard_map/ppermute | solution.py:204
  134.3 9.7 %collective-permute-start.10 = (bf16[256,512]{1,0:T(8,128)(2,1)S(1)}, bf16[256,512]{1,0:T(8,128)(2,1)S(1)}, u32[]{:S(2)}, u32[]{:S(2)}) collective-permute-start(bf16[256,512]{1,0:T(8,128)(2,1)S(1)} %shard_map.69), channel_id=1, source_target_pairs={{0,2},{2,4},{4,6},{6,8},{8,10},{10,12},{12,14},{14,0},{1,3},{3,5},... | collective-permute-start | bytes 786440 | tf_op jit(solution)/shard_map/ppermute | solution.py:204
  136.3 9.0 %collective-permute-start.20 = (bf16[256,512]{1,0:T(8,128)(2,1)S(1)}, bf16[256,512]{1,0:T(8,128)(2,1)S(1)}, u32[]{:S(2)}, u32[]{:S(2)}) collective-permute-start(bf16[256,512]{1,0:T(8,128)(2,1)S(1)} %shard_map.79), channel_id=1, source_target_pairs={{0,14},{2,0},{4,2},{6,4},{8,6},{10,8},{12,10},{14,12},{1,15},{3,1}... | collective-permute-start | bytes 786440 | tf_op jit(solution)/shard_map/ppermute | solution.py:204

commit v2 on v1

--- a/solution.py
+++ b/solution.py
@@ -157,20 +157,49 @@
 
 
 def pick_kernel(piece_count, index, *refs):
-    pieces, out_ref = refs[:piece_count], refs[piece_count]
+    pieces, out_ref, sems = refs[:piece_count], refs[piece_count], refs[piece_count + 1]
+    copies = [
+        pltpu.make_async_copy(
+            piece.at[index[r * piece_count + d]],
+            out_ref.at[r, d],
+            sems.at[r * piece_count + d],
+        )
+        for r in range(out_ref.shape[0])
+        for d, piece in enumerate(pieces)
+    ]
+    for copy in copies:
+        copy.start()
+    for copy in copies:
+        copy.wait()
+
+
+def info_kernel(tok_rows, me, docs_ref, lists_ref, out_ref):
+    docs = docs_ref[...]
+    shape = docs.shape
+    positions = (
+        me[0] * tok_rows
+        + lax.broadcasted_iota(jnp.int32, shape, 0) * shape[1]
+        + lax.broadcasted_iota(jnp.int32, shape, 1)
+    )
+    lane = lax.broadcasted_iota(jnp.int32, (1, TOPK), 1)
+    firsts = jnp.full((1, TOPK), far_position, jnp.int32)
+    for d in range(DOCS):
+        first = jnp.min(jnp.where(docs == d, positions, far_position))
+        firsts = jnp.where(lane == d, first, firsts)
+    rows = lists_ref.shape[0]
     for r in range(out_ref.shape[0]):
-        for d, piece in enumerate(pieces):
-            out_ref[r, d] = piece[index[r * piece_count + d]]
-
-
-def small_kernel(body, out_shape, scalars, *operands):
+        out_ref[r, :rows, :] = lists_ref[...]
+        out_ref[r, rows:, :] = firsts
+
+
+def small_kernel(body, out_shape, scalars, *operands, mib=8):
     return pl.pallas_call(
         body,
         out_shape=out_shape,
         in_specs=[pl.BlockSpec(memory_space=pltpu.SMEM)]
         + [pl.BlockSpec(memory_space=pltpu.VMEM)] * len(operands),
         out_specs=jax.tree.map(lambda _: pl.BlockSpec(memory_space=pltpu.VMEM), out_shape),
-        compiler_params=pltpu.CompilerParams(vmem_limit_bytes=8 * 1024 * 1024),
+        compiler_params=pltpu.CompilerParams(vmem_limit_bytes=mib and mib * 1024 * 1024),
         cost_estimate=pl.CostEstimate(
             flops=1024 * 1024, bytes_accessed=1024 * 1024, transcendentals=0
         ),
@@ -178,9 +207,19 @@
 
 
 def pick(pieces, index):
-    out = jax.ShapeDtypeStruct((*index.shape, *pieces[0].shape[1:]), pieces[0].dtype)
-    body = functools.partial(pick_kernel, len(pieces))
-    return small_kernel(body, out, index.reshape(-1), *pieces)
+    return pl.pallas_call(
+        functools.partial(pick_kernel, len(pieces)),
+        out_shape=jax.ShapeDtypeStruct((*index.shape, *pieces[0].shape[1:]), pieces[0].dtype),
+        in_specs=[pl.BlockSpec(memory_space=pltpu.SMEM)]
+        + [pl.BlockSpec(memory_space=pl.ANY)] * len(pieces),
+        out_specs=pl.BlockSpec(memory_space=pl.ANY),
+        scratch_shapes=[pltpu.SemaphoreType.DMA((index.size,))],
+        compiler_params=pltpu.CompilerParams(vmem_limit_bytes=1024 * 1024),
+        cost_estimate=pl.CostEstimate(
+            flops=1024 * 1024, bytes_accessed=1024 * 1024, transcendentals=0
+        ),
+        name="pick",
+    )(index.reshape(-1), *pieces)
 
 
 def hold_kernel(source_ref, *refs):
@@ -272,14 +311,15 @@
     )
     column = ring_gather(own_blocks, "y")
 
-    positions = own_index * tok_rows + jnp.arange(tok_rows, dtype=jnp.int32)
     doc_range = jnp.arange(DOCS, dtype=jnp.int32)
-    first_local = jnp.min(
-        jnp.where(doc_ids[None, :] == doc_range[:, None], positions[None, :], far_position), axis=1
-    )
-    first_local = jnp.pad(first_local, (0, TOPK - DOCS), constant_values=far_position)
-    info = jnp.concatenate([block_lists, first_local[None]], axis=0)
-    info = jnp.broadcast_to(info[None], (seq_count, *info.shape))
+    info = small_kernel(
+        functools.partial(info_kernel, tok_rows),
+        jax.ShapeDtypeStruct((seq_count, blocks_dev + 1, TOPK), jnp.int32),
+        own_index.reshape(1).astype(jnp.int32),
+        doc_ids.reshape(blocks_dev, BLOCK_TOKENS),
+        block_lists,
+        mib=None,
+    )
     info = lax.all_to_all(info, ("y", "x"), 0, 0, tiled=True)
     quarter = y_count // 4
     info = hold(info, column[quarter], column[-quarter])

time: 147 us -> 148 us (level)
  Pallas kernels: 14.5 us -> 16.2 us
  other arithmetic: 3.14 us -> 1.64 us
    pallas_call x0 -> x2, Pallas kernels: none -> 3.37 us  [pick(): pl.pallas_call(functools.partial(pick_kernel, len(pieces)), out_shape=jax...]
    pallas_call x17 -> x16, Pallas kernels: 4.99 us -> 3.37 us  [small_kernel(): pl.pallas_call(body, out_shape=out_shape, in_specs=[pl.BlockSpec(memory_s...]
  transfers between devices with their start and end apart: 24 -> 24, of which waited for: 8 -> 8; matrix products, arithmetic and copies ran while one was open for 2% -> 0% of each run, Pallas kernels for 2% -> 3%
where the time goes in v2:
time: 148 us; the launch traced here: 147 us
  starting transfers between devices  93.3 us (63%)
  waiting for transfers between devices  34.3 us (23%)
  Pallas kernels  16.2 us (11%)
  other arithmetic  1.64 us (1%)
    ppermute x21, starting transfers between devices, shifted(): return lax.ppermute(x, axis, [(i, (i + shift) % size) for i in range(size)])  75.3 us
    ppermute x21, waiting for transfers between devices, shifted(): return lax.ppermute(x, axis, [(i, (i + shift) % size) for i in range(size)])  17.9 us
    all_to_all x2, starting transfers between devices, per_device(): arrived = lax.all_to_all(outgoing, 'x', 0, 0, tiled=True)  10.2 us
    pallas_call x1, Pallas kernels, attention(): pl.pallas_call(attention_kernel, out_shape=jax.ShapeDtypeStruct((tokens,...  9.45 us
    all_to_all x1, waiting for transfers between devices, per_device(): info = lax.all_to_all(info, ('y', 'x'), 0, 0, tiled=True)  8.84 us
    all_to_all x1, starting transfers between devices, per_device(): info = lax.all_to_all(info, ('y', 'x'), 0, 0, tiled=True)  7.78 us
    all_to_all x2, waiting for transfers between devices, per_device(): arrived = lax.all_to_all(outgoing, 'x', 0, 0, tiled=True)  7.56 us
    pallas_call x16, Pallas kernels, small_kernel(): pl.pallas_call(body, out_shape=out_shape, in_specs=[pl.BlockSpec(memory_s...  3.37 us
  transfers between devices with their start and end apart: 24, of which 8 were waited for; matrix products, arithmetic and copies ran while one was open for 0% of the time, Pallas kernels for 3%

profile of v2, /device:TPU:2, one launch (start us, length us, event | category | flops | bytes accessed | tf_op | source)
XLA Modules:
  0.0 146.7 jit_solution(7676049767111058076)
XLA Ops:
  1.0 5.4 %collective-permute-start.2 = (bf16[4,128,256]{2,1,0:T(8,128)(2,1)S(1)}, bf16[4,128,256]{2,1,0:T(8,128)(2,1)S(1)}, u32[]{:S(2)}, u32[]{:S(2)}) collective-permute-start(bf16[4,128,256]{2,1,0:T(8,128)(2,1)S(1)} %bitcast.7), channel_id=1, source_target_pairs={{0,448},{64,0},{128,64},{192,128},{256,192},{320,256},{384,320},{4... | collective-permute-start | bytes 786440 | tf_op jit(solution)/shard_map/ppermute | solution.py:243
  6.4 1.9 %collective-permute-start = (bf16[4,128,256]{2,1,0:T(8,128)(2,1)S(1)}, bf16[4,128,256]{2,1,0:T(8,128)(2,1)S(1)}, u32[]{:S(2)}, u32[]{:S(2)}) collective-permute-start(bf16[4,128,256]{2,1,0:T(8,128)(2,1)S(1)} %bitcast.8), channel_id=1, source_target_pairs={{0,64},{64,128},{128,192},{192,256},{256,320},{320,384},{384,448},... | collective-permute-start | bytes 786440 | tf_op jit(solution)/shard_map/ppermute | solution.py:243
  8.3 3.6 %collective-permute-done.2.refs_4_ = bf16[4,128,256]{2,1,0:T(8,128)(2,1)S(1)} collective-permute-done((bf16[4,128,256]{2,1,0:T(8,128)(2,1)S(1)}, bf16[4,128,256]{2,1,0:T(8,128)(2,1)S(1)}, u32[]{:S(2)}, u32[]{:S(2)}) %collective-permute-start.2) | collective-permute-done | bytes 262176 | tf_op jit(solution)/shard_map/ppermute | solution.py:243
  11.9 5.6 %collective-permute-start.3 = (bf16[4,128,256]{2,1,0:T(8,128)(2,1)S(1)}, bf16[4,128,256]{2,1,0:T(8,128)(2,1)S(1)}, u32[]{:S(2)}, u32[]{:S(2)}) collective-permute-start(bf16[4,128,256]{2,1,0:T(8,128)(2,1)S(1)} %collective-permute-done.2.refs_4_), channel_id=1, source_target_pairs={{0,448},{64,0},{128,64},{192,128},{256,192},{320,256},{384,320},{4... | collective-permute-start | bytes 786440 | tf_op jit(solution)/shard_map/ppermute | solution.py:243
  17.5 1.9 %collective-permute-start.1 = (bf16[4,128,256]{2,1,0:T(8,128)(2,1)S(1)}, bf16[4,128,256]{2,1,0:T(8,128)(2,1)S(1)}, u32[]{:S(2)}, u32[]{:S(2)}) collective-permute-start(bf16[4,128,256]{2,1,0:T(8,128)(2,1)S(1)} %collective-permute-done.refs_1_), channel_id=1, source_target_pairs={{0,64},{64,128},{128,192},{192,256},{256,320},{320,384},{384,448},... | collective-permute-start | bytes 786440 | tf_op jit(solution)/shard_map/ppermute | solution.py:243
  21.0 7.8 %all-to-all-start = ((s32[32,5,16]{2,1,0:T(8,128)}), s32[32,5,16]{2,1,0:T(8,128)S(1)}, u32[]{:S(2)}, u32[]{:S(2)}) async-start(s32[32,5,16]{2,1,0:T(8,128)} %shard_map.64), calls=%async_computation | async-start | bytes 262144 | tf_op jit(solution)/shard_map/all_to_all | solution.py:323
  28.9 8.8 %all-to-all-done.source_ref = s32[32,5,16]{2,1,0:T(8,128)S(1)} async-done(((s32[32,5,16]{2,1,0:T(8,128)}), s32[32,5,16]{2,1,0:T(8,128)S(1)}, u32[]{:S(2)}, u32[]{:S(2)}) %all-to-all-start) | async-done | bytes 10272 | tf_op jit(solution)/shard_map/all_to_all | solution.py:323
  38.3 1.8 %pick.2 = bf16[4,5,128,256]{3,2,1,0:T(8,128)(2,1)} custom-call(s32[20]{0:T(128)S(1)} %reshape.87.index, bf16[4,128,256]{2,1,0:T(8,128)(2,1)S(1)} %bitcast.9, bf16[4,128,256]{2,1,0:T(8,128)(2,1)S(1)} %collective-permute-done.refs_1_, bf16[4,128,256]{2,1,0:T(8,128)(2,1)S(1)} %collective-permute-done.1.refs_0_.refs_2_, ...), custom_call_target="tpu_custom_call" | custom-call | flops 1048576 | bytes 1048576 | tf_op jit(solution)/shard_map/pick/pallas_call | solution.py:210
  40.2 5.4 %all-to-all-start.1 = ((bf16[4,5,128,256]{3,2,1,0:T(8,128)(2,1)}), bf16[4,5,128,256]{3,2,1,0:T(8,128)(2,1)S(1)}, u32[]{:S(2)}, u32[]{:S(2)}) async-start(bf16[4,5,128,256]{3,2,1,0:T(8,128)(2,1)} %pick.2), calls=%async_computation.1 | async-start | bytes 2621440 | tf_op jit(solution)/shard_map/all_to_all | solution.py:347
  45.6 2.7 %collective-permute-start.4 = (bf16[4,128,256]{2,1,0:T(8,128)(2,1)S(1)}, bf16[4,128,256]{2,1,0:T(8,128)(2,1)S(1)}, u32[]{:S(2)}, u32[]{:S(2)}) collective-permute-start(bf16[4,128,256]{2,1,0:T(8,128)(2,1)S(1)} %collective-permute-done.1.refs_0_.refs_2_), channel_id=1, source_target_pairs={{0,64},{64,128},{128,192},{192,256},{256,320},{320,384},{384,448},... | collective-permute-start | bytes 786440 | tf_op jit(solution)/shard_map/ppermute | solution.py:243
  48.3 4.3 %collective-permute-start.6 = (bf16[4,128,256]{2,1,0:T(8,128)(2,1)S(1)}, bf16[4,128,256]{2,1,0:T(8,128)(2,1)S(1)}, u32[]{:S(2)}, u32[]{:S(2)}) collective-permute-start(bf16[4,128,256]{2,1,0:T(8,128)(2,1)S(1)} %collective-permute-done.3.refs_1_.refs_3_), channel_id=1, source_target_pairs={{0,448},{64,0},{128,64},{192,128},{256,192},{320,256},{384,320},{4... | collective-permute-start | bytes 786440 | tf_op jit(solution)/shard_map/ppermute | solution.py:243
  52.7 2.4 %collective-permute-done.4.refs_0_ = bf16[4,128,256]{2,1,0:T(8,128)(2,1)S(1)} collective-permute-done((bf16[4,128,256]{2,1,0:T(8,128)(2,1)S(1)}, bf16[4,128,256]{2,1,0:T(8,128)(2,1)S(1)}, u32[]{:S(2)}, u32[]{:S(2)}) %collective-permute-start.4) | collective-permute-done | bytes 262176 | tf_op jit(solution)/shard_map/ppermute | solution.py:243
  55.1 1.9 %collective-permute-start.5 = (bf16[4,128,256]{2,1,0:T(8,128)(2,1)S(1)}, bf16[4,128,256]{2,1,0:T(8,128)(2,1)S(1)}, u32[]{:S(2)}, u32[]{:S(2)}) collective-permute-start(bf16[4,128,256]{2,1,0:T(8,128)(2,1)S(1)} %collective-permute-done.4.refs_0_), channel_id=1, source_target_pairs={{0,64},{64,128},{128,192},{192,256},{256,320},{320,384},{384,448},... | collective-permute-start | bytes 786440 | tf_op jit(solution)/shard_map/ppermute | solution.py:243
  57.1 7.5 %collective-permute-done.5.refs_1_ = bf16[4,128,256]{2,1,0:T(8,128)(2,1)S(1)} collective-permute-done((bf16[4,128,256]{2,1,0:T(8,128)(2,1)S(1)}, bf16[4,128,256]{2,1,0:T(8,128)(2,1)S(1)}, u32[]{:S(2)}, u32[]{:S(2)}) %collective-permute-start.5) | collective-permute-done | bytes 262176 | tf_op jit(solution)/shard_map/ppermute | solution.py:243
  66.1 4.8 %all-to-all-start.2 = ((bf16[4,3,128,256]{3,2,1,0:T(8,128)(2,1)}), bf16[4,3,128,256]{3,2,1,0:T(8,128)(2,1)S(1)}, u32[]{:S(2)}, u32[]{:S(2)}) async-start(bf16[4,3,128,256]{3,2,1,0:T(8,128)(2,1)} %pick.3), calls=%async_computation.2 | async-start | bytes 1572864 | tf_op jit(solution)/shard_map/all_to_all | solution.py:347
  71.4 7.6 %all-to-all-done.2 = bf16[4,3,128,256]{3,2,1,0:T(8,128)(2,1)S(1)} async-done(((bf16[4,3,128,256]{3,2,1,0:T(8,128)(2,1)}), bf16[4,3,128,256]{3,2,1,0:T(8,128)(2,1)S(1)}, u32[]{:S(2)}, u32[]{:S(2)}) %all-to-all-start.2) | async-done | bytes 786464 | tf_op jit(solution)/shard_map/all_to_all | solution.py:347
  79.2 9.5 %attention.1.partial_ref = bf16[512,4096]{1,0:T(8,128)(2,1)S(1)} custom-call(s32[64]{0:T(128)S(1)} %reshape.82.slot, s32[64]{0:T(128)S(1)} %reshape.83.base, s32[512,128]{1,0:T(8,128)S(1)} %broadcast_in_dim.72.start_ref, s32[512,128]{1,0:T(8,128)S(1)} %broadcast_in_dim.76.end_ref, bf16[512,512]{1,0:T(8,128)(2,1)S(1)} %copy-done, bf16[512,4096]{1,0:T(8,128)(2,1)} %w_hbm.1, ...), custom_call_target="tpu_custom_call" | custom-call | flops 4294967296 | bytes 4194304 | tf_op jit(solution)/shard_map/attention/pallas_call | solution.py:125
  88.7 4.3 %collective-permute-start.7 = (bf16[256,512]{1,0:T(8,128)(2,1)S(1)}, bf16[256,512]{1,0:T(8,128)(2,1)S(1)}, u32[]{:S(2)}, u32[]{:S(2)}) collective-permute-start(bf16[256,512]{1,0:T(8,128)(2,1)S(1)} %shard_map.65), channel_id=1, source_target_pairs={{0,2},{2,4},{4,6},{6,8},{8,10},{10,12},{12,14},{14,0},{1,3},{3,5},... | collective-permute-start | bytes 786440 | tf_op jit(solution)/shard_map/ppermute | solution.py:243
  93.0 8.6 %collective-permute-start.17 = (bf16[256,512]{1,0:T(8,128)(2,1)S(1)}, bf16[256,512]{1,0:T(8,128)(2,1)S(1)}, u32[]{:S(2)}, u32[]{:S(2)}) collective-permute-start(bf16[256,512]{1,0:T(8,128)(2,1)S(1)} %shard_map.75), channel_id=1, source_target_pairs={{0,14},{2,0},{4,2},{6,4},{8,6},{10,8},{12,10},{14,12},{1,15},{3,1}... | collective-permute-start | bytes 786440 | tf_op jit(solution)/shard_map/ppermute | solution.py:243
  101.7 3.9 %collective-permute-start.11 = (bf16[256,512]{1,0:T(8,128)(2,1)S(1)}, bf16[256,512]{1,0:T(8,128)(2,1)S(1)}, u32[]{:S(2)}, u32[]{:S(2)}) collective-permute-start(bf16[256,512]{1,0:T(8,128)(2,1)S(1)} %shard_map.69), channel_id=1, source_target_pairs={{0,14},{2,0},{4,2},{6,4},{8,6},{10,8},{12,10},{14,12},{1,15},{3,1}... | collective-permute-start | bytes 786440 | tf_op jit(solution)/shard_map/ppermute | solution.py:243
  105.6 1.9 %collective-permute-start.14 = (bf16[256,512]{1,0:T(8,128)(2,1)S(1)}, bf16[256,512]{1,0:T(8,128)(2,1)S(1)}, u32[]{:S(2)}, u32[]{:S(2)}) collective-permute-start(bf16[256,512]{1,0:T(8,128)(2,1)S(1)} %shard_map.72), channel_id=1, source_target_pairs={{0,2},{2,4},{4,6},{6,8},{8,10},{10,12},{12,14},{14,0},{1,3},{3,5},... | collective-permute-start | bytes 786440 | tf_op jit(solution)/shard_map/ppermute | solution.py:243
  107.6 1.9 %collective-permute-start.8 = (bf16[256,512]{1,0:T(8,128)(2,1)S(1)}, bf16[256,512]{1,0:T(8,128)(2,1)S(1)}, u32[]{:S(2)}, u32[]{:S(2)}) collective-permute-start(bf16[256,512]{1,0:T(8,128)(2,1)S(1)} %shard_map.66), channel_id=1, source_target_pairs={{0,2},{2,4},{4,6},{6,8},{8,10},{10,12},{12,14},{14,0},{1,3},{3,5},... | collective-permute-start | bytes 786440 | tf_op jit(solution)/shard_map/ppermute | solution.py:243
  109.7 5.1 %collective-permute-start.18 = (bf16[256,512]{1,0:T(8,128)(2,1)S(1)}, bf16[256,512]{1,0:T(8,128)(2,1)S(1)}, u32[]{:S(2)}, u32[]{:S(2)}) collective-permute-start(bf16[256,512]{1,0:T(8,128)(2,1)S(1)} %shard_map.76), channel_id=1, source_target_pairs={{0,14},{2,0},{4,2},{6,4},{8,6},{10,8},{12,10},{14,12},{1,15},{3,1}... | collective-permute-start | bytes 786440 | tf_op jit(solution)/shard_map/ppermute | solution.py:243
  114.9 3.9 %collective-permute-start.12 = (bf16[256,512]{1,0:T(8,128)(2,1)S(1)}, bf16[256,512]{1,0:T(8,128)(2,1)S(1)}, u32[]{:S(2)}, u32[]{:S(2)}) collective-permute-start(bf16[256,512]{1,0:T(8,128)(2,1)S(1)} %shard_map.70), channel_id=1, source_target_pairs={{0,14},{2,0},{4,2},{6,4},{8,6},{10,8},{12,10},{14,12},{1,15},{3,1}... | collective-permute-start | bytes 786440 | tf_op jit(solution)/shard_map/ppermute | solution.py:243
  118.9 1.9 %collective-permute-start.15 = (bf16[256,512]{1,0:T(8,128)(2,1)S(1)}, bf16[256,512]{1,0:T(8,128)(2,1)S(1)}, u32[]{:S(2)}, u32[]{:S(2)}) collective-permute-start(bf16[256,512]{1,0:T(8,128)(2,1)S(1)} %shard_map.73), channel_id=1, source_target_pairs={{0,2},{2,4},{4,6},{6,8},{8,10},{10,12},{12,14},{14,0},{1,3},{3,5},... | collective-permute-start | bytes 786440 | tf_op jit(solution)/shard_map/ppermute | solution.py:243
  120.9 1.9 %collective-permute-start.9 = (bf16[256,512]{1,0:T(8,128)(2,1)S(1)}, bf16[256,512]{1,0:T(8,128)(2,1)S(1)}, u32[]{:S(2)}, u32[]{:S(2)}) collective-permute-start(bf16[256,512]{1,0:T(8,128)(2,1)S(1)} %shard_map.67), channel_id=1, source_target_pairs={{0,2},{2,4},{4,6},{6,8},{8,10},{10,12},{12,14},{14,0},{1,3},{3,5},... | collective-permute-start | bytes 786440 | tf_op jit(solution)/shard_map/ppermute | solution.py:243
  122.9 5.1 %collective-permute-start.19 = (bf16[256,512]{1,0:T(8,128)(2,1)S(1)}, bf16[256,512]{1,0:T(8,128)(2,1)S(1)}, u32[]{:S(2)}, u32[]{:S(2)}) collective-permute-start(bf16[256,512]{1,0:T(8,128)(2,1)S(1)} %shard_map.77), channel_id=1, source_target_pairs={{0,14},{2,0},{4,2},{6,4},{8,6},{10,8},{12,10},{14,12},{1,15},{3,1}... | collective-permute-start | bytes 786440 | tf_op jit(solution)/shard_map/ppermute | solution.py:243
  128.2 3.9 %collective-permute-start.13 = (bf16[256,512]{1,0:T(8,128)(2,1)S(1)}, bf16[256,512]{1,0:T(8,128)(2,1)S(1)}, u32[]{:S(2)}, u32[]{:S(2)}) collective-permute-start(bf16[256,512]{1,0:T(8,128)(2,1)S(1)} %shard_map.71), channel_id=1, source_target_pairs={{0,14},{2,0},{4,2},{6,4},{8,6},{10,8},{12,10},{14,12},{1,15},{3,1}... | collective-permute-start | bytes 786440 | tf_op jit(solution)/shard_map/ppermute | solution.py:243
  132.2 1.9 %collective-permute-start.16 = (bf16[256,512]{1,0:T(8,128)(2,1)S(1)}, bf16[256,512]{1,0:T(8,128)(2,1)S(1)}, u32[]{:S(2)}, u32[]{:S(2)}) collective-permute-start(bf16[256,512]{1,0:T(8,128)(2,1)S(1)} %shard_map.74), channel_id=1, source_target_pairs={{0,2},{2,4},{4,6},{6,8},{8,10},{10,12},{12,14},{14,0},{1,3},{3,5},... | collective-permute-start | bytes 786440 | tf_op jit(solution)/shard_map/ppermute | solution.py:243
  134.7 1.9 %collective-permute-start.10 = (bf16[256,512]{1,0:T(8,128)(2,1)S(1)}, bf16[256,512]{1,0:T(8,128)(2,1)S(1)}, u32[]{:S(2)}, u32[]{:S(2)}) collective-permute-start(bf16[256,512]{1,0:T(8,128)(2,1)S(1)} %shard_map.68), channel_id=1, source_target_pairs={{0,2},{2,4},{4,6},{6,8},{8,10},{10,12},{12,14},{14,0},{1,3},{3,5},... | collective-permute-start | bytes 786440 | tf_op jit(solution)/shard_map/ppermute | solution.py:243
  136.7 5.1 %collective-permute-start.20 = (bf16[256,512]{1,0:T(8,128)(2,1)S(1)}, bf16[256,512]{1,0:T(8,128)(2,1)S(1)}, u32[]{:S(2)}, u32[]{:S(2)}) collective-permute-start(bf16[256,512]{1,0:T(8,128)(2,1)S(1)} %shard_map.78), channel_id=1, source_target_pairs={{0,14},{2,0},{4,2},{6,4},{8,6},{10,8},{12,10},{14,12},{1,15},{3,1}... | collective-permute-start | bytes 786440 | tf_op jit(solution)/shard_map/ppermute | solution.py:243
  141.9 2.6 %collective-permute-done.10.refs_0_ = bf16[256,512]{1,0:T(8,128)(2,1)S(1)} collective-permute-done((bf16[256,512]{1,0:T(8,128)(2,1)S(1)}, bf16[256,512]{1,0:T(8,128)(2,1)S(1)}, u32[]{:S(2)}, u32[]{:S(2)}) %collective-permute-start.10) | collective-permute-done | bytes 262176 | tf_op jit(solution)/shard_map/ppermute | solution.py:243
  (61 shorter events, 9.2 us)
Async XLA Ops:
  1.0 10.9 %collective-permute-start.2 = (bf16[4,128,256]{2,1,0:T(8,128)(2,1)S(1)}, bf16[4,128,256]{2,1,0:T(8,128)(2,1)S(1)}, u32[]{:S(2)}, u32[]{:S(2)}) collective-permute-start(bf16[4,128,256]{2,1,0:T(8,128)(2,1)S(1)} %bitcast.7), channel_id=1, source_target_pairs={{0,448},{64,0},{128,64},{192,128},{256,192},{320,256},{384,320},{4... | collective-permute-start | bytes 786440 | tf_op jit(solution)/shard_map/ppermute | solution.py:243
  6.4 11.1 %collective-permute-start = (bf16[4,128,256]{2,1,0:T(8,128)(2,1)S(1)}, bf16[4,128,256]{2,1,0:T(8,128)(2,1)S(1)}, u32[]{:S(2)}, u32[]{:S(2)}) collective-permute-start(bf16[4,128,256]{2,1,0:T(8,128)(2,1)S(1)} %bitcast.8), channel_id=1, source_target_pairs={{0,64},{64,128},{128,192},{192,256},{256,320},{320,384},{384,448},... | collective-permute-start | bytes 786440 | tf_op jit(solution)/shard_map/ppermute | solution.py:243
  11.9 25.8 %collective-permute-start.3 = (bf16[4,128,256]{2,1,0:T(8,128)(2,1)S(1)}, bf16[4,128,256]{2,1,0:T(8,128)(2,1)S(1)}, u32[]{:S(2)}, u32[]{:S(2)}) collective-permute-start(bf16[4,128,256]{2,1,0:T(8,128)(2,1)S(1)} %collective-permute-done.2.refs_4_), channel_id=1, source_target_pairs={{0,448},{64,0},{128,64},{192,128},{256,192},{320,256},{384,320},{4... | collective-permute-start | bytes 786440 | tf_op jit(solution)/shard_map/ppermute | solution.py:243
  17.5 20.2 %collective-permute-start.1 = (bf16[4,128,256]{2,1,0:T(8,128)(2,1)S(1)}, bf16[4,128,256]{2,1,0:T(8,128)(2,1)S(1)}, u32[]{:S(2)}, u32[]{:S(2)}) collective-permute-start(bf16[4,128,256]{2,1,0:T(8,128)(2,1)S(1)} %collective-permute-done.refs_1_), channel_id=1, source_target_pairs={{0,64},{64,128},{128,192},{192,256},{256,320},{320,384},{384,448},... | collective-permute-start | bytes 786440 | tf_op jit(solution)/shard_map/ppermute | solution.py:243
  21.0 16.7 %all-to-all-start = ((s32[32,5,16]{2,1,0:T(8,128)}), s32[32,5,16]{2,1,0:T(8,128)S(1)}, u32[]{:S(2)}, u32[]{:S(2)}) async-start(s32[32,5,16]{2,1,0:T(8,128)} %shard_map.64), calls=%async_computation | async-start | bytes 262144 | tf_op jit(solution)/shard_map/all_to_all | solution.py:323
  38.3 32.6 %copy-start.1 = (s32[4,16]{1,0:T(4,128)S(1)}, s32[4,16]{1,0:T(4,128)}, u32[]{:S(2)}) copy-start(s32[4,16]{1,0:T(4,128)} %lists_ref.1) | copy-start | bytes 772
  38.3 33.0 %copy-start.2 = (s32[512]{0:T(512)S(1)}, s32[512]{0:T(512)}, u32[]{:S(2)}) copy-start(s32[512]{0:T(512)} %param.9) | copy-start | bytes 6148
  38.3 40.9 %copy-start = (bf16[512,512]{1,0:T(8,128)(2,1)S(1)}, bf16[512,512]{1,0:T(8,128)(2,1)}, u32[]{:S(2)}) copy-start(bf16[512,512]{1,0:T(8,128)(2,1)} %q_hbm.1) | copy-start | bytes 1572868
  40.2 25.9 %all-to-all-start.1 = ((bf16[4,5,128,256]{3,2,1,0:T(8,128)(2,1)}), bf16[4,5,128,256]{3,2,1,0:T(8,128)(2,1)S(1)}, u32[]{:S(2)}, u32[]{:S(2)}) async-start(bf16[4,5,128,256]{3,2,1,0:T(8,128)(2,1)} %pick.2), calls=%async_computation.1 | async-start | bytes 2621440 | tf_op jit(solution)/shard_map/all_to_all | solution.py:347
  45.6 9.5 %collective-permute-start.4 = (bf16[4,128,256]{2,1,0:T(8,128)(2,1)S(1)}, bf16[4,128,256]{2,1,0:T(8,128)(2,1)S(1)}, u32[]{:S(2)}, u32[]{:S(2)}) collective-permute-start(bf16[4,128,256]{2,1,0:T(8,128)(2,1)S(1)} %collective-permute-done.1.refs_0_.refs_2_), channel_id=1, source_target_pairs={{0,64},{64,128},{128,192},{192,256},{256,320},{320,384},{384,448},... | collective-permute-start | bytes 786440 | tf_op jit(solution)/shard_map/ppermute | solution.py:243
  48.3 8.8 %collective-permute-start.6 = (bf16[4,128,256]{2,1,0:T(8,128)(2,1)S(1)}, bf16[4,128,256]{2,1,0:T(8,128)(2,1)S(1)}, u32[]{:S(2)}, u32[]{:S(2)}) collective-permute-start(bf16[4,128,256]{2,1,0:T(8,128)(2,1)S(1)} %collective-permute-done.3.refs_1_.refs_3_), channel_id=1, source_target_pairs={{0,448},{64,0},{128,64},{192,128},{256,192},{320,256},{384,320},{4... | collective-permute-start | bytes 786440 | tf_op jit(solution)/shard_map/ppermute | solution.py:243
  55.1 9.5 %collective-permute-start.5 = (bf16[4,128,256]{2,1,0:T(8,128)(2,1)S(1)}, bf16[4,128,256]{2,1,0:T(8,128)(2,1)S(1)}, u32[]{:S(2)}, u32[]{:S(2)}) collective-permute-start(bf16[4,128,256]{2,1,0:T(8,128)(2,1)S(1)} %collective-permute-done.4.refs_0_), channel_id=1, source_target_pairs={{0,64},{64,128},{128,192},{192,256},{256,320},{320,384},{384,448},... | collective-permute-start | bytes 786440 | tf_op jit(solution)/shard_map/ppermute | solution.py:243
  66.1 12.8 %all-to-all-start.2 = ((bf16[4,3,128,256]{3,2,1,0:T(8,128)(2,1)}), bf16[4,3,128,256]{3,2,1,0:T(8,128)(2,1)S(1)}, u32[]{:S(2)}, u32[]{:S(2)}) async-start(bf16[4,3,128,256]{3,2,1,0:T(8,128)(2,1)} %pick.3), calls=%async_computation.2 | async-start | bytes 1572864 | tf_op jit(solution)/shard_map/all_to_all | solution.py:347
  88.7 18.8 %collective-permute-start.7 = (bf16[256,512]{1,0:T(8,128)(2,1)S(1)}, bf16[256,512]{1,0:T(8,128)(2,1)S(1)}, u32[]{:S(2)}, u32[]{:S(2)}) collective-permute-start(bf16[256,512]{1,0:T(8,128)(2,1)S(1)} %shard_map.65), channel_id=1, source_target_pairs={{0,2},{2,4},{4,6},{6,8},{8,10},{10,12},{12,14},{14,0},{1,3},{3,5},... | collective-permute-start | bytes 786440 | tf_op jit(solution)/shard_map/ppermute | solution.py:243
  93.0 16.5 %collective-permute-start.17 = (bf16[256,512]{1,0:T(8,128)(2,1)S(1)}, bf16[256,512]{1,0:T(8,128)(2,1)S(1)}, u32[]{:S(2)}, u32[]{:S(2)}) collective-permute-start(bf16[256,512]{1,0:T(8,128)(2,1)S(1)} %shard_map.75), channel_id=1, source_target_pairs={{0,14},{2,0},{4,2},{6,4},{8,6},{10,8},{12,10},{14,12},{1,15},{3,1}... | collective-permute-start | bytes 786440 | tf_op jit(solution)/shard_map/ppermute | solution.py:243
  101.7 13.1 %collective-permute-start.11 = (bf16[256,512]{1,0:T(8,128)(2,1)S(1)}, bf16[256,512]{1,0:T(8,128)(2,1)S(1)}, u32[]{:S(2)}, u32[]{:S(2)}) collective-permute-start(bf16[256,512]{1,0:T(8,128)(2,1)S(1)} %shard_map.69), channel_id=1, source_target_pairs={{0,14},{2,0},{4,2},{6,4},{8,6},{10,8},{12,10},{14,12},{1,15},{3,1}... | collective-permute-start | bytes 786440 | tf_op jit(solution)/shard_map/ppermute | solution.py:243
  105.6 13.2 %collective-permute-start.14 = (bf16[256,512]{1,0:T(8,128)(2,1)S(1)}, bf16[256,512]{1,0:T(8,128)(2,1)S(1)}, u32[]{:S(2)}, u32[]{:S(2)}) collective-permute-start(bf16[256,512]{1,0:T(8,128)(2,1)S(1)} %shard_map.72), channel_id=1, source_target_pairs={{0,2},{2,4},{4,6},{6,8},{8,10},{10,12},{12,14},{14,0},{1,3},{3,5},... | collective-permute-start | bytes 786440 | tf_op jit(solution)/shard_map/ppermute | solution.py:243
  107.6 13.2 %collective-permute-start.8 = (bf16[256,512]{1,0:T(8,128)(2,1)S(1)}, bf16[256,512]{1,0:T(8,128)(2,1)S(1)}, u32[]{:S(2)}, u32[]{:S(2)}) collective-permute-start(bf16[256,512]{1,0:T(8,128)(2,1)S(1)} %shard_map.66), channel_id=1, source_target_pairs={{0,2},{2,4},{4,6},{6,8},{8,10},{10,12},{12,14},{14,0},{1,3},{3,5},... | collective-permute-start | bytes 786440 | tf_op jit(solution)/shard_map/ppermute | solution.py:243
  109.7 13.2 %collective-permute-start.18 = (bf16[256,512]{1,0:T(8,128)(2,1)S(1)}, bf16[256,512]{1,0:T(8,128)(2,1)S(1)}, u32[]{:S(2)}, u32[]{:S(2)}) collective-permute-start(bf16[256,512]{1,0:T(8,128)(2,1)S(1)} %shard_map.76), channel_id=1, source_target_pairs={{0,14},{2,0},{4,2},{6,4},{8,6},{10,8},{12,10},{14,12},{1,15},{3,1}... | collective-permute-start | bytes 786440 | tf_op jit(solution)/shard_map/ppermute | solution.py:243
  114.9 13.2 %collective-permute-start.12 = (bf16[256,512]{1,0:T(8,128)(2,1)S(1)}, bf16[256,512]{1,0:T(8,128)(2,1)S(1)}, u32[]{:S(2)}, u32[]{:S(2)}) collective-permute-start(bf16[256,512]{1,0:T(8,128)(2,1)S(1)} %shard_map.70), channel_id=1, source_target_pairs={{0,14},{2,0},{4,2},{6,4},{8,6},{10,8},{12,10},{14,12},{1,15},{3,1}... | collective-permute-start | bytes 786440 | tf_op jit(solution)/shard_map/ppermute | solution.py:243
  118.9 13.2 %collective-permute-start.15 = (bf16[256,512]{1,0:T(8,128)(2,1)S(1)}, bf16[256,512]{1,0:T(8,128)(2,1)S(1)}, u32[]{:S(2)}, u32[]{:S(2)}) collective-permute-start(bf16[256,512]{1,0:T(8,128)(2,1)S(1)} %shard_map.73), channel_id=1, source_target_pairs={{0,2},{2,4},{4,6},{6,8},{8,10},{10,12},{12,14},{14,0},{1,3},{3,5},... | collective-permute-start | bytes 786440 | tf_op jit(solution)/shard_map/ppermute | solution.py:243
  120.9 13.7 %collective-permute-start.9 = (bf16[256,512]{1,0:T(8,128)(2,1)S(1)}, bf16[256,512]{1,0:T(8,128)(2,1)S(1)}, u32[]{:S(2)}, u32[]{:S(2)}) collective-permute-start(bf16[256,512]{1,0:T(8,128)(2,1)S(1)} %shard_map.67), channel_id=1, source_target_pairs={{0,2},{2,4},{4,6},{6,8},{8,10},{10,12},{12,14},{14,0},{1,3},{3,5},... | collective-permute-start | bytes 786440 | tf_op jit(solution)/shard_map/ppermute | solution.py:243
  122.9 13.7 %collective-permute-start.19 = (bf16[256,512]{1,0:T(8,128)(2,1)S(1)}, bf16[256,512]{1,0:T(8,128)(2,1)S(1)}, u32[]{:S(2)}, u32[]{:S(2)}) collective-permute-start(bf16[256,512]{1,0:T(8,128)(2,1)S(1)} %shard_map.77), channel_id=1, source_target_pairs={{0,14},{2,0},{4,2},{6,4},{8,6},{10,8},{12,10},{14,12},{1,15},{3,1}... | collective-permute-start | bytes 786440 | tf_op jit(solution)/shard_map/ppermute | solution.py:243
  128.2 13.7 %collective-permute-start.13 = (bf16[256,512]{1,0:T(8,128)(2,1)S(1)}, bf16[256,512]{1,0:T(8,128)(2,1)S(1)}, u32[]{:S(2)}, u32[]{:S(2)}) collective-permute-start(bf16[256,512]{1,0:T(8,128)(2,1)S(1)} %shard_map.71), channel_id=1, source_target_pairs={{0,14},{2,0},{4,2},{6,4},{8,6},{10,8},{12,10},{14,12},{1,15},{3,1}... | collective-permute-start | bytes 786440 | tf_op jit(solution)/shard_map/ppermute | solution.py:243
  132.2 9.7 %collective-permute-start.16 = (bf16[256,512]{1,0:T(8,128)(2,1)S(1)}, bf16[256,512]{1,0:T(8,128)(2,1)S(1)}, u32[]{:S(2)}, u32[]{:S(2)}) collective-permute-start(bf16[256,512]{1,0:T(8,128)(2,1)S(1)} %shard_map.74), channel_id=1, source_target_pairs={{0,2},{2,4},{4,6},{6,8},{8,10},{10,12},{12,14},{14,0},{1,3},{3,5},... | collective-permute-start | bytes 786440 | tf_op jit(solution)/shard_map/ppermute | solution.py:243
  134.7 9.8 %collective-permute-start.10 = (bf16[256,512]{1,0:T(8,128)(2,1)S(1)}, bf16[256,512]{1,0:T(8,128)(2,1)S(1)}, u32[]{:S(2)}, u32[]{:S(2)}) collective-permute-start(bf16[256,512]{1,0:T(8,128)(2,1)S(1)} %shard_map.68), channel_id=1, source_target_pairs={{0,2},{2,4},{4,6},{6,8},{8,10},{10,12},{12,14},{14,0},{1,3},{3,5},... | collective-permute-start | bytes 786440 | tf_op jit(solution)/shard_map/ppermute | solution.py:243
  136.7 9.0 %collective-permute-start.20 = (bf16[256,512]{1,0:T(8,128)(2,1)S(1)}, bf16[256,512]{1,0:T(8,128)(2,1)S(1)}, u32[]{:S(2)}, u32[]{:S(2)}) collective-permute-start(bf16[256,512]{1,0:T(8,128)(2,1)S(1)} %shard_map.78), channel_id=1, source_target_pairs={{0,14},{2,0},{4,2},{6,4},{8,6},{10,8},{12,10},{14,12},{1,15},{3,1}... | collective-permute-start | bytes 786440 | tf_op jit(solution)/shard_map/ppermute | solution.py:243

commit v3 on v2

--- a/solution.py
+++ b/solution.py
@@ -267,11 +267,14 @@
         at += rows
 
 
-def ring_scatter(partial, axis, streams):
+def ring_scatter(partial, axis):
     size = lax.axis_size(axis)
     me = lax.axis_index(axis).reshape(1).astype(jnp.int32)
     width = partial.shape[1] // size
-    rows = partial.shape[0] // streams
+    tokens = partial.shape[0]
+    split = tokens * 5 // 8 if tokens % 128 == 0 else tokens // 2
+    parts = ((0, split), (split, tokens - split))
+    streams = len(parts)
 
     def add(groups, *arrived):
         out = jax.ShapeDtypeStruct((sum(g[1] for g in groups), width), partial.dtype)
@@ -280,22 +283,18 @@
 
     far = size // 2
     lengths = [(far, size - 1 - far) if b % 2 == 0 else (size - 1 - far, far) for b in range(streams)]
-    sums = [[None, None] for _ in range(streams)]
-    for b in range(streams):
-        for side, sign in enumerate((1, -1)):
-            sums[b][side] = add(((b * rows, rows, sign * lengths[b][side], 0),))
-    for step in range(1, far + 1):
+    moved = [[None, None] for _ in range(streams)]
+    for step in range(far):
         for b in range(streams):
             for side, sign in enumerate((1, -1)):
                 left = lengths[b][side] - step
-                if left < 0:
+                if left <= 0:
                     continue
-                moved = shifted(sums[b][side], axis, sign)
-                if left:
-                    moved = add(((b * rows, rows, sign * left, 1),), moved)
-                sums[b][side] = moved
-    groups = tuple((b * rows, rows, 0, 2) for b in range(streams))
-    return add(groups, *[term for pair in sums for term in pair])
+                arrived = [moved[b][side]] if step else []
+                running = add(((*parts[b], sign * left, len(arrived)),), *arrived)
+                moved[b][side] = shifted(running, axis, sign)
+    groups = tuple((*part, 0, 2) for part in parts)
+    return add(groups, *[term for pair in moved for term in pair])
 
 
 def per_device(y_count, x_count, queries, keys, values, doc_ids, block_lists, w_out):
@@ -368,7 +367,7 @@
     ends = jnp.broadcast_to(ends[:, None], (tok_rows, BLOCK_TOKENS))
 
     partial = attention(queries, starts, ends, w_out, tables, slot, base)
-    return ring_scatter(partial, "head", 2)
+    return ring_scatter(partial, "head")
 
 
 def solution(mesh):

time: 148 us -> 160 us (1.081)
  waiting for transfers between devices: 34.3 us -> 46 us
    ppermute x21, waiting for transfers between devices: 17.9 us -> 29.6 us  [shifted(): return lax.ppermute(x, axis, [(i, (i + shift) % size) for i in range(size)])]
  transfers between devices with their start and end apart: 24 -> 24, of which waited for: 8 -> 10; matrix products, arithmetic and copies ran while one was open for 0% -> 0% of each run, Pallas kernels for 3% -> 2%
where the time goes in v3:
time: 160 us
  starting transfers between devices  94.6 us (59%)
  waiting for transfers between devices  46 us (29%)
  Pallas kernels  16.2 us (10%)
  other arithmetic  1.64 us (1%)
    ppermute x21, starting transfers between devices, shifted(): return lax.ppermute(x, axis, [(i, (i + shift) % size) for i in range(size)])  76.6 us
    ppermute x21, waiting for transfers between devices, shifted(): return lax.ppermute(x, axis, [(i, (i + shift) % size) for i in range(size)])  29.6 us
    all_to_all x2, starting transfers between devices, per_device(): arrived = lax.all_to_all(outgoing, 'x', 0, 0, tiled=True)  10.2 us
    pallas_call x1, Pallas kernels, attention(): pl.pallas_call(attention_kernel, out_shape=jax.ShapeDtypeStruct((tokens,...  9.45 us
    all_to_all x1, waiting for transfers between devices, per_device(): info = lax.all_to_all(info, ('y', 'x'), 0, 0, tiled=True)  8.84 us
    all_to_all x1, starting transfers between devices, per_device(): info = lax.all_to_all(info, ('y', 'x'), 0, 0, tiled=True)  7.78 us
    all_to_all x2, waiting for transfers between devices, per_device(): arrived = lax.all_to_all(outgoing, 'x', 0, 0, tiled=True)  7.56 us
    pallas_call x2, Pallas kernels, pick(): pl.pallas_call(functools.partial(pick_kernel, len(pieces)), out_shape=jax...  3.37 us
  transfers between devices with their start and end apart: 24, of which 10 were waited for; matrix products, arithmetic and copies ran while one was open for 0% of the time, Pallas kernels for 2%

profile of v3, /device:TPU:2, one launch (start us, length us, event | category | flops | bytes accessed | tf_op | source)
XLA Modules:
  0.0 159.6 jit_solution(41200692534840665)
XLA Ops:
  1.0 5.4 %collective-permute-start.2 = (bf16[4,128,256]{2,1,0:T(8,128)(2,1)S(1)}, bf16[4,128,256]{2,1,0:T(8,128)(2,1)S(1)}, u32[]{:S(2)}, u32[]{:S(2)}) collective-permute-start(bf16[4,128,256]{2,1,0:T(8,128)(2,1)S(1)} %bitcast.7), channel_id=1, source_target_pairs={{0,448},{64,0},{128,64},{192,128},{256,192},{320,256},{384,320},{4... | collective-permute-start | bytes 786440 | tf_op jit(solution)/shard_map/ppermute | solution.py:243
  6.4 1.9 %collective-permute-start = (bf16[4,128,256]{2,1,0:T(8,128)(2,1)S(1)}, bf16[4,128,256]{2,1,0:T(8,128)(2,1)S(1)}, u32[]{:S(2)}, u32[]{:S(2)}) collective-permute-start(bf16[4,128,256]{2,1,0:T(8,128)(2,1)S(1)} %bitcast.8), channel_id=1, source_target_pairs={{0,64},{64,128},{128,192},{192,256},{256,320},{320,384},{384,448},... | collective-permute-start | bytes 786440 | tf_op jit(solution)/shard_map/ppermute | solution.py:243
  8.3 3.6 %collective-permute-done.2.refs_4_ = bf16[4,128,256]{2,1,0:T(8,128)(2,1)S(1)} collective-permute-done((bf16[4,128,256]{2,1,0:T(8,128)(2,1)S(1)}, bf16[4,128,256]{2,1,0:T(8,128)(2,1)S(1)}, u32[]{:S(2)}, u32[]{:S(2)}) %collective-permute-start.2) | collective-permute-done | bytes 262176 | tf_op jit(solution)/shard_map/ppermute | solution.py:243
  11.9 5.6 %collective-permute-start.3 = (bf16[4,128,256]{2,1,0:T(8,128)(2,1)S(1)}, bf16[4,128,256]{2,1,0:T(8,128)(2,1)S(1)}, u32[]{:S(2)}, u32[]{:S(2)}) collective-permute-start(bf16[4,128,256]{2,1,0:T(8,128)(2,1)S(1)} %collective-permute-done.2.refs_4_), channel_id=1, source_target_pairs={{0,448},{64,0},{128,64},{192,128},{256,192},{320,256},{384,320},{4... | collective-permute-start | bytes 786440 | tf_op jit(solution)/shard_map/ppermute | solution.py:243
  17.5 1.9 %collective-permute-start.1 = (bf16[4,128,256]{2,1,0:T(8,128)(2,1)S(1)}, bf16[4,128,256]{2,1,0:T(8,128)(2,1)S(1)}, u32[]{:S(2)}, u32[]{:S(2)}) collective-permute-start(bf16[4,128,256]{2,1,0:T(8,128)(2,1)S(1)} %collective-permute-done.refs_1_), channel_id=1, source_target_pairs={{0,64},{64,128},{128,192},{192,256},{256,320},{320,384},{384,448},... | collective-permute-start | bytes 786440 | tf_op jit(solution)/shard_map/ppermute | solution.py:243
  21.0 7.8 %all-to-all-start = ((s32[32,5,16]{2,1,0:T(8,128)}), s32[32,5,16]{2,1,0:T(8,128)S(1)}, u32[]{:S(2)}, u32[]{:S(2)}) async-start(s32[32,5,16]{2,1,0:T(8,128)} %shard_map.64), calls=%async_computation | async-start | bytes 262144 | tf_op jit(solution)/shard_map/all_to_all | solution.py:322
  28.9 8.8 %all-to-all-done.source_ref = s32[32,5,16]{2,1,0:T(8,128)S(1)} async-done(((s32[32,5,16]{2,1,0:T(8,128)}), s32[32,5,16]{2,1,0:T(8,128)S(1)}, u32[]{:S(2)}, u32[]{:S(2)}) %all-to-all-start) | async-done | bytes 10272 | tf_op jit(solution)/shard_map/all_to_all | solution.py:322
  40.2 5.4 %all-to-all-start.1 = ((bf16[4,5,128,256]{3,2,1,0:T(8,128)(2,1)}), bf16[4,5,128,256]{3,2,1,0:T(8,128)(2,1)S(1)}, u32[]{:S(2)}, u32[]{:S(2)}) async-start(bf16[4,5,128,256]{3,2,1,0:T(8,128)(2,1)} %pick.2), calls=%async_computation.1 | async-start | bytes 2621440 | tf_op jit(solution)/shard_map/all_to_all | solution.py:346
  45.6 2.7 %collective-permute-start.4 = (bf16[4,128,256]{2,1,0:T(8,128)(2,1)S(1)}, bf16[4,128,256]{2,1,0:T(8,128)(2,1)S(1)}, u32[]{:S(2)}, u32[]{:S(2)}) collective-permute-start(bf16[4,128,256]{2,1,0:T(8,128)(2,1)S(1)} %collective-permute-done.1.refs_0_.refs_2_), channel_id=1, source_target_pairs={{0,64},{64,128},{128,192},{192,256},{256,320},{320,384},{384,448},... | collective-permute-start | bytes 786440 | tf_op jit(solution)/shard_map/ppermute | solution.py:243
  48.3 4.3 %collective-permute-start.6 = (bf16[4,128,256]{2,1,0:T(8,128)(2,1)S(1)}, bf16[4,128,256]{2,1,0:T(8,128)(2,1)S(1)}, u32[]{:S(2)}, u32[]{:S(2)}) collective-permute-start(bf16[4,128,256]{2,1,0:T(8,128)(2,1)S(1)} %collective-permute-done.3.refs_1_.refs_3_), channel_id=1, source_target_pairs={{0,448},{64,0},{128,64},{192,128},{256,192},{320,256},{384,320},{4... | collective-permute-start | bytes 786440 | tf_op jit(solution)/shard_map/ppermute | solution.py:243
  52.7 2.4 %collective-permute-done.4.refs_0_ = bf16[4,128,256]{2,1,0:T(8,128)(2,1)S(1)} collective-permute-done((bf16[4,128,256]{2,1,0:T(8,128)(2,1)S(1)}, bf16[4,128,256]{2,1,0:T(8,128)(2,1)S(1)}, u32[]{:S(2)}, u32[]{:S(2)}) %collective-permute-start.4) | collective-permute-done | bytes 262176 | tf_op jit(solution)/shard_map/ppermute | solution.py:243
  57.1 7.5 %collective-permute-done.5.refs_1_ = bf16[4,128,256]{2,1,0:T(8,128)(2,1)S(1)} collective-permute-done((bf16[4,128,256]{2,1,0:T(8,128)(2,1)S(1)}, bf16[4,128,256]{2,1,0:T(8,128)(2,1)S(1)}, u32[]{:S(2)}, u32[]{:S(2)}) %collective-permute-start.5) | collective-permute-done | bytes 262176 | tf_op jit(solution)/shard_map/ppermute | solution.py:243
  66.1 4.8 %all-to-all-start.2 = ((bf16[4,3,128,256]{3,2,1,0:T(8,128)(2,1)}), bf16[4,3,128,256]{3,2,1,0:T(8,128)(2,1)S(1)}, u32[]{:S(2)}, u32[]{:S(2)}) async-start(bf16[4,3,128,256]{3,2,1,0:T(8,128)(2,1)} %pick.3), calls=%async_computation.2 | async-start | bytes 1572864 | tf_op jit(solution)/shard_map/all_to_all | solution.py:346
  71.4 7.6 %all-to-all-done.2 = bf16[4,3,128,256]{3,2,1,0:T(8,128)(2,1)S(1)} async-done(((bf16[4,3,128,256]{3,2,1,0:T(8,128)(2,1)}), bf16[4,3,128,256]{3,2,1,0:T(8,128)(2,1)S(1)}, u32[]{:S(2)}, u32[]{:S(2)}) %all-to-all-start.2) | async-done | bytes 786464 | tf_op jit(solution)/shard_map/all_to_all | solution.py:346
  79.2 9.5 %attention.1.partial_ref = bf16[512,4096]{1,0:T(8,128)(2,1)S(1)} custom-call(s32[64]{0:T(128)S(1)} %reshape.82.slot, s32[64]{0:T(128)S(1)} %reshape.83.base, s32[512,128]{1,0:T(8,128)S(1)} %broadcast_in_dim.72.start_ref, s32[512,128]{1,0:T(8,128)S(1)} %broadcast_in_dim.76.end_ref, bf16[512,512]{1,0:T(8,128)(2,1)S(1)} %copy-done, bf16[512,4096]{1,0:T(8,128)(2,1)} %w_hbm.1, ...), custom_call_target="tpu_custom_call" | custom-call | flops 4294967296 | bytes 4194304 | tf_op jit(solution)/shard_map/attention/pallas_call | solution.py:125
  88.7 4.3 %collective-permute-start.7 = (bf16[320,512]{1,0:T(8,128)(2,1)S(1)}, bf16[320,512]{1,0:T(8,128)(2,1)S(1)}, u32[]{:S(2)}, u32[]{:S(2)}) collective-permute-start(bf16[320,512]{1,0:T(8,128)(2,1)S(1)} %shard_map.65), channel_id=1, source_target_pairs={{0,2},{2,4},{4,6},{6,8},{8,10},{10,12},{12,14},{14,0},{1,3},{3,5},... | collective-permute-start | bytes 983048 | tf_op jit(solution)/shard_map/ppermute | solution.py:243
  93.1 8.6 %collective-permute-start.11 = (bf16[320,512]{1,0:T(8,128)(2,1)S(1)}, bf16[320,512]{1,0:T(8,128)(2,1)S(1)}, u32[]{:S(2)}, u32[]{:S(2)}) collective-permute-start(bf16[320,512]{1,0:T(8,128)(2,1)S(1)} %shard_map.69), channel_id=1, source_target_pairs={{0,14},{2,0},{4,2},{6,4},{8,6},{10,8},{12,10},{14,12},{1,15},{3,1}... | collective-permute-start | bytes 983048 | tf_op jit(solution)/shard_map/ppermute | solution.py:243
  101.6 5.2 %collective-permute-done.7.refs_0_ = bf16[320,512]{1,0:T(8,128)(2,1)S(1)} collective-permute-done((bf16[320,512]{1,0:T(8,128)(2,1)S(1)}, bf16[320,512]{1,0:T(8,128)(2,1)S(1)}, u32[]{:S(2)}, u32[]{:S(2)}) %collective-permute-start.7) | collective-permute-done | bytes 327712 | tf_op jit(solution)/shard_map/ppermute | solution.py:243
  106.9 1.9 %collective-permute-start.8 = (bf16[320,512]{1,0:T(8,128)(2,1)S(1)}, bf16[320,512]{1,0:T(8,128)(2,1)S(1)}, u32[]{:S(2)}, u32[]{:S(2)}) collective-permute-start(bf16[320,512]{1,0:T(8,128)(2,1)S(1)} %shard_map.66), channel_id=1, source_target_pairs={{0,2},{2,4},{4,6},{6,8},{8,10},{10,12},{12,14},{14,0},{1,3},{3,5},... | collective-permute-start | bytes 983048 | tf_op jit(solution)/shard_map/ppermute | solution.py:243
  108.9 5.2 %collective-permute-start.17 = (bf16[192,512]{1,0:T(8,128)(2,1)S(1)}, bf16[192,512]{1,0:T(8,128)(2,1)S(1)}, u32[]{:S(2)}, u32[]{:S(2)}) collective-permute-start(bf16[192,512]{1,0:T(8,128)(2,1)S(1)} %shard_map.75), channel_id=1, source_target_pairs={{0,14},{2,0},{4,2},{6,4},{8,6},{10,8},{12,10},{14,12},{1,15},{3,1}... | collective-permute-start | bytes 589832 | tf_op jit(solution)/shard_map/ppermute | solution.py:243
  114.2 3.9 %collective-permute-start.12 = (bf16[320,512]{1,0:T(8,128)(2,1)S(1)}, bf16[320,512]{1,0:T(8,128)(2,1)S(1)}, u32[]{:S(2)}, u32[]{:S(2)}) collective-permute-start(bf16[320,512]{1,0:T(8,128)(2,1)S(1)} %shard_map.70), channel_id=1, source_target_pairs={{0,14},{2,0},{4,2},{6,4},{8,6},{10,8},{12,10},{14,12},{1,15},{3,1}... | collective-permute-start | bytes 983048 | tf_op jit(solution)/shard_map/ppermute | solution.py:243
  118.1 2.4 %collective-permute-done.8.refs_0_ = bf16[320,512]{1,0:T(8,128)(2,1)S(1)} collective-permute-done((bf16[320,512]{1,0:T(8,128)(2,1)S(1)}, bf16[320,512]{1,0:T(8,128)(2,1)S(1)}, u32[]{:S(2)}, u32[]{:S(2)}) %collective-permute-start.8) | collective-permute-done | bytes 327712 | tf_op jit(solution)/shard_map/ppermute | solution.py:243
  120.6 1.9 %collective-permute-start.9 = (bf16[320,512]{1,0:T(8,128)(2,1)S(1)}, bf16[320,512]{1,0:T(8,128)(2,1)S(1)}, u32[]{:S(2)}, u32[]{:S(2)}) collective-permute-start(bf16[320,512]{1,0:T(8,128)(2,1)S(1)} %shard_map.67), channel_id=1, source_target_pairs={{0,2},{2,4},{4,6},{6,8},{8,10},{10,12},{12,14},{14,0},{1,3},{3,5},... | collective-permute-start | bytes 983048 | tf_op jit(solution)/shard_map/ppermute | solution.py:243
  122.5 1.9 %collective-permute-start.14 = (bf16[192,512]{1,0:T(8,128)(2,1)S(1)}, bf16[192,512]{1,0:T(8,128)(2,1)S(1)}, u32[]{:S(2)}, u32[]{:S(2)}) collective-permute-start(bf16[192,512]{1,0:T(8,128)(2,1)S(1)} %shard_map.72), channel_id=1, source_target_pairs={{0,2},{2,4},{4,6},{6,8},{8,10},{10,12},{12,14},{14,0},{1,3},{3,5},... | collective-permute-start | bytes 589832 | tf_op jit(solution)/shard_map/ppermute | solution.py:243
  124.5 5.1 %collective-permute-start.18 = (bf16[192,512]{1,0:T(8,128)(2,1)S(1)}, bf16[192,512]{1,0:T(8,128)(2,1)S(1)}, u32[]{:S(2)}, u32[]{:S(2)}) collective-permute-start(bf16[192,512]{1,0:T(8,128)(2,1)S(1)} %shard_map.76), channel_id=1, source_target_pairs={{0,14},{2,0},{4,2},{6,4},{8,6},{10,8},{12,10},{14,12},{1,15},{3,1}... | collective-permute-start | bytes 589832 | tf_op jit(solution)/shard_map/ppermute | solution.py:243
  129.7 5.3 %collective-permute-done.14.refs_0_ = bf16[192,512]{1,0:T(8,128)(2,1)S(1)} collective-permute-done((bf16[192,512]{1,0:T(8,128)(2,1)S(1)}, bf16[192,512]{1,0:T(8,128)(2,1)S(1)}, u32[]{:S(2)}, u32[]{:S(2)}) %collective-permute-start.14) | collective-permute-done | bytes 196640 | tf_op jit(solution)/shard_map/ppermute | solution.py:243
  135.0 1.9 %collective-permute-start.15 = (bf16[192,512]{1,0:T(8,128)(2,1)S(1)}, bf16[192,512]{1,0:T(8,128)(2,1)S(1)}, u32[]{:S(2)}, u32[]{:S(2)}) collective-permute-start(bf16[192,512]{1,0:T(8,128)(2,1)S(1)} %shard_map.73), channel_id=1, source_target_pairs={{0,2},{2,4},{4,6},{6,8},{8,10},{10,12},{12,14},{14,0},{1,3},{3,5},... | collective-permute-start | bytes 589832 | tf_op jit(solution)/shard_map/ppermute | solution.py:243
  137.0 5.1 %collective-permute-start.19 = (bf16[192,512]{1,0:T(8,128)(2,1)S(1)}, bf16[192,512]{1,0:T(8,128)(2,1)S(1)}, u32[]{:S(2)}, u32[]{:S(2)}) collective-permute-start(bf16[192,512]{1,0:T(8,128)(2,1)S(1)} %shard_map.77), channel_id=1, source_target_pairs={{0,14},{2,0},{4,2},{6,4},{8,6},{10,8},{12,10},{14,12},{1,15},{3,1}... | collective-permute-start | bytes 589832 | tf_op jit(solution)/shard_map/ppermute | solution.py:243
  142.2 1.9 %collective-permute-start.13 = (bf16[320,512]{1,0:T(8,128)(2,1)S(1)}, bf16[320,512]{1,0:T(8,128)(2,1)S(1)}, u32[]{:S(2)}, u32[]{:S(2)}) collective-permute-start(bf16[320,512]{1,0:T(8,128)(2,1)S(1)} %shard_map.71), channel_id=1, source_target_pairs={{0,14},{2,0},{4,2},{6,4},{8,6},{10,8},{12,10},{14,12},{1,15},{3,1}... | collective-permute-start | bytes 983048 | tf_op jit(solution)/shard_map/ppermute | solution.py:243
  144.3 3.9 %collective-permute-start.10 = (bf16[320,512]{1,0:T(8,128)(2,1)S(1)}, bf16[320,512]{1,0:T(8,128)(2,1)S(1)}, u32[]{:S(2)}, u32[]{:S(2)}) collective-permute-start(bf16[320,512]{1,0:T(8,128)(2,1)S(1)} %shard_map.68), channel_id=1, source_target_pairs={{0,2},{2,4},{4,6},{6,8},{8,10},{10,12},{12,14},{14,0},{1,3},{3,5},... | collective-permute-start | bytes 983048 | tf_op jit(solution)/shard_map/ppermute | solution.py:243
  148.3 1.9 %collective-permute-start.16 = (bf16[192,512]{1,0:T(8,128)(2,1)S(1)}, bf16[192,512]{1,0:T(8,128)(2,1)S(1)}, u32[]{:S(2)}, u32[]{:S(2)}) collective-permute-start(bf16[192,512]{1,0:T(8,128)(2,1)S(1)} %shard_map.74), channel_id=1, source_target_pairs={{0,2},{2,4},{4,6},{6,8},{8,10},{10,12},{12,14},{14,0},{1,3},{3,5},... | collective-permute-start | bytes 589832 | tf_op jit(solution)/shard_map/ppermute | solution.py:243
  150.3 5.1 %collective-permute-start.20 = (bf16[192,512]{1,0:T(8,128)(2,1)S(1)}, bf16[192,512]{1,0:T(8,128)(2,1)S(1)}, u32[]{:S(2)}, u32[]{:S(2)}) collective-permute-start(bf16[192,512]{1,0:T(8,128)(2,1)S(1)} %shard_map.78), channel_id=1, source_target_pairs={{0,14},{2,0},{4,2},{6,4},{8,6},{10,8},{12,10},{14,12},{1,15},{3,1}... | collective-permute-start | bytes 589832 | tf_op jit(solution)/shard_map/ppermute | solution.py:243
  (61 shorter events, 14.2 us)
Async XLA Ops:
  1.0 10.9 %collective-permute-start.2 = (bf16[4,128,256]{2,1,0:T(8,128)(2,1)S(1)}, bf16[4,128,256]{2,1,0:T(8,128)(2,1)S(1)}, u32[]{:S(2)}, u32[]{:S(2)}) collective-permute-start(bf16[4,128,256]{2,1,0:T(8,128)(2,1)S(1)} %bitcast.7), channel_id=1, source_target_pairs={{0,448},{64,0},{128,64},{192,128},{256,192},{320,256},{384,320},{4... | collective-permute-start | bytes 786440 | tf_op jit(solution)/shard_map/ppermute | solution.py:243
  6.4 11.1 %collective-permute-start = (bf16[4,128,256]{2,1,0:T(8,128)(2,1)S(1)}, bf16[4,128,256]{2,1,0:T(8,128)(2,1)S(1)}, u32[]{:S(2)}, u32[]{:S(2)}) collective-permute-start(bf16[4,128,256]{2,1,0:T(8,128)(2,1)S(1)} %bitcast.8), channel_id=1, source_target_pairs={{0,64},{64,128},{128,192},{192,256},{256,320},{320,384},{384,448},... | collective-permute-start | bytes 786440 | tf_op jit(solution)/shard_map/ppermute | solution.py:243
  11.9 25.8 %collective-permute-start.3 = (bf16[4,128,256]{2,1,0:T(8,128)(2,1)S(1)}, bf16[4,128,256]{2,1,0:T(8,128)(2,1)S(1)}, u32[]{:S(2)}, u32[]{:S(2)}) collective-permute-start(bf16[4,128,256]{2,1,0:T(8,128)(2,1)S(1)} %collective-permute-done.2.refs_4_), channel_id=1, source_target_pairs={{0,448},{64,0},{128,64},{192,128},{256,192},{320,256},{384,320},{4... | collective-permute-start | bytes 786440 | tf_op jit(solution)/shard_map/ppermute | solution.py:243
  17.5 20.2 %collective-permute-start.1 = (bf16[4,128,256]{2,1,0:T(8,128)(2,1)S(1)}, bf16[4,128,256]{2,1,0:T(8,128)(2,1)S(1)}, u32[]{:S(2)}, u32[]{:S(2)}) collective-permute-start(bf16[4,128,256]{2,1,0:T(8,128)(2,1)S(1)} %collective-permute-done.refs_1_), channel_id=1, source_target_pairs={{0,64},{64,128},{128,192},{192,256},{256,320},{320,384},{384,448},... | collective-permute-start | bytes 786440 | tf_op jit(solution)/shard_map/ppermute | solution.py:243
  21.0 16.7 %all-to-all-start = ((s32[32,5,16]{2,1,0:T(8,128)}), s32[32,5,16]{2,1,0:T(8,128)S(1)}, u32[]{:S(2)}, u32[]{:S(2)}) async-start(s32[32,5,16]{2,1,0:T(8,128)} %shard_map.64), calls=%async_computation | async-start | bytes 262144 | tf_op jit(solution)/shard_map/all_to_all | solution.py:322
  38.3 32.6 %copy-start.1 = (s32[4,16]{1,0:T(4,128)S(1)}, s32[4,16]{1,0:T(4,128)}, u32[]{:S(2)}) copy-start(s32[4,16]{1,0:T(4,128)} %lists_ref.1) | copy-start | bytes 772
  38.3 33.0 %copy-start.2 = (s32[512]{0:T(512)S(1)}, s32[512]{0:T(512)}, u32[]{:S(2)}) copy-start(s32[512]{0:T(512)} %param.9) | copy-start | bytes 6148
  38.3 40.9 %copy-start = (bf16[512,512]{1,0:T(8,128)(2,1)S(1)}, bf16[512,512]{1,0:T(8,128)(2,1)}, u32[]{:S(2)}) copy-start(bf16[512,512]{1,0:T(8,128)(2,1)} %q_hbm.1) | copy-start | bytes 1572868
  40.2 25.9 %all-to-all-start.1 = ((bf16[4,5,128,256]{3,2,1,0:T(8,128)(2,1)}), bf16[4,5,128,256]{3,2,1,0:T(8,128)(2,1)S(1)}, u32[]{:S(2)}, u32[]{:S(2)}) async-start(bf16[4,5,128,256]{3,2,1,0:T(8,128)(2,1)} %pick.2), calls=%async_computation.1 | async-start | bytes 2621440 | tf_op jit(solution)/shard_map/all_to_all | solution.py:346
  45.6 9.5 %collective-permute-start.4 = (bf16[4,128,256]{2,1,0:T(8,128)(2,1)S(1)}, bf16[4,128,256]{2,1,0:T(8,128)(2,1)S(1)}, u32[]{:S(2)}, u32[]{:S(2)}) collective-permute-start(bf16[4,128,256]{2,1,0:T(8,128)(2,1)S(1)} %collective-permute-done.1.refs_0_.refs_2_), channel_id=1, source_target_pairs={{0,64},{64,128},{128,192},{192,256},{256,320},{320,384},{384,448},... | collective-permute-start | bytes 786440 | tf_op jit(solution)/shard_map/ppermute | solution.py:243
  48.3 8.8 %collective-permute-start.6 = (bf16[4,128,256]{2,1,0:T(8,128)(2,1)S(1)}, bf16[4,128,256]{2,1,0:T(8,128)(2,1)S(1)}, u32[]{:S(2)}, u32[]{:S(2)}) collective-permute-start(bf16[4,128,256]{2,1,0:T(8,128)(2,1)S(1)} %collective-permute-done.3.refs_1_.refs_3_), channel_id=1, source_target_pairs={{0,448},{64,0},{128,64},{192,128},{256,192},{320,256},{384,320},{4... | collective-permute-start | bytes 786440 | tf_op jit(solution)/shard_map/ppermute | solution.py:243
  55.1 9.5 %collective-permute-start.5 = (bf16[4,128,256]{2,1,0:T(8,128)(2,1)S(1)}, bf16[4,128,256]{2,1,0:T(8,128)(2,1)S(1)}, u32[]{:S(2)}, u32[]{:S(2)}) collective-permute-start(bf16[4,128,256]{2,1,0:T(8,128)(2,1)S(1)} %collective-permute-done.4.refs_0_), channel_id=1, source_target_pairs={{0,64},{64,128},{128,192},{192,256},{256,320},{320,384},{384,448},... | collective-permute-start | bytes 786440 | tf_op jit(solution)/shard_map/ppermute | solution.py:243
  66.1 12.8 %all-to-all-start.2 = ((bf16[4,3,128,256]{3,2,1,0:T(8,128)(2,1)}), bf16[4,3,128,256]{3,2,1,0:T(8,128)(2,1)S(1)}, u32[]{:S(2)}, u32[]{:S(2)}) async-start(bf16[4,3,128,256]{3,2,1,0:T(8,128)(2,1)} %pick.3), calls=%async_computation.2 | async-start | bytes 1572864 | tf_op jit(solution)/shard_map/all_to_all | solution.py:346
  88.7 18.1 %collective-permute-start.7 = (bf16[320,512]{1,0:T(8,128)(2,1)S(1)}, bf16[320,512]{1,0:T(8,128)(2,1)S(1)}, u32[]{:S(2)}, u32[]{:S(2)}) collective-permute-start(bf16[320,512]{1,0:T(8,128)(2,1)S(1)} %shard_map.65), channel_id=1, source_target_pairs={{0,2},{2,4},{4,6},{6,8},{8,10},{10,12},{12,14},{14,0},{1,3},{3,5},... | collective-permute-start | bytes 983048 | tf_op jit(solution)/shard_map/ppermute | solution.py:243
  93.1 21.0 %collective-permute-start.11 = (bf16[320,512]{1,0:T(8,128)(2,1)S(1)}, bf16[320,512]{1,0:T(8,128)(2,1)S(1)}, u32[]{:S(2)}, u32[]{:S(2)}) collective-permute-start(bf16[320,512]{1,0:T(8,128)(2,1)S(1)} %shard_map.69), channel_id=1, source_target_pairs={{0,14},{2,0},{4,2},{6,4},{8,6},{10,8},{12,10},{14,12},{1,15},{3,1}... | collective-permute-start | bytes 983048 | tf_op jit(solution)/shard_map/ppermute | solution.py:243
  106.9 13.5 %collective-permute-start.8 = (bf16[320,512]{1,0:T(8,128)(2,1)S(1)}, bf16[320,512]{1,0:T(8,128)(2,1)S(1)}, u32[]{:S(2)}, u32[]{:S(2)}) collective-permute-start(bf16[320,512]{1,0:T(8,128)(2,1)S(1)} %shard_map.66), channel_id=1, source_target_pairs={{0,2},{2,4},{4,6},{6,8},{8,10},{10,12},{12,14},{14,0},{1,3},{3,5},... | collective-permute-start | bytes 983048 | tf_op jit(solution)/shard_map/ppermute | solution.py:243
  108.9 15.6 %collective-permute-start.17 = (bf16[192,512]{1,0:T(8,128)(2,1)S(1)}, bf16[192,512]{1,0:T(8,128)(2,1)S(1)}, u32[]{:S(2)}, u32[]{:S(2)}) collective-permute-start(bf16[192,512]{1,0:T(8,128)(2,1)S(1)} %shard_map.75), channel_id=1, source_target_pairs={{0,14},{2,0},{4,2},{6,4},{8,6},{10,8},{12,10},{14,12},{1,15},{3,1}... | collective-permute-start | bytes 589832 | tf_op jit(solution)/shard_map/ppermute | solution.py:243
  114.2 28.0 %collective-permute-start.12 = (bf16[320,512]{1,0:T(8,128)(2,1)S(1)}, bf16[320,512]{1,0:T(8,128)(2,1)S(1)}, u32[]{:S(2)}, u32[]{:S(2)}) collective-permute-start(bf16[320,512]{1,0:T(8,128)(2,1)S(1)} %shard_map.70), channel_id=1, source_target_pairs={{0,14},{2,0},{4,2},{6,4},{8,6},{10,8},{12,10},{14,12},{1,15},{3,1}... | collective-permute-start | bytes 983048 | tf_op jit(solution)/shard_map/ppermute | solution.py:243
  120.6 23.6 %collective-permute-start.9 = (bf16[320,512]{1,0:T(8,128)(2,1)S(1)}, bf16[320,512]{1,0:T(8,128)(2,1)S(1)}, u32[]{:S(2)}, u32[]{:S(2)}) collective-permute-start(bf16[320,512]{1,0:T(8,128)(2,1)S(1)} %shard_map.67), channel_id=1, source_target_pairs={{0,2},{2,4},{4,6},{6,8},{8,10},{10,12},{12,14},{14,0},{1,3},{3,5},... | collective-permute-start | bytes 983048 | tf_op jit(solution)/shard_map/ppermute | solution.py:243
  122.5 12.4 %collective-permute-start.14 = (bf16[192,512]{1,0:T(8,128)(2,1)S(1)}, bf16[192,512]{1,0:T(8,128)(2,1)S(1)}, u32[]{:S(2)}, u32[]{:S(2)}) collective-permute-start(bf16[192,512]{1,0:T(8,128)(2,1)S(1)} %shard_map.72), channel_id=1, source_target_pairs={{0,2},{2,4},{4,6},{6,8},{8,10},{10,12},{12,14},{14,0},{1,3},{3,5},... | collective-permute-start | bytes 589832 | tf_op jit(solution)/shard_map/ppermute | solution.py:243
  124.5 12.4 %collective-permute-start.18 = (bf16[192,512]{1,0:T(8,128)(2,1)S(1)}, bf16[192,512]{1,0:T(8,128)(2,1)S(1)}, u32[]{:S(2)}, u32[]{:S(2)}) collective-permute-start(bf16[192,512]{1,0:T(8,128)(2,1)S(1)} %shard_map.76), channel_id=1, source_target_pairs={{0,14},{2,0},{4,2},{6,4},{8,6},{10,8},{12,10},{14,12},{1,15},{3,1}... | collective-permute-start | bytes 589832 | tf_op jit(solution)/shard_map/ppermute | solution.py:243
  135.0 13.2 %collective-permute-start.15 = (bf16[192,512]{1,0:T(8,128)(2,1)S(1)}, bf16[192,512]{1,0:T(8,128)(2,1)S(1)}, u32[]{:S(2)}, u32[]{:S(2)}) collective-permute-start(bf16[192,512]{1,0:T(8,128)(2,1)S(1)} %shard_map.73), channel_id=1, source_target_pairs={{0,2},{2,4},{4,6},{6,8},{8,10},{10,12},{12,14},{14,0},{1,3},{3,5},... | collective-permute-start | bytes 589832 | tf_op jit(solution)/shard_map/ppermute | solution.py:243
  137.0 13.2 %collective-permute-start.19 = (bf16[192,512]{1,0:T(8,128)(2,1)S(1)}, bf16[192,512]{1,0:T(8,128)(2,1)S(1)}, u32[]{:S(2)}, u32[]{:S(2)}) collective-permute-start(bf16[192,512]{1,0:T(8,128)(2,1)S(1)} %shard_map.77), channel_id=1, source_target_pairs={{0,14},{2,0},{4,2},{6,4},{8,6},{10,8},{12,10},{14,12},{1,15},{3,1}... | collective-permute-start | bytes 589832 | tf_op jit(solution)/shard_map/ppermute | solution.py:243
  142.2 16.3 %collective-permute-start.13 = (bf16[320,512]{1,0:T(8,128)(2,1)S(1)}, bf16[320,512]{1,0:T(8,128)(2,1)S(1)}, u32[]{:S(2)}, u32[]{:S(2)}) collective-permute-start(bf16[320,512]{1,0:T(8,128)(2,1)S(1)} %shard_map.71), channel_id=1, source_target_pairs={{0,14},{2,0},{4,2},{6,4},{8,6},{10,8},{12,10},{14,12},{1,15},{3,1}... | collective-permute-start | bytes 983048 | tf_op jit(solution)/shard_map/ppermute | solution.py:243
  144.3 14.3 %collective-permute-start.10 = (bf16[320,512]{1,0:T(8,128)(2,1)S(1)}, bf16[320,512]{1,0:T(8,128)(2,1)S(1)}, u32[]{:S(2)}, u32[]{:S(2)}) collective-permute-start(bf16[320,512]{1,0:T(8,128)(2,1)S(1)} %shard_map.68), channel_id=1, source_target_pairs={{0,2},{2,4},{4,6},{6,8},{8,10},{10,12},{12,14},{14,0},{1,3},{3,5},... | collective-permute-start | bytes 983048 | tf_op jit(solution)/shard_map/ppermute | solution.py:243
  148.3 8.8 %collective-permute-start.16 = (bf16[192,512]{1,0:T(8,128)(2,1)S(1)}, bf16[192,512]{1,0:T(8,128)(2,1)S(1)}, u32[]{:S(2)}, u32[]{:S(2)}) collective-permute-start(bf16[192,512]{1,0:T(8,128)(2,1)S(1)} %shard_map.74), channel_id=1, source_target_pairs={{0,2},{2,4},{4,6},{6,8},{8,10},{10,12},{12,14},{14,0},{1,3},{3,5},... | collective-permute-start | bytes 589832 | tf_op jit(solution)/shard_map/ppermute | solution.py:243
  150.3 8.3 %collective-permute-start.20 = (bf16[192,512]{1,0:T(8,128)(2,1)S(1)}, bf16[192,512]{1,0:T(8,128)(2,1)S(1)}, u32[]{:S(2)}, u32[]{:S(2)}) collective-permute-start(bf16[192,512]{1,0:T(8,128)(2,1)S(1)} %shard_map.78), channel_id=1, source_target_pairs={{0,14},{2,0},{4,2},{6,4},{8,6},{10,8},{12,10},{14,12},{1,15},{3,1}... | collective-permute-start | bytes 589832 | tf_op jit(solution)/shard_map/ppermute | solution.py:243

commit v4 on v3

--- a/solution.py
+++ b/solution.py
@@ -272,7 +272,7 @@
     me = lax.axis_index(axis).reshape(1).astype(jnp.int32)
     width = partial.shape[1] // size
     tokens = partial.shape[0]
-    split = tokens * 5 // 8 if tokens % 128 == 0 else tokens // 2
+    split = tokens * 21 // 32 if tokens % 256 == 0 else tokens // 2
     parts = ((0, split), (split, tokens - split))
     streams = len(parts)
 
@@ -285,14 +285,14 @@
     lengths = [(far, size - 1 - far) if b % 2 == 0 else (size - 1 - far, far) for b in range(streams)]
     moved = [[None, None] for _ in range(streams)]
     for step in range(far):
-        for b in range(streams):
-            for side, sign in enumerate((1, -1)):
-                left = lengths[b][side] - step
-                if left <= 0:
-                    continue
-                arrived = [moved[b][side]] if step else []
-                running = add(((*parts[b], sign * left, len(arrived)),), *arrived)
-                moved[b][side] = shifted(running, axis, sign)
+        for b, side in ((0, 0), (1, 1), (0, 1), (1, 0)):
+            sign = (1, -1)[side]
+            left = lengths[b][side] - step
+            if left <= 0:
+                continue
+            arrived = [moved[b][side]] if step else []
+            running = add(((*parts[b], sign * left, len(arrived)),), *arrived)
+            moved[b][side] = shifted(running, axis, sign)
     groups = tuple((*part, 0, 2) for part in parts)
     return add(groups, *[term for pair in moved for term in pair])
 

time: 160 us -> 161 us (level)
  no operation moved by 1% of the time
where the time goes in v4:
time: 161 us; the launch traced here: 160 us
  starting transfers between devices  94.8 us (59%)
  waiting for transfers between devices  46.2 us (29%)
  Pallas kernels  16.2 us (10%)
  other arithmetic  1.64 us (1%)
    ppermute x21, starting transfers between devices, shifted(): return lax.ppermute(x, axis, [(i, (i + shift) % size) for i in range(size)])  76.8 us
    ppermute x21, waiting for transfers between devices, shifted(): return lax.ppermute(x, axis, [(i, (i + shift) % size) for i in range(size)])  29.8 us
    all_to_all x2, starting transfers between devices, per_device(): arrived = lax.all_to_all(outgoing, 'x', 0, 0, tiled=True)  10.2 us
    pallas_call x1, Pallas kernels, attention(): pl.pallas_call(attention_kernel, out_shape=jax.ShapeDtypeStruct((tokens,...  9.45 us
    all_to_all x1, waiting for transfers between devices, per_device(): info = lax.all_to_all(info, ('y', 'x'), 0, 0, tiled=True)  8.84 us
    all_to_all x1, starting transfers between devices, per_device(): info = lax.all_to_all(info, ('y', 'x'), 0, 0, tiled=True)  7.78 us
    all_to_all x2, waiting for transfers between devices, per_device(): arrived = lax.all_to_all(outgoing, 'x', 0, 0, tiled=True)  7.56 us
    pallas_call x2, Pallas kernels, pick(): pl.pallas_call(functools.partial(pick_kernel, len(pieces)), out_shape=jax...  3.37 us
  transfers between devices with their start and end apart: 24, of which 10 were waited for; matrix products, arithmetic and copies ran while one was open for 0% of the time, Pallas kernels for 2%

profile of v4, /device:TPU:2, one launch (start us, length us, event | category | flops | bytes accessed | tf_op | source)
XLA Modules:
  0.0 160.0 jit_solution(617756344641667680)
XLA Ops:
  1.0 5.4 %collective-permute-start.2 = (bf16[4,128,256]{2,1,0:T(8,128)(2,1)S(1)}, bf16[4,128,256]{2,1,0:T(8,128)(2,1)S(1)}, u32[]{:S(2)}, u32[]{:S(2)}) collective-permute-start(bf16[4,128,256]{2,1,0:T(8,128)(2,1)S(1)} %bitcast.7), channel_id=1, source_target_pairs={{0,448},{64,0},{128,64},{192,128},{256,192},{320,256},{384,320},{4... | collective-permute-start | bytes 786440 | tf_op jit(solution)/shard_map/ppermute | solution.py:243
  6.4 1.9 %collective-permute-start = (bf16[4,128,256]{2,1,0:T(8,128)(2,1)S(1)}, bf16[4,128,256]{2,1,0:T(8,128)(2,1)S(1)}, u32[]{:S(2)}, u32[]{:S(2)}) collective-permute-start(bf16[4,128,256]{2,1,0:T(8,128)(2,1)S(1)} %bitcast.8), channel_id=1, source_target_pairs={{0,64},{64,128},{128,192},{192,256},{256,320},{320,384},{384,448},... | collective-permute-start | bytes 786440 | tf_op jit(solution)/shard_map/ppermute | solution.py:243
  8.3 3.6 %collective-permute-done.2.refs_4_ = bf16[4,128,256]{2,1,0:T(8,128)(2,1)S(1)} collective-permute-done((bf16[4,128,256]{2,1,0:T(8,128)(2,1)S(1)}, bf16[4,128,256]{2,1,0:T(8,128)(2,1)S(1)}, u32[]{:S(2)}, u32[]{:S(2)}) %collective-permute-start.2) | collective-permute-done | bytes 262176 | tf_op jit(solution)/shard_map/ppermute | solution.py:243
  11.9 5.6 %collective-permute-start.3 = (bf16[4,128,256]{2,1,0:T(8,128)(2,1)S(1)}, bf16[4,128,256]{2,1,0:T(8,128)(2,1)S(1)}, u32[]{:S(2)}, u32[]{:S(2)}) collective-permute-start(bf16[4,128,256]{2,1,0:T(8,128)(2,1)S(1)} %collective-permute-done.2.refs_4_), channel_id=1, source_target_pairs={{0,448},{64,0},{128,64},{192,128},{256,192},{320,256},{384,320},{4... | collective-permute-start | bytes 786440 | tf_op jit(solution)/shard_map/ppermute | solution.py:243
  17.5 1.9 %collective-permute-start.1 = (bf16[4,128,256]{2,1,0:T(8,128)(2,1)S(1)}, bf16[4,128,256]{2,1,0:T(8,128)(2,1)S(1)}, u32[]{:S(2)}, u32[]{:S(2)}) collective-permute-start(bf16[4,128,256]{2,1,0:T(8,128)(2,1)S(1)} %collective-permute-done.refs_1_), channel_id=1, source_target_pairs={{0,64},{64,128},{128,192},{192,256},{256,320},{320,384},{384,448},... | collective-permute-start | bytes 786440 | tf_op jit(solution)/shard_map/ppermute | solution.py:243
  21.0 7.8 %all-to-all-start = ((s32[32,5,16]{2,1,0:T(8,128)}), s32[32,5,16]{2,1,0:T(8,128)S(1)}, u32[]{:S(2)}, u32[]{:S(2)}) async-start(s32[32,5,16]{2,1,0:T(8,128)} %shard_map.64), calls=%async_computation | async-start | bytes 262144 | tf_op jit(solution)/shard_map/all_to_all | solution.py:322
  28.9 8.8 %all-to-all-done.source_ref = s32[32,5,16]{2,1,0:T(8,128)S(1)} async-done(((s32[32,5,16]{2,1,0:T(8,128)}), s32[32,5,16]{2,1,0:T(8,128)S(1)}, u32[]{:S(2)}, u32[]{:S(2)}) %all-to-all-start) | async-done | bytes 10272 | tf_op jit(solution)/shard_map/all_to_all | solution.py:322
  40.2 5.4 %all-to-all-start.1 = ((bf16[4,5,128,256]{3,2,1,0:T(8,128)(2,1)}), bf16[4,5,128,256]{3,2,1,0:T(8,128)(2,1)S(1)}, u32[]{:S(2)}, u32[]{:S(2)}) async-start(bf16[4,5,128,256]{3,2,1,0:T(8,128)(2,1)} %pick.2), calls=%async_computation.1 | async-start | bytes 2621440 | tf_op jit(solution)/shard_map/all_to_all | solution.py:346
  45.6 2.7 %collective-permute-start.4 = (bf16[4,128,256]{2,1,0:T(8,128)(2,1)S(1)}, bf16[4,128,256]{2,1,0:T(8,128)(2,1)S(1)}, u32[]{:S(2)}, u32[]{:S(2)}) collective-permute-start(bf16[4,128,256]{2,1,0:T(8,128)(2,1)S(1)} %collective-permute-done.1.refs_0_.refs_2_), channel_id=1, source_target_pairs={{0,64},{64,128},{128,192},{192,256},{256,320},{320,384},{384,448},... | collective-permute-start | bytes 786440 | tf_op jit(solution)/shard_map/ppermute | solution.py:243
  48.3 4.3 %collective-permute-start.6 = (bf16[4,128,256]{2,1,0:T(8,128)(2,1)S(1)}, bf16[4,128,256]{2,1,0:T(8,128)(2,1)S(1)}, u32[]{:S(2)}, u32[]{:S(2)}) collective-permute-start(bf16[4,128,256]{2,1,0:T(8,128)(2,1)S(1)} %collective-permute-done.3.refs_1_.refs_3_), channel_id=1, source_target_pairs={{0,448},{64,0},{128,64},{192,128},{256,192},{320,256},{384,320},{4... | collective-permute-start | bytes 786440 | tf_op jit(solution)/shard_map/ppermute | solution.py:243
  52.7 2.4 %collective-permute-done.4.refs_0_ = bf16[4,128,256]{2,1,0:T(8,128)(2,1)S(1)} collective-permute-done((bf16[4,128,256]{2,1,0:T(8,128)(2,1)S(1)}, bf16[4,128,256]{2,1,0:T(8,128)(2,1)S(1)}, u32[]{:S(2)}, u32[]{:S(2)}) %collective-permute-start.4) | collective-permute-done | bytes 262176 | tf_op jit(solution)/shard_map/ppermute | solution.py:243
  57.1 7.5 %collective-permute-done.5.refs_1_ = bf16[4,128,256]{2,1,0:T(8,128)(2,1)S(1)} collective-permute-done((bf16[4,128,256]{2,1,0:T(8,128)(2,1)S(1)}, bf16[4,128,256]{2,1,0:T(8,128)(2,1)S(1)}, u32[]{:S(2)}, u32[]{:S(2)}) %collective-permute-start.5) | collective-permute-done | bytes 262176 | tf_op jit(solution)/shard_map/ppermute | solution.py:243
  66.1 4.8 %all-to-all-start.2 = ((bf16[4,3,128,256]{3,2,1,0:T(8,128)(2,1)}), bf16[4,3,128,256]{3,2,1,0:T(8,128)(2,1)S(1)}, u32[]{:S(2)}, u32[]{:S(2)}) async-start(bf16[4,3,128,256]{3,2,1,0:T(8,128)(2,1)} %pick.3), calls=%async_computation.2 | async-start | bytes 1572864 | tf_op jit(solution)/shard_map/all_to_all | solution.py:346
  71.4 7.6 %all-to-all-done.2 = bf16[4,3,128,256]{3,2,1,0:T(8,128)(2,1)S(1)} async-done(((bf16[4,3,128,256]{3,2,1,0:T(8,128)(2,1)}), bf16[4,3,128,256]{3,2,1,0:T(8,128)(2,1)S(1)}, u32[]{:S(2)}, u32[]{:S(2)}) %all-to-all-start.2) | async-done | bytes 786464 | tf_op jit(solution)/shard_map/all_to_all | solution.py:346
  79.2 9.5 %attention.1.partial_ref = bf16[512,4096]{1,0:T(8,128)(2,1)S(1)} custom-call(s32[64]{0:T(128)S(1)} %reshape.82.slot, s32[64]{0:T(128)S(1)} %reshape.83.base, s32[512,128]{1,0:T(8,128)S(1)} %broadcast_in_dim.72.start_ref, s32[512,128]{1,0:T(8,128)S(1)} %broadcast_in_dim.76.end_ref, bf16[512,512]{1,0:T(8,128)(2,1)S(1)} %copy-done, bf16[512,4096]{1,0:T(8,128)(2,1)} %w_hbm.1, ...), custom_call_target="tpu_custom_call" | custom-call | flops 4294967296 | bytes 4194304 | tf_op jit(solution)/shard_map/attention/pallas_call | solution.py:125
  88.7 4.3 %collective-permute-start.7 = (bf16[336,512]{1,0:T(8,128)(2,1)S(1)}, bf16[336,512]{1,0:T(8,128)(2,1)S(1)}, u32[]{:S(2)}, u32[]{:S(2)}) collective-permute-start(bf16[336,512]{1,0:T(8,128)(2,1)S(1)} %shard_map.65), channel_id=1, source_target_pairs={{0,2},{2,4},{4,6},{6,8},{8,10},{10,12},{12,14},{14,0},{1,3},{3,5},... | collective-permute-start | bytes 1032200 | tf_op jit(solution)/shard_map/ppermute | solution.py:243
  93.1 8.6 %collective-permute-start.11 = (bf16[336,512]{1,0:T(8,128)(2,1)S(1)}, bf16[336,512]{1,0:T(8,128)(2,1)S(1)}, u32[]{:S(2)}, u32[]{:S(2)}) collective-permute-start(bf16[336,512]{1,0:T(8,128)(2,1)S(1)} %shard_map.69), channel_id=1, source_target_pairs={{0,14},{2,0},{4,2},{6,4},{8,6},{10,8},{12,10},{14,12},{1,15},{3,1}... | collective-permute-start | bytes 1032200 | tf_op jit(solution)/shard_map/ppermute | solution.py:243
  101.6 5.4 %collective-permute-done.7.refs_0_ = bf16[336,512]{1,0:T(8,128)(2,1)S(1)} collective-permute-done((bf16[336,512]{1,0:T(8,128)(2,1)S(1)}, bf16[336,512]{1,0:T(8,128)(2,1)S(1)}, u32[]{:S(2)}, u32[]{:S(2)}) %collective-permute-start.7) | collective-permute-done | bytes 344096 | tf_op jit(solution)/shard_map/ppermute | solution.py:243
  107.1 1.9 %collective-permute-start.8 = (bf16[336,512]{1,0:T(8,128)(2,1)S(1)}, bf16[336,512]{1,0:T(8,128)(2,1)S(1)}, u32[]{:S(2)}, u32[]{:S(2)}) collective-permute-start(bf16[336,512]{1,0:T(8,128)(2,1)S(1)} %shard_map.66), channel_id=1, source_target_pairs={{0,2},{2,4},{4,6},{6,8},{8,10},{10,12},{12,14},{14,0},{1,3},{3,5},... | collective-permute-start | bytes 1032200 | tf_op jit(solution)/shard_map/ppermute | solution.py:243
  109.1 5.4 %collective-permute-start.17 = (bf16[176,512]{1,0:T(8,128)(2,1)S(1)}, bf16[176,512]{1,0:T(8,128)(2,1)S(1)}, u32[]{:S(2)}, u32[]{:S(2)}) collective-permute-start(bf16[176,512]{1,0:T(8,128)(2,1)S(1)} %shard_map.75), channel_id=1, source_target_pairs={{0,14},{2,0},{4,2},{6,4},{8,6},{10,8},{12,10},{14,12},{1,15},{3,1}... | collective-permute-start | bytes 540680 | tf_op jit(solution)/shard_map/ppermute | solution.py:243
  114.6 3.9 %collective-permute-start.12 = (bf16[336,512]{1,0:T(8,128)(2,1)S(1)}, bf16[336,512]{1,0:T(8,128)(2,1)S(1)}, u32[]{:S(2)}, u32[]{:S(2)}) collective-permute-start(bf16[336,512]{1,0:T(8,128)(2,1)S(1)} %shard_map.70), channel_id=1, source_target_pairs={{0,14},{2,0},{4,2},{6,4},{8,6},{10,8},{12,10},{14,12},{1,15},{3,1}... | collective-permute-start | bytes 1032200 | tf_op jit(solution)/shard_map/ppermute | solution.py:243
  118.5 2.8 %collective-permute-done.8.refs_0_ = bf16[336,512]{1,0:T(8,128)(2,1)S(1)} collective-permute-done((bf16[336,512]{1,0:T(8,128)(2,1)S(1)}, bf16[336,512]{1,0:T(8,128)(2,1)S(1)}, u32[]{:S(2)}, u32[]{:S(2)}) %collective-permute-start.8) | collective-permute-done | bytes 344096 | tf_op jit(solution)/shard_map/ppermute | solution.py:243
  121.4 1.9 %collective-permute-start.9 = (bf16[336,512]{1,0:T(8,128)(2,1)S(1)}, bf16[336,512]{1,0:T(8,128)(2,1)S(1)}, u32[]{:S(2)}, u32[]{:S(2)}) collective-permute-start(bf16[336,512]{1,0:T(8,128)(2,1)S(1)} %shard_map.67), channel_id=1, source_target_pairs={{0,2},{2,4},{4,6},{6,8},{8,10},{10,12},{12,14},{14,0},{1,3},{3,5},... | collective-permute-start | bytes 1032200 | tf_op jit(solution)/shard_map/ppermute | solution.py:243
  123.3 1.9 %collective-permute-start.14 = (bf16[176,512]{1,0:T(8,128)(2,1)S(1)}, bf16[176,512]{1,0:T(8,128)(2,1)S(1)}, u32[]{:S(2)}, u32[]{:S(2)}) collective-permute-start(bf16[176,512]{1,0:T(8,128)(2,1)S(1)} %shard_map.72), channel_id=1, source_target_pairs={{0,2},{2,4},{4,6},{6,8},{8,10},{10,12},{12,14},{14,0},{1,3},{3,5},... | collective-permute-start | bytes 540680 | tf_op jit(solution)/shard_map/ppermute | solution.py:243
  125.3 5.1 %collective-permute-start.18 = (bf16[176,512]{1,0:T(8,128)(2,1)S(1)}, bf16[176,512]{1,0:T(8,128)(2,1)S(1)}, u32[]{:S(2)}, u32[]{:S(2)}) collective-permute-start(bf16[176,512]{1,0:T(8,128)(2,1)S(1)} %shard_map.76), channel_id=1, source_target_pairs={{0,14},{2,0},{4,2},{6,4},{8,6},{10,8},{12,10},{14,12},{1,15},{3,1}... | collective-permute-start | bytes 540680 | tf_op jit(solution)/shard_map/ppermute | solution.py:243
  130.5 5.1 %collective-permute-done.14.refs_0_ = bf16[176,512]{1,0:T(8,128)(2,1)S(1)} collective-permute-done((bf16[176,512]{1,0:T(8,128)(2,1)S(1)}, bf16[176,512]{1,0:T(8,128)(2,1)S(1)}, u32[]{:S(2)}, u32[]{:S(2)}) %collective-permute-start.14) | collective-permute-done | bytes 180256 | tf_op jit(solution)/shard_map/ppermute | solution.py:243
  135.7 1.9 %collective-permute-start.15 = (bf16[176,512]{1,0:T(8,128)(2,1)S(1)}, bf16[176,512]{1,0:T(8,128)(2,1)S(1)}, u32[]{:S(2)}, u32[]{:S(2)}) collective-permute-start(bf16[176,512]{1,0:T(8,128)(2,1)S(1)} %shard_map.73), channel_id=1, source_target_pairs={{0,2},{2,4},{4,6},{6,8},{8,10},{10,12},{12,14},{14,0},{1,3},{3,5},... | collective-permute-start | bytes 540680 | tf_op jit(solution)/shard_map/ppermute | solution.py:243
  137.6 5.1 %collective-permute-start.19 = (bf16[176,512]{1,0:T(8,128)(2,1)S(1)}, bf16[176,512]{1,0:T(8,128)(2,1)S(1)}, u32[]{:S(2)}, u32[]{:S(2)}) collective-permute-start(bf16[176,512]{1,0:T(8,128)(2,1)S(1)} %shard_map.77), channel_id=1, source_target_pairs={{0,14},{2,0},{4,2},{6,4},{8,6},{10,8},{12,10},{14,12},{1,15},{3,1}... | collective-permute-start | bytes 540680 | tf_op jit(solution)/shard_map/ppermute | solution.py:243
  142.9 1.9 %collective-permute-start.13 = (bf16[336,512]{1,0:T(8,128)(2,1)S(1)}, bf16[336,512]{1,0:T(8,128)(2,1)S(1)}, u32[]{:S(2)}, u32[]{:S(2)}) collective-permute-start(bf16[336,512]{1,0:T(8,128)(2,1)S(1)} %shard_map.71), channel_id=1, source_target_pairs={{0,14},{2,0},{4,2},{6,4},{8,6},{10,8},{12,10},{14,12},{1,15},{3,1}... | collective-permute-start | bytes 1032200 | tf_op jit(solution)/shard_map/ppermute | solution.py:243
  144.9 3.9 %collective-permute-start.10 = (bf16[336,512]{1,0:T(8,128)(2,1)S(1)}, bf16[336,512]{1,0:T(8,128)(2,1)S(1)}, u32[]{:S(2)}, u32[]{:S(2)}) collective-permute-start(bf16[336,512]{1,0:T(8,128)(2,1)S(1)} %shard_map.68), channel_id=1, source_target_pairs={{0,2},{2,4},{4,6},{6,8},{8,10},{10,12},{12,14},{14,0},{1,3},{3,5},... | collective-permute-start | bytes 1032200 | tf_op jit(solution)/shard_map/ppermute | solution.py:243
  148.9 1.9 %collective-permute-start.16 = (bf16[176,512]{1,0:T(8,128)(2,1)S(1)}, bf16[176,512]{1,0:T(8,128)(2,1)S(1)}, u32[]{:S(2)}, u32[]{:S(2)}) collective-permute-start(bf16[176,512]{1,0:T(8,128)(2,1)S(1)} %shard_map.74), channel_id=1, source_target_pairs={{0,2},{2,4},{4,6},{6,8},{8,10},{10,12},{12,14},{14,0},{1,3},{3,5},... | collective-permute-start | bytes 540680 | tf_op jit(solution)/shard_map/ppermute | solution.py:243
  150.9 5.1 %collective-permute-start.20 = (bf16[176,512]{1,0:T(8,128)(2,1)S(1)}, bf16[176,512]{1,0:T(8,128)(2,1)S(1)}, u32[]{:S(2)}, u32[]{:S(2)}) collective-permute-start(bf16[176,512]{1,0:T(8,128)(2,1)S(1)} %shard_map.78), channel_id=1, source_target_pairs={{0,14},{2,0},{4,2},{6,4},{8,6},{10,8},{12,10},{14,12},{1,15},{3,1}... | collective-permute-start | bytes 540680 | tf_op jit(solution)/shard_map/ppermute | solution.py:243
  (61 shorter events, 14.1 us)
Async XLA Ops:
  1.0 10.9 %collective-permute-start.2 = (bf16[4,128,256]{2,1,0:T(8,128)(2,1)S(1)}, bf16[4,128,256]{2,1,0:T(8,128)(2,1)S(1)}, u32[]{:S(2)}, u32[]{:S(2)}) collective-permute-start(bf16[4,128,256]{2,1,0:T(8,128)(2,1)S(1)} %bitcast.7), channel_id=1, source_target_pairs={{0,448},{64,0},{128,64},{192,128},{256,192},{320,256},{384,320},{4... | collective-permute-start | bytes 786440 | tf_op jit(solution)/shard_map/ppermute | solution.py:243
  6.4 11.1 %collective-permute-start = (bf16[4,128,256]{2,1,0:T(8,128)(2,1)S(1)}, bf16[4,128,256]{2,1,0:T(8,128)(2,1)S(1)}, u32[]{:S(2)}, u32[]{:S(2)}) collective-permute-start(bf16[4,128,256]{2,1,0:T(8,128)(2,1)S(1)} %bitcast.8), channel_id=1, source_target_pairs={{0,64},{64,128},{128,192},{192,256},{256,320},{320,384},{384,448},... | collective-permute-start | bytes 786440 | tf_op jit(solution)/shard_map/ppermute | solution.py:243
  11.9 25.8 %collective-permute-start.3 = (bf16[4,128,256]{2,1,0:T(8,128)(2,1)S(1)}, bf16[4,128,256]{2,1,0:T(8,128)(2,1)S(1)}, u32[]{:S(2)}, u32[]{:S(2)}) collective-permute-start(bf16[4,128,256]{2,1,0:T(8,128)(2,1)S(1)} %collective-permute-done.2.refs_4_), channel_id=1, source_target_pairs={{0,448},{64,0},{128,64},{192,128},{256,192},{320,256},{384,320},{4... | collective-permute-start | bytes 786440 | tf_op jit(solution)/shard_map/ppermute | solution.py:243
  17.5 20.2 %collective-permute-start.1 = (bf16[4,128,256]{2,1,0:T(8,128)(2,1)S(1)}, bf16[4,128,256]{2,1,0:T(8,128)(2,1)S(1)}, u32[]{:S(2)}, u32[]{:S(2)}) collective-permute-start(bf16[4,128,256]{2,1,0:T(8,128)(2,1)S(1)} %collective-permute-done.refs_1_), channel_id=1, source_target_pairs={{0,64},{64,128},{128,192},{192,256},{256,320},{320,384},{384,448},... | collective-permute-start | bytes 786440 | tf_op jit(solution)/shard_map/ppermute | solution.py:243
  21.0 16.7 %all-to-all-start = ((s32[32,5,16]{2,1,0:T(8,128)}), s32[32,5,16]{2,1,0:T(8,128)S(1)}, u32[]{:S(2)}, u32[]{:S(2)}) async-start(s32[32,5,16]{2,1,0:T(8,128)} %shard_map.64), calls=%async_computation | async-start | bytes 262144 | tf_op jit(solution)/shard_map/all_to_all | solution.py:322
  38.3 32.6 %copy-start.1 = (s32[4,16]{1,0:T(4,128)S(1)}, s32[4,16]{1,0:T(4,128)}, u32[]{:S(2)}) copy-start(s32[4,16]{1,0:T(4,128)} %lists_ref.1) | copy-start | bytes 772
  38.3 33.0 %copy-start.2 = (s32[512]{0:T(512)S(1)}, s32[512]{0:T(512)}, u32[]{:S(2)}) copy-start(s32[512]{0:T(512)} %param.9) | copy-start | bytes 6148
  38.3 40.9 %copy-start = (bf16[512,512]{1,0:T(8,128)(2,1)S(1)}, bf16[512,512]{1,0:T(8,128)(2,1)}, u32[]{:S(2)}) copy-start(bf16[512,512]{1,0:T(8,128)(2,1)} %q_hbm.1) | copy-start | bytes 1572868
  40.2 25.9 %all-to-all-start.1 = ((bf16[4,5,128,256]{3,2,1,0:T(8,128)(2,1)}), bf16[4,5,128,256]{3,2,1,0:T(8,128)(2,1)S(1)}, u32[]{:S(2)}, u32[]{:S(2)}) async-start(bf16[4,5,128,256]{3,2,1,0:T(8,128)(2,1)} %pick.2), calls=%async_computation.1 | async-start | bytes 2621440 | tf_op jit(solution)/shard_map/all_to_all | solution.py:346
  45.6 9.5 %collective-permute-start.4 = (bf16[4,128,256]{2,1,0:T(8,128)(2,1)S(1)}, bf16[4,128,256]{2,1,0:T(8,128)(2,1)S(1)}, u32[]{:S(2)}, u32[]{:S(2)}) collective-permute-start(bf16[4,128,256]{2,1,0:T(8,128)(2,1)S(1)} %collective-permute-done.1.refs_0_.refs_2_), channel_id=1, source_target_pairs={{0,64},{64,128},{128,192},{192,256},{256,320},{320,384},{384,448},... | collective-permute-start | bytes 786440 | tf_op jit(solution)/shard_map/ppermute | solution.py:243
  48.3 8.8 %collective-permute-start.6 = (bf16[4,128,256]{2,1,0:T(8,128)(2,1)S(1)}, bf16[4,128,256]{2,1,0:T(8,128)(2,1)S(1)}, u32[]{:S(2)}, u32[]{:S(2)}) collective-permute-start(bf16[4,128,256]{2,1,0:T(8,128)(2,1)S(1)} %collective-permute-done.3.refs_1_.refs_3_), channel_id=1, source_target_pairs={{0,448},{64,0},{128,64},{192,128},{256,192},{320,256},{384,320},{4... | collective-permute-start | bytes 786440 | tf_op jit(solution)/shard_map/ppermute | solution.py:243
  55.1 9.5 %collective-permute-start.5 = (bf16[4,128,256]{2,1,0:T(8,128)(2,1)S(1)}, bf16[4,128,256]{2,1,0:T(8,128)(2,1)S(1)}, u32[]{:S(2)}, u32[]{:S(2)}) collective-permute-start(bf16[4,128,256]{2,1,0:T(8,128)(2,1)S(1)} %collective-permute-done.4.refs_0_), channel_id=1, source_target_pairs={{0,64},{64,128},{128,192},{192,256},{256,320},{320,384},{384,448},... | collective-permute-start | bytes 786440 | tf_op jit(solution)/shard_map/ppermute | solution.py:243
  66.1 12.8 %all-to-all-start.2 = ((bf16[4,3,128,256]{3,2,1,0:T(8,128)(2,1)}), bf16[4,3,128,256]{3,2,1,0:T(8,128)(2,1)S(1)}, u32[]{:S(2)}, u32[]{:S(2)}) async-start(bf16[4,3,128,256]{3,2,1,0:T(8,128)(2,1)} %pick.3), calls=%async_computation.2 | async-start | bytes 1572864 | tf_op jit(solution)/shard_map/all_to_all | solution.py:346
  88.7 18.3 %collective-permute-start.7 = (bf16[336,512]{1,0:T(8,128)(2,1)S(1)}, bf16[336,512]{1,0:T(8,128)(2,1)S(1)}, u32[]{:S(2)}, u32[]{:S(2)}) collective-permute-start(bf16[336,512]{1,0:T(8,128)(2,1)S(1)} %shard_map.65), channel_id=1, source_target_pairs={{0,2},{2,4},{4,6},{6,8},{8,10},{10,12},{12,14},{14,0},{1,3},{3,5},... | collective-permute-start | bytes 1032200 | tf_op jit(solution)/shard_map/ppermute | solution.py:243
  93.1 21.4 %collective-permute-start.11 = (bf16[336,512]{1,0:T(8,128)(2,1)S(1)}, bf16[336,512]{1,0:T(8,128)(2,1)S(1)}, u32[]{:S(2)}, u32[]{:S(2)}) collective-permute-start(bf16[336,512]{1,0:T(8,128)(2,1)S(1)} %shard_map.69), channel_id=1, source_target_pairs={{0,14},{2,0},{4,2},{6,4},{8,6},{10,8},{12,10},{14,12},{1,15},{3,1}... | collective-permute-start | bytes 1032200 | tf_op jit(solution)/shard_map/ppermute | solution.py:243
  107.1 14.2 %collective-permute-start.8 = (bf16[336,512]{1,0:T(8,128)(2,1)S(1)}, bf16[336,512]{1,0:T(8,128)(2,1)S(1)}, u32[]{:S(2)}, u32[]{:S(2)}) collective-permute-start(bf16[336,512]{1,0:T(8,128)(2,1)S(1)} %shard_map.66), channel_id=1, source_target_pairs={{0,2},{2,4},{4,6},{6,8},{8,10},{10,12},{12,14},{14,0},{1,3},{3,5},... | collective-permute-start | bytes 1032200 | tf_op jit(solution)/shard_map/ppermute | solution.py:243
  109.1 16.2 %collective-permute-start.17 = (bf16[176,512]{1,0:T(8,128)(2,1)S(1)}, bf16[176,512]{1,0:T(8,128)(2,1)S(1)}, u32[]{:S(2)}, u32[]{:S(2)}) collective-permute-start(bf16[176,512]{1,0:T(8,128)(2,1)S(1)} %shard_map.75), channel_id=1, source_target_pairs={{0,14},{2,0},{4,2},{6,4},{8,6},{10,8},{12,10},{14,12},{1,15},{3,1}... | collective-permute-start | bytes 540680 | tf_op jit(solution)/shard_map/ppermute | solution.py:243
  114.6 28.2 %collective-permute-start.12 = (bf16[336,512]{1,0:T(8,128)(2,1)S(1)}, bf16[336,512]{1,0:T(8,128)(2,1)S(1)}, u32[]{:S(2)}, u32[]{:S(2)}) collective-permute-start(bf16[336,512]{1,0:T(8,128)(2,1)S(1)} %shard_map.70), channel_id=1, source_target_pairs={{0,14},{2,0},{4,2},{6,4},{8,6},{10,8},{12,10},{14,12},{1,15},{3,1}... | collective-permute-start | bytes 1032200 | tf_op jit(solution)/shard_map/ppermute | solution.py:243
  121.4 23.4 %collective-permute-start.9 = (bf16[336,512]{1,0:T(8,128)(2,1)S(1)}, bf16[336,512]{1,0:T(8,128)(2,1)S(1)}, u32[]{:S(2)}, u32[]{:S(2)}) collective-permute-start(bf16[336,512]{1,0:T(8,128)(2,1)S(1)} %shard_map.67), channel_id=1, source_target_pairs={{0,2},{2,4},{4,6},{6,8},{8,10},{10,12},{12,14},{14,0},{1,3},{3,5},... | collective-permute-start | bytes 1032200 | tf_op jit(solution)/shard_map/ppermute | solution.py:243
  123.3 12.3 %collective-permute-start.14 = (bf16[176,512]{1,0:T(8,128)(2,1)S(1)}, bf16[176,512]{1,0:T(8,128)(2,1)S(1)}, u32[]{:S(2)}, u32[]{:S(2)}) collective-permute-start(bf16[176,512]{1,0:T(8,128)(2,1)S(1)} %shard_map.72), channel_id=1, source_target_pairs={{0,2},{2,4},{4,6},{6,8},{8,10},{10,12},{12,14},{14,0},{1,3},{3,5},... | collective-permute-start | bytes 540680 | tf_op jit(solution)/shard_map/ppermute | solution.py:243
  125.3 12.2 %collective-permute-start.18 = (bf16[176,512]{1,0:T(8,128)(2,1)S(1)}, bf16[176,512]{1,0:T(8,128)(2,1)S(1)}, u32[]{:S(2)}, u32[]{:S(2)}) collective-permute-start(bf16[176,512]{1,0:T(8,128)(2,1)S(1)} %shard_map.76), channel_id=1, source_target_pairs={{0,14},{2,0},{4,2},{6,4},{8,6},{10,8},{12,10},{14,12},{1,15},{3,1}... | collective-permute-start | bytes 540680 | tf_op jit(solution)/shard_map/ppermute | solution.py:243
  135.7 13.2 %collective-permute-start.15 = (bf16[176,512]{1,0:T(8,128)(2,1)S(1)}, bf16[176,512]{1,0:T(8,128)(2,1)S(1)}, u32[]{:S(2)}, u32[]{:S(2)}) collective-permute-start(bf16[176,512]{1,0:T(8,128)(2,1)S(1)} %shard_map.73), channel_id=1, source_target_pairs={{0,2},{2,4},{4,6},{6,8},{8,10},{10,12},{12,14},{14,0},{1,3},{3,5},... | collective-permute-start | bytes 540680 | tf_op jit(solution)/shard_map/ppermute | solution.py:243
  137.6 13.2 %collective-permute-start.19 = (bf16[176,512]{1,0:T(8,128)(2,1)S(1)}, bf16[176,512]{1,0:T(8,128)(2,1)S(1)}, u32[]{:S(2)}, u32[]{:S(2)}) collective-permute-start(bf16[176,512]{1,0:T(8,128)(2,1)S(1)} %shard_map.77), channel_id=1, source_target_pairs={{0,14},{2,0},{4,2},{6,4},{8,6},{10,8},{12,10},{14,12},{1,15},{3,1}... | collective-permute-start | bytes 540680 | tf_op jit(solution)/shard_map/ppermute | solution.py:243
  142.9 16.2 %collective-permute-start.13 = (bf16[336,512]{1,0:T(8,128)(2,1)S(1)}, bf16[336,512]{1,0:T(8,128)(2,1)S(1)}, u32[]{:S(2)}, u32[]{:S(2)}) collective-permute-start(bf16[336,512]{1,0:T(8,128)(2,1)S(1)} %shard_map.71), channel_id=1, source_target_pairs={{0,14},{2,0},{4,2},{6,4},{8,6},{10,8},{12,10},{14,12},{1,15},{3,1}... | collective-permute-start | bytes 1032200 | tf_op jit(solution)/shard_map/ppermute | solution.py:243
  144.9 14.1 %collective-permute-start.10 = (bf16[336,512]{1,0:T(8,128)(2,1)S(1)}, bf16[336,512]{1,0:T(8,128)(2,1)S(1)}, u32[]{:S(2)}, u32[]{:S(2)}) collective-permute-start(bf16[336,512]{1,0:T(8,128)(2,1)S(1)} %shard_map.68), channel_id=1, source_target_pairs={{0,2},{2,4},{4,6},{6,8},{8,10},{10,12},{12,14},{14,0},{1,3},{3,5},... | collective-permute-start | bytes 1032200 | tf_op jit(solution)/shard_map/ppermute | solution.py:243
  148.9 8.6 %collective-permute-start.16 = (bf16[176,512]{1,0:T(8,128)(2,1)S(1)}, bf16[176,512]{1,0:T(8,128)(2,1)S(1)}, u32[]{:S(2)}, u32[]{:S(2)}) collective-permute-start(bf16[176,512]{1,0:T(8,128)(2,1)S(1)} %shard_map.74), channel_id=1, source_target_pairs={{0,2},{2,4},{4,6},{6,8},{8,10},{10,12},{12,14},{14,0},{1,3},{3,5},... | collective-permute-start | bytes 540680 | tf_op jit(solution)/shard_map/ppermute | solution.py:243
  150.9 8.1 %collective-permute-start.20 = (bf16[176,512]{1,0:T(8,128)(2,1)S(1)}, bf16[176,512]{1,0:T(8,128)(2,1)S(1)}, u32[]{:S(2)}, u32[]{:S(2)}) collective-permute-start(bf16[176,512]{1,0:T(8,128)(2,1)S(1)} %shard_map.78), channel_id=1, source_target_pairs={{0,14},{2,0},{4,2},{6,4},{8,6},{10,8},{12,10},{14,12},{1,15},{3,1}... | collective-permute-start | bytes 540680 | tf_op jit(solution)/shard_map/ppermute | solution.py:243
